TPU v7x, 256 devices: a whole 4x4x8 slice. The times are simulated.
256 devices in a mesh: leaf: 64 (over x, z, core), rhs: 4 (over y).
Axes of the slice: x: 4, y: 4, z: 8, core: 2. Of those that a mesh axis runs over, the one named last changes fastest.
Arguments:
- coords: bfloat16 [64, 262144], P(None, 'leaf'), may hold values from -1.5 to 1.5
- rhs: bfloat16 [256, 262144], P('rhs', 'leaf'), parts along dimension 0, may hold values from -6 to 6
- basis: bfloat16 [512, 512, 256], P('leaf'), may hold values from -0.25 to 0.25
- transfer_one: bfloat16 [256, 512, 256], P('leaf'), may hold values from -0.25 to 0.25
- transfer_two: bfloat16 [128, 512, 256], P('leaf'), may hold values from -0.25 to 0.25
- far_blocks: bfloat16 [896, 4, 256, 256], P('leaf'), may hold values from -0.375 to 0.375
- neighbours: int32 [512, 8], replicated, may hold values from 0 to 511, as said below
- far_lists: int32 [896, 4], replicated, may hold values from 0 to 895, as said below
Outputs:
- product: float32 [256, 262144], P('rhs', 'leaf'), parts along dimension 0
There are 4 independent parts, one for each index of `rhs`. A program takes and returns all parts, laid end to end along the dimension named above; an argument that names none is the same for every part. Nothing has to cross between parts.
Inputs may be any that keep to these rules, and one draw needn't show every extreme that they name: `neighbours`: row i starts with leaf i itself; its other entries name leaves of other devices (leaf i lies on device i // 8). The entries after the first in the lists of one device's leaves name no other device more than 1 times, and the leaves of every device are named exactly 56 times by such entries over all lists. `far_lists`: entry (n, f) names a node of the same level as node n on another device (node n lies on device n // 14). The entries of one device's nodes name no other device more than 1 times, and the nodes of every device are named exactly 56 times over all entries.
All inputs are finite; a program needn't handle non-finite values.
Results may differ from a plain program's by a relative error of at most 0.005.
Values may be sent and summed in bfloat16 or wider, within the bound.
No kernel may reach another device: no remote copies, remote signals or barrier semaphores. Data moves between devices by JAX's collectives and lax.ppermute only.
A program may use at most 128 MiB of HBM per device.

v0:
```python
import jax
import jax.numpy as jnp
from jax import lax
from jax.sharding import PartitionSpec as P

FEAT = 64
RANK = 256
R = 64
LEAF = 512
NB = 8
FAR = 4


def kernel_tiles(sources, targets):
    inner = jnp.einsum("...fa,...fb->...ab", sources, targets, preferred_element_type=jnp.float32)
    src_f = sources.astype(jnp.float32)
    dst_f = targets.astype(jnp.float32)
    src_sq = jnp.sum(src_f * src_f, axis=-2)
    dst_sq = jnp.sum(dst_f * dst_f, axis=-2)
    return jnp.exp(inner - 0.5 * src_sq[..., :, None] - 0.5 * dst_sq[..., None, :]).astype(
        jnp.bfloat16
    )


def tile_products(sources, targets):
    kernel = kernel_tiles(sources[:, :FEAT], targets)
    return jnp.einsum("gra,gab->grb", sources[:, FEAT:], kernel, preferred_element_type=jnp.float32)


def grouped_products(sources, targets):
    groups = sources.shape[0] // 4
    paired = (
        sources.reshape(groups, 4, sources.shape[1], sources.shape[2]),
        targets.reshape(groups, 4, targets.shape[1], targets.shape[2]),
    )
    outcome = lax.map(lambda couple: tile_products(couple[0], couple[1]), paired)
    return outcome.reshape(sources.shape[0], R, sources.shape[2])


def slot_ranks(owners):
    entry_count = owners.shape[1]
    position = jnp.arange(entry_count, dtype=jnp.int32)
    earlier = position[None, :] < position[:, None]
    matches = owners[:, :, None] == owners[:, None, :]
    return jnp.sum(jnp.logical_and(matches, earlier[None]), axis=2)


def arrivals(owners, ranks, entries, device_index, slot_count):
    entry_count = owners.shape[1]
    located = jnp.nonzero((owners == device_index).reshape(-1), size=entry_count, fill_value=0)[
        0
    ].astype(jnp.int32)
    requester = located // entry_count
    target_slot = requester * slot_count + ranks.reshape(-1)[located]
    return (target_slot, entries.reshape(-1)[located])


def join_pairs(skeleton):
    return skeleton.reshape(-1, 2, R, RANK).transpose(0, 2, 1, 3).reshape(-1, R, 2 * RANK)


def descend(parent, transfer, child_far):
    rounded = parent.astype(jnp.bfloat16)
    spread = jnp.einsum("mrk,mjk->mrj", rounded, transfer, preferred_element_type=jnp.float32)
    spread = spread.reshape(-1, R, 2, RANK).transpose(0, 2, 1, 3).reshape(-1, R, RANK)
    return child_far + spread


def on_device(coords, rhs, basis, transfer_one, transfer_two, far_blocks, neighbours, far_lists):
    peer_count = lax.axis_size("leaf")
    device_index = lax.axis_index("leaf")
    local_leaves = basis.shape[0]
    node_count = far_blocks.shape[0]
    remote_count = (NB - 1) * local_leaves
    near_slots = (remote_count + peer_count - 2) // (peer_count - 1)
    far_count = node_count * FAR
    far_slots = (far_count + peer_count - 2) // (peer_count - 1)
    points = coords.reshape(FEAT, local_leaves, LEAF).transpose(1, 0, 2)
    charges = rhs.reshape(R, local_leaves, LEAF).transpose(1, 0, 2)
    blocks = jnp.concatenate([points, charges], axis=1)
    remote = neighbours.reshape(peer_count, local_leaves, NB)[:, :, 1:].reshape(
        peer_count, remote_count
    )
    owners = remote // local_leaves
    ranks = slot_ranks(owners)
    my_owners = lax.dynamic_index_in_dim(owners, device_index, 0, keepdims=False)
    my_ranks = lax.dynamic_index_in_dim(ranks, device_index, 0, keepdims=False)
    my_slots = my_owners * near_slots + my_ranks
    outgoing, wanted = arrivals(owners, ranks, remote, device_index, near_slots)
    item_leaf = jnp.arange(remote_count, dtype=jnp.int32) // (NB - 1)
    skel_zero = jnp.einsum(
        "lra,lak->lrk", charges, basis, preferred_element_type=jnp.float32
    ).astype(jnp.bfloat16)
    skel_one = jnp.einsum(
        "mrj,mjk->mrk", join_pairs(skel_zero), transfer_one, preferred_element_type=jnp.float32
    ).astype(jnp.bfloat16)
    skel_two = jnp.einsum(
        "mrj,mjk->mrk", join_pairs(skel_one), transfer_two, preferred_element_type=jnp.float32
    ).astype(jnp.bfloat16)
    skeleton = jnp.concatenate([skel_zero, skel_one, skel_two], axis=0)
    far_remote = far_lists.reshape(peer_count, far_count)
    far_owners = far_remote // node_count
    far_ranks = slot_ranks(far_owners)
    far_outgoing, far_wanted = arrivals(far_owners, far_ranks, far_remote, device_index, far_slots)
    far_buffer = (
        jnp.zeros((peer_count * far_slots, R, RANK), jnp.bfloat16)
        .at[far_outgoing]
        .set(skeleton[far_wanted % node_count])
    )
    far_arrived = lax.all_to_all(
        far_buffer.reshape(peer_count, far_slots, R, RANK),
        "leaf",
        split_axis=0,
        concat_axis=0,
        tiled=True,
    )
    my_far = lax.dynamic_index_in_dim(
        far_owners, device_index, 0, keepdims=False
    ) * far_slots + lax.dynamic_index_in_dim(far_ranks, device_index, 0, keepdims=False)
    partners = far_arrived.reshape(peer_count * far_slots, R, RANK)[my_far].reshape(
        node_count, FAR, R, RANK
    )
    leaf_buffer = (
        jnp.zeros((peer_count * near_slots, FEAT + R, LEAF), jnp.bfloat16)
        .at[outgoing]
        .set(blocks[wanted % local_leaves])
    )
    leaf_arrived = lax.all_to_all(
        leaf_buffer.reshape(peer_count, near_slots, FEAT + R, LEAF),
        "leaf",
        split_axis=0,
        concat_axis=0,
        tiled=True,
    )
    sources = leaf_arrived.reshape(peer_count * near_slots, FEAT + R, LEAF)[my_slots]
    per_item = grouped_products(sources, points[item_leaf])
    self_terms = tile_products(blocks, points)
    near = self_terms + jnp.sum(per_item.reshape(local_leaves, NB - 1, R, LEAF), axis=1)
    far = jnp.einsum("nfrk,nfkj->nrj", partners, far_blocks, preferred_element_type=jnp.float32)
    far_zero = far[:local_leaves]
    far_one = far[local_leaves : local_leaves * 3 // 2]
    far_two = far[local_leaves * 3 // 2 :]
    middle = descend(far_two, transfer_two, far_one)
    lowest = descend(middle, transfer_one, far_zero)
    result = near + jnp.einsum(
        "lrk,lak->lra", lowest.astype(jnp.bfloat16), basis, preferred_element_type=jnp.float32
    )
    return result.transpose(1, 0, 2).reshape(R, local_leaves * LEAF)


def solution(mesh):
    return jax.shard_map(
        on_device,
        mesh=mesh,
        in_specs=(
            P(None, "leaf"),
            P("rhs", "leaf"),
            P("leaf", None, None),
            P("leaf", None, None),
            P("leaf", None, None),
            P("leaf", None, None, None),
            P(),
            P(),
        ),
        out_specs=P("rhs", "leaf"),
        check_vma=False,
    )
```

profile of v0, /device:TPU:1, one launch (start us, length us, event | category | flops | bytes accessed | tf_op | source)
XLA Modules:
  0.0 433.0 jit_solution(569077205230775826)
XLA Ops:
  0.0 1.5 convert_reduce_fusion.3
  3.9 1.5 convert_reduce_fusion.2
  5.3 1.5 copy.151
  8.5 1.7 copy.175
  11.7 25.2 %scatter_custom_fusion.2 = s32[56]{0:T(128)S(1)} fusion(s32[3584]{0:T(1024)S(1)} %fusion.59, s32[3584]{0:T(1024)S(1)} %broadcast.740, s32[]{:T(128)} %copy.211), kind=kCustom, calls=%fused_computation.157 | custom fusion | flops 3584 | bytes 228 | tf_op jit(solution)/shard_map/scatter-add | solution.py:50
  40.8 2.1 convert_reduce_fusion
  42.9 1.4 copy.171
  46.6 1.5 fusion.44
  48.1 1.3 reshape_reshape.11
  50.4 1.5 convolution_convert_fusion
  52.6 2.0 gather_fusion.7
  54.6 1.6 broadcast_in_dim.23
  56.2 9.7 %scatter_fusion.1 = bf16[64,64,256]{2,1,0:T(8,128)(2,1)} fusion(bf16[64,64,256]{2,1,0:T(8,128)(2,1)} %broadcast_in_dim.23, s32[56]{0:T(128)S(1)} %fusion.44, bf16[56,64,256]{2,1,0:T(8,128)(2,1)} %gather_fusion.7), kind=kCustom, calls=%fused_computation.12 | custom fusion | bytes 5505248 | tf_op jit(solution)/shard_map/scatter | solution.py:108
  65.9 13.3 %all-to-all-start.1 = ((bf16[64,1,64,256]{3,2,1,0:T(8,128)(2,1)}), bf16[64,1,64,256]{3,2,1,0:T(8,128)(2,1)}, u32[]{:S(2)}, u32[]{:S(2)}) async-start(bf16[64,1,64,256]{3,2,1,0:T(8,128)(2,1)} %bitcast.121), calls=%async_computation.1 | async-start | bytes 4194304 | tf_op jit(solution)/shard_map/all_to_all | solution.py:110
  80.1 25.6 %scatter_custom_fusion = s32[56]{0:T(128)S(1)} fusion(s32[3584]{0:T(1024)S(1)} %fusion.58, s32[3584]{0:T(1024)} %copy-done.12, s32[]{:T(128)} %copy.211), kind=kCustom, calls=%fused_computation.159 | custom fusion | flops 3584 | bytes 736 | tf_op jit(solution)/shard_map/scatter-add | solution.py:50
  108.7 1.1 bitcast_bitcast_fusion
  110.7 5.3 %gather_fusion.2 = bf16[56,128,512]{2,1,0:T(8,128)(2,1)} fusion(bf16[8,128,512]{2,1,0:T(8,128)(2,1)S(1)} %pad_maximum_fusion, s32[1024]{0:T(1024)S(1)} %pad_clamp_fusion.5), kind=kCustom, calls=%fused_computation.2 | custom fusion | bytes 14680288 | tf_op jit(solution)/shard_map/gather | solution.py:126
  116.8 4.2 broadcast_in_dim.21
  121.0 19.6 %scatter_fusion = bf16[64,128,512]{2,1,0:T(8,128)(2,1)} fusion(bf16[64,128,512]{2,1,0:T(8,128)(2,1)} %broadcast_in_dim.21, s32[56]{0:T(128)S(1)} %fusion.40, bf16[56,128,512]{2,1,0:T(8,128)(2,1)} %gather_fusion.2), kind=kCustom, calls=%fused_computation.10 | custom fusion | bytes 22020320 | tf_op jit(solution)/shard_map/scatter | solution.py:126
  140.5 10.6 %all-to-all-start = ((bf16[64,1,128,512]{3,2,1,0:T(8,128)(2,1)}), bf16[64,1,128,512]{3,2,1,0:T(8,128)(2,1)}, u32[]{:S(2)}, u32[]{:S(2)}) async-start(bf16[64,1,128,512]{3,2,1,0:T(8,128)(2,1)} %bitcast.120), calls=%async_computation | async-start | bytes 16777216 | tf_op jit(solution)/shard_map/all_to_all | solution.py:128
  151.3 2.7 gather_fusion.4
  155.2 3.5 gather_fusion.8
  158.7 5.1 %convolution_bitcast_fusion.1 = f32[14,64,256]{2,1,0:T(8,128)S(1)} fusion(bf16[14,4,64,256]{3,2,1,0:T(8,128)(2,1)} %bitcast.123, bf16[14,4,256,256]{3,2,1,0:T(8,128)(2,1)} %param.15), kind=kOutput, calls=%fused_computation.38 | convolution fusion | flops 469762048 | bytes 10092544 | tf_op jit(solution)/shard_map/nfrk,nfkj->nrj/dot_general | solution.py:139
  165.6 171.3 %all-to-all-done = bf16[64,1,128,512]{3,2,1,0:T(8,128)(2,1)} async-done(((bf16[64,1,128,512]{3,2,1,0:T(8,128)(2,1)}), bf16[64,1,128,512]{3,2,1,0:T(8,128)(2,1)}, u32[]{:S(2)}, u32[]{:S(2)}) %all-to-all-start) | async-done | bytes 8388640 | tf_op jit(solution)/shard_map/all_to_all | solution.py:128
  336.9 8.7 %gather_fusion.3 = bf16[56,128,512]{2,1,0:T(8,128)(2,1)} fusion(bf16[64,128,512]{2,1,0:T(8,128)(2,1)} %bitcast.10, s32[1024]{0:T(1024)S(1)} %pad_clamp_fusion.4), kind=kCustom, calls=%fused_computation.3 | custom fusion | bytes 14680288 | tf_op jit(solution)/shard_map/gather | solution.py:135
  345.6 74.0 %while.10 = (s32[]{:T(128)}, f32[14,4,64,512]{3,2,1,0:T(8,128)}, bf16[14,4,128,512]{3,2,1,0:T(8,128)(2,1)}, bf16[14,4,64,512]{3,2,1,0:T(8,128)(2,1)}, s32[]{:T(128)}) while((s32[]{:T(128)}, f32[14,4,64,512]{3,2,1,0:T(8,128)}, bf16[14,4,128,512]{3,2,1,0:T(8,128)(2,1)}, bf16[14,4,64,512]{3,2,1,0:T(8,128)(2,1)}, s32[]{:T(128)}) %tuple.34), condition=%wide.region_11.12_spmd, body=%wide.region_8.11_spmd.sunk | while | flops 272367616 | bytes 2950213 | solution.py:36
  345.6 1.1 dynamic-slice_bitcast_fusion.2
  347.8 3.1 fusion.86
  350.8 1.1 dynamic-slice_bitcast_fusion.2
  353.0 3.1 fusion.86
  356.1 1.1 dynamic-slice_bitcast_fusion.2
  358.3 3.1 fusion.86
  363.6 3.1 fusion.86
  368.9 3.1 fusion.86
  374.2 3.1 fusion.86
  377.3 1.1 dynamic-slice_bitcast_fusion.2
  379.5 3.1 fusion.86
  384.7 3.1 fusion.86
  390.0 3.1 fusion.86
  393.1 1.1 dynamic-slice_bitcast_fusion.2
  395.3 3.1 fusion.86
  400.6 3.1 fusion.86
  405.9 3.1 fusion.86
  411.2 3.1 fusion.86
  416.4 3.1 fusion.86
  419.5 5.1 %reduce_sum.81 = f32[8,64,512]{2,1,0:T(8,128)} reduce(f32[8,7,64,512]{3,2,1,0:T(8,128)} %bitcast.124, f32[]{:T(128)} %constant.131.clone.1), dimensions={1}, to_apply=%region_12.13 | reduce | flops 1572864 | bytes 8388612 | tf_op jit(solution)/shard_map/reduce_sum | solution.py:138
  424.6 5.3 %fusion.20 = f32[64,8,512]{2,0,1:T(8,128)} fusion(f32[8,512]{1,0:T(8,128)S(1)} %copy-done.13, f32[8,64,512]{2,1,0:T(8,128)} %reduce_sum.81, bf16[8,8,8,512]{3,2,1,0:T(8,128)(2,1)} %bitcast.133, bf16[8,8,8,512]{3,2,1,0:T(8,128)(2,1)} %bitcast.128), kind=kOutput, calls=%fused_computation.39 | convolution fusion | flops 543424512 | bytes 3162112 | tf_op jit(solution)/shard_map/gra,gab->grb/dot_general | solution.py:27
  430.0 2.0 fusion.19
  (156 shorter events, 47.9 us)
Async XLA Ops:
  0.0 50.4 %copy-start = (bf16[8,512,256]{2,1,0:T(8,128)(2,1)S(1)}, bf16[8,512,256]{2,1,0:T(8,128)(2,1)}, u32[]{:S(2)}) copy-start(bf16[8,512,256]{2,1,0:T(8,128)(2,1)} %param.12) | copy-start | bytes 6291460
  5.3 46.7 %copy-start.3 = (bf16[4,512,256]{2,1,0:T(8,128)(2,1)S(1)}, bf16[4,512,256]{2,1,0:T(8,128)(2,1)}, u32[]{:S(2)}) copy-start(bf16[4,512,256]{2,1,0:T(8,128)(2,1)} %param.13) | copy-start | bytes 3145732
  11.7 27.5 %copy-start.12 = (s32[3584]{0:T(1024)}, s32[3584]{0:T(1024)S(1)}, u32[]{:S(2)}) copy-start(s32[3584]{0:T(1024)S(1)} %broadcast.740) | copy-start | bytes 43012
  50.3 2.0 copy-start.6
  56.2 23.2 %copy-start.11 = (s32[28,128]{1,0:T(8,128)S(1)}, s32[28,128]{1,0:T(8,128)}, u32[]{:S(2)}) copy-start(s32[28,128]{1,0:T(8,128)} %get-tuple-element.50) | copy-start | bytes 43012
  65.9 42.8 %copy-start.8 = (bf16[64,4096]{1,0:T(8,128)(2,1)S(1)}, bf16[64,4096]{1,0:T(8,128)(2,1)}, u32[]{:S(2)}) copy-start(bf16[64,4096]{1,0:T(8,128)(2,1)} %param.10) | copy-start | bytes 1572868
  65.9 74.6 %all-to-all-start.1 = ((bf16[64,1,64,256]{3,2,1,0:T(8,128)(2,1)}), bf16[64,1,64,256]{3,2,1,0:T(8,128)(2,1)}, u32[]{:S(2)}, u32[]{:S(2)}) async-start(bf16[64,1,64,256]{3,2,1,0:T(8,128)(2,1)} %bitcast.121), calls=%async_computation.1 | async-start | bytes 4194304 | tf_op jit(solution)/shard_map/all_to_all | solution.py:110
  109.8 0.8 copy-start.1
  140.5 10.7 %copy-start.2 = (bf16[8,64,512]{2,1,0:T(8,128)(2,1)S(1)}, bf16[8,64,512]{2,1,0:T(8,128)(2,1)}, u32[]{:S(2)}) copy-start(bf16[8,64,512]{2,1,0:T(8,128)(2,1)} %copy-done.1) | copy-start | bytes 1572868
  140.5 196.3 %all-to-all-start = ((bf16[64,1,128,512]{3,2,1,0:T(8,128)(2,1)}), bf16[64,1,128,512]{3,2,1,0:T(8,128)(2,1)}, u32[]{:S(2)}, u32[]{:S(2)}) async-start(bf16[64,1,128,512]{3,2,1,0:T(8,128)(2,1)} %bitcast.120), calls=%async_computation | async-start | bytes 16777216 | tf_op jit(solution)/shard_map/all_to_all | solution.py:128
  151.3 2.8 copy-start.10
  151.3 3.2 copy-start.9
  158.7 5.1 %copy-start.7 = (bf16[2,512,256]{2,1,0:T(8,128)(2,1)S(1)}, bf16[2,512,256]{2,1,0:T(8,128)(2,1)}, u32[]{:S(2)}) copy-start(bf16[2,512,256]{2,1,0:T(8,128)(2,1)} %param.14) | copy-start | bytes 1572868
  158.7 5.5 %copy-start.4 = (bf16[4,512,256]{2,1,0:T(8,128)(2,1)S(1)}, bf16[4,512,256]{2,1,0:T(8,128)(2,1)}, u32[]{:S(2)}) copy-start(bf16[4,512,256]{2,1,0:T(8,128)(2,1)} %param.13) | copy-start | bytes 3145732
  419.5 5.1 %copy-start.13 = (f32[8,512]{1,0:T(8,128)S(1)}, f32[8,512]{1,0:T(8,128)}, u32[]{:S(2)}) copy-start(f32[8,512]{1,0:T(8,128)} %broadcast_multiply_fusion.2) | copy-start | bytes 49156
  424.6 5.3 %copy-start.5 = (f32[4,128,256]{2,1,0:T(8,128)S(1)}, f32[4,128,256]{2,1,0:T(8,128)}, u32[]{:S(2)}) copy-start(f32[4,128,256]{2,1,0:T(8,128)} %pad_maximum_fusion.1) | copy-start | bytes 1572868
where the time goes:
time: 436 us; the launch traced here: 433 us
  waiting for transfers between devices  171 us (39%)
  local copies, waits for them, and re-layouts  92.1 us (21%)
  other arithmetic  86.7 us (20%)
  matrix products  58.4 us (13%)
  starting transfers between devices  23.9 us (5%)
    all_to_all x1, waiting for transfers between devices, on_device(): lax.all_to_all(leaf_buffer.reshape(peer_count, near_slots, FEAT + R, LEAF...  171 us
    scatter-add x2, other arithmetic, arrivals(): jnp.nonzero((owners == device_index).reshape(-1), size=entry_count, fill_...  50.9 us
    dot_general x15, matrix products, tile_products(): jnp.einsum('gra,gab->grb', sources[:, FEAT:], kernel, preferred_element_t...  48.5 us
    scatter x1, local copies, waits for them, and re-layouts, on_device(): leaf_buffer = jnp.zeros((peer_count * near_slots, FEAT + R, LEAF), jnp.bf...  19.6 us
    squeeze x14, local copies, waits for them, and re-layouts, grouped_products(): lax.map(lambda couple: tile_products(couple[0], couple[1]), paired)  15.1 us
    reduce_sum x14, other arithmetic, kernel_tiles(): dst_sq = jnp.sum(dst_f * dst_f, axis=-2)  14.4 us
    all_to_all x1, starting transfers between devices, on_device(): lax.all_to_all(far_buffer.reshape(peer_count, far_slots, R, RANK), 'leaf'...  13.3 us
    all_to_all x1, starting transfers between devices, on_device(): lax.all_to_all(leaf_buffer.reshape(peer_count, near_slots, FEAT + R, LEAF...  10.6 us
  transfers between devices with their start and end apart: 2, of which 1 were waited for; matrix products, arithmetic and copies ran while one was open for 17% of the time, Pallas kernels for 0%

commit v1 on v0

v1 whole, which is shorter than its diff:
```python
import functools

import jax
import jax.numpy as jnp
from jax import lax
from jax.experimental import pallas as pl
from jax.experimental.pallas import tpu as pltpu
from jax.sharding import PartitionSpec as P


FEAT = 64
RANK = 256
R = 64
LEAF = 512
NB = 8
FAR = 4
NX, NZ, NC, NY = 4, 8, 2, 4
GROUP = NX * NC
LEAF_DEV = 8
NODE_DEV = 14
QUART = FEAT // NY
ROWS = R + QUART
AUG = 128
OFFSETS = (0, -1, 1, -2, 2, -3, 3, 4)
LEAF_CHUNKS = (((0, 3), (3, 5)), ((5, 7),), ((7, 8),))
NODE_CHUNKS = ((0, 5), (5, 8))


F32 = jnp.float32
BF16 = jnp.bfloat16


def place(x, z, c):
    return (x * NZ + z % NZ) * NC + c


def ring(step):
    return [
        (place(x, z, c), place(x, z + step, c))
        for x in range(NX)
        for z in range(NZ)
        for c in range(NC)
    ]


ROW_GROUPS = [[place(x, z, c) for x in range(NX) for c in range(NC)] for z in range(NZ)]


def cost(micros):
    return pl.CostEstimate(flops=int(micros * 1e9), bytes_accessed=0, transcendentals=0)


VMEM = pl.BlockSpec(memory_space=pltpu.VMEM)
SMEM = pl.BlockSpec(memory_space=pltpu.SMEM)


def call(kernel, micros, out, tables, arrays, scratch=(), megabytes=16):
    return pl.pallas_call(
        kernel,
        in_specs=[SMEM] * len(tables) + [VMEM] * len(arrays),
        out_specs=jax.tree.map(lambda _: VMEM, out),
        out_shape=out,
        scratch_shapes=list(scratch),
        compiler_params=pltpu.CompilerParams(vmem_limit_bytes=megabytes << 20),
        cost_estimate=cost(micros),
    )(*tables, *arrays)


def shaped(shape, kind):
    return jax.ShapeDtypeStruct(shape, kind)


def nt(a, b):
    return lax.dot_general(a, b, (((1,), (1,)), ((), ())), preferred_element_type=F32)


def pack_kernel(y_ref, rhs_ref, coords_ref, out_ref):
    start = pl.multiple_of(y_ref[0] * QUART, QUART)
    for leaf in range(LEAF_DEV):
        columns = slice(leaf * LEAF, (leaf + 1) * LEAF)
        out_ref[leaf, :R, :] = rhs_ref[:, columns]
        out_ref[leaf, R:, :] = coords_ref[pl.ds(start, QUART), columns]


def pack(y, rhs, coords):
    out = shaped((LEAF_DEV, ROWS, LEAF), BF16)
    return call(pack_kernel, 1, out, (y,), (rhs, coords), megabytes=8)


def square_rows(pieces, source):
    total = None
    for piece in pieces:
        wide = piece.astype(F32)
        part = jnp.sum(wide * wide, axis=0, keepdims=True)
        total = part if total is None else total + part
    total = total * -0.5
    high = total.astype(BF16).astype(F32)
    rest = total - high
    middle = rest.astype(BF16).astype(F32)
    low = rest - middle
    row = lax.broadcasted_iota(jnp.int32, (16, LEAF), 0)
    own = row if source else row - 3
    other = row - 3 if source else row
    block = jnp.where(own == 0, high, jnp.where(own == 1, middle, jnp.where(own == 2, low, 0.0)))
    block = jnp.where(jnp.logical_and(other >= 0, other < 3), 1.0, block)
    return block.astype(BF16)


def tile_product(target, spread, charges):
    exponent = jnp.dot(target, spread, preferred_element_type=F32)
    return nt(jnp.exp(exponent).astype(BF16), charges)


def own_kernel(y_ref, rhs_ref, coords_ref, target_ref, near_ref, spread_ref):
    y = y_ref[0]
    empty = jnp.zeros((AUG - FEAT - 16, LEAF), BF16)
    for leaf in range(LEAF_DEV):
        columns = slice(leaf * LEAF, (leaf + 1) * LEAF)
        pieces = []
        for shift in (0, NY - 1, 1, 2):
            start = pl.multiple_of(lax.rem(y + shift, NY) * QUART, QUART)
            pieces.append(coords_ref[pl.ds(start, QUART), columns])
        wide = jnp.concatenate(pieces + [square_rows(pieces, False), empty], axis=0)
        target_ref[leaf] = wide.astype(F32).T.astype(BF16)
        spread_ref[leaf, :FEAT, :] = jnp.concatenate(pieces, axis=0)
        spread_ref[leaf, FEAT : FEAT + 16, :] = square_rows(pieces, True)
        spread_ref[leaf, FEAT + 16 :, :] = empty

    def pair(i, carry):
        for leaf in (2 * i, 2 * i + 1):
            charges = rhs_ref[:, pl.ds(pl.multiple_of(leaf * LEAF, LEAF), LEAF)]
            near_ref[leaf] = tile_product(target_ref[leaf], spread_ref[leaf], charges)
        return carry

    lax.fori_loop(0, LEAF_DEV // 2, pair, 0)


def own_tiles(y, rhs, coords):
    out = [shaped((LEAF_DEV, LEAF, AUG), BF16), shaped((LEAF_DEV, LEAF, R), F32)]
    scratch = [pltpu.VMEM((LEAF_DEV, AUG, LEAF), BF16)]
    return call(own_kernel, 5, out, (y,), (rhs, coords), scratch)


UNROLL = 4


def near_kernel(chunks, take_ref, *refs):
    got_refs = refs[: len(chunks)]
    a_ref, b_ref, c_ref, target_ref, before_ref, near_ref, spread_ref = refs[len(chunks) :]
    near_ref[...] = before_ref[...]
    spread_ref[:, FEAT + 16 :, :] = jnp.zeros((UNROLL, AUG - FEAT - 16, LEAF), BF16)
    start = chunks[0][0]
    for (low, high), got_ref in zip(chunks, got_refs, strict=True):
        count = high - low

        def some(i, carry, low=low, count=count, got_ref=got_ref):
            for buffer in range(UNROLL):
                item = i * UNROLL + buffer
                source, slot = item // count, item % count
                which = take_ref[source, low + slot]
                place_of = low - start + slot
                pieces = [got_ref[source, slot, R:, :]]
                pieces += [ref[source, place_of] for ref in (a_ref, b_ref, c_ref)]
                for q, piece in enumerate(pieces):
                    spread_ref[buffer, q * QUART : (q + 1) * QUART, :] = piece
                spread_ref[buffer, FEAT : FEAT + 16, :] = square_rows(pieces, True)
                charges = got_ref[source, slot, :R, :]
                charges = jnp.where(which >= 0, charges, jnp.zeros_like(charges))
                leaf = jnp.maximum(which, 0)
                near_ref[leaf] += tile_product(target_ref[leaf], spread_ref[buffer], charges)
            return carry

        lax.fori_loop(0, GROUP * count // UNROLL, some, 0)


def near_chunk(chunks, take, got, others, targets, before):
    slots = sum(high - low for low, high in chunks)
    return call(
        functools.partial(near_kernel, chunks),
        3.2 * slots,
        shaped((LEAF_DEV, LEAF, R), F32),
        (take,),
        (*got, *others, targets, before),
        [pltpu.VMEM((UNROLL, AUG, LEAF), BF16)],
        32,
    )


def choose_kernel(first, halves, send_ref, *refs):
    out_ref = refs[-1]
    at = 0
    for slot, parts in enumerate(halves):
        for target in range(GROUP):
            item = send_ref[target, first + slot]
            size = refs[at].shape[0]
            block = refs[at][jnp.minimum(item, size - 1)]
            if parts == 2:
                block = jnp.where(item >= size, refs[at + 1][jnp.maximum(item - size, 0)], block)
            out_ref[target, slot] = block
        at += parts


def choose(first, send, sources):
    halves = tuple(len(s) for s in sources)
    shape = sources[0][0].shape[1:]
    out = shaped((GROUP, len(sources), *shape), BF16)
    arrays = [array for parts in sources for array in parts]
    kernel = functools.partial(choose_kernel, first, halves)
    return call(kernel, 1, out, (send,), arrays)


def skeleton_kernel(leaves_ref, basis_ref, one_ref, two_ref, out_ref):
    def rounded_dot(a, b):
        return jnp.dot(a, b, preferred_element_type=F32).astype(BF16)

    for leaf in range(LEAF_DEV):
        out_ref[leaf] = rounded_dot(leaves_ref[leaf, :R, :], basis_ref[leaf])
    for m in range(LEAF_DEV // 2):
        joined = jnp.concatenate([out_ref[2 * m], out_ref[2 * m + 1]], axis=1)
        out_ref[LEAF_DEV + m] = rounded_dot(joined, one_ref[m])
    for m in range(LEAF_DEV // 4):
        low = LEAF_DEV + 2 * m
        joined = jnp.concatenate([out_ref[low], out_ref[low + 1]], axis=1)
        out_ref[LEAF_DEV * 3 // 2 + m] = rounded_dot(joined, two_ref[m])


def skeletons(leaves, basis, one, two):
    out = shaped((NODE_DEV, R, RANK), BF16)
    return call(skeleton_kernel, 3, out, (), (leaves, basis, one, two))


def far_kernel(low, high, fresh, take_ref, got_ref, blocks_ref, *refs):
    out_ref = refs[-1]
    out_ref[...] = jnp.zeros_like(out_ref) if fresh else refs[0][...]
    count = high - low

    def source_of(source, carry):
        for slot in range(count):
            which = take_ref[source, low + slot]
            weights = got_ref[source, slot]
            weights = jnp.where(which >= 0, weights, jnp.zeros_like(weights))
            at = jnp.maximum(which, 0)
            out_ref[at // FAR] += jnp.dot(
                weights, blocks_ref[at], preferred_element_type=F32
            )
        return carry

    lax.fori_loop(0, GROUP, source_of, 0)


def far_chunk(low, high, take, got, blocks, before):
    fresh = before is None
    return call(
        functools.partial(far_kernel, low, high, fresh),
        high - low,
        shaped((NODE_DEV, R, RANK), F32),
        (take,),
        (got, blocks) + (() if fresh else (before,)),
    )


def finish_kernel(far_ref, one_ref, two_ref, basis_ref, near_ref, out_ref):
    for m in range(LEAF_DEV // 4):
        spread = nt(far_ref[LEAF_DEV * 3 // 2 + m].astype(BF16), two_ref[m])
        for side in range(2):
            node = 2 * m + side
            middle = far_ref[LEAF_DEV + node] + spread[:, side * RANK : (side + 1) * RANK]
            lower = nt(middle.astype(BF16), one_ref[node])
            for part in range(2):
                leaf = 2 * node + part
                lowest = far_ref[leaf] + lower[:, part * RANK : (part + 1) * RANK]
                columns = slice(leaf * LEAF, (leaf + 1) * LEAF)
                out_ref[:, columns] = near_ref[leaf].T + nt(lowest.astype(BF16), basis_ref[leaf])


def finish(far, one, two, basis, near):
    out = shaped((R, LEAF_DEV * LEAF), F32)
    return call(finish_kernel, 4, out, (), (far, one, two, basis, near))


def tables(neighbours, far_lists, x, z, c, group):
    offsets = jnp.asarray(OFFSETS, jnp.int32)
    there = (z + offsets + NZ) % NZ
    row_near = lax.dynamic_index_in_dim(
        neighbours.reshape(NX, NZ, NC, LEAF_DEV * NB), z, 1, keepdims=False
    ).reshape(GROUP, LEAF_DEV * NB)
    row_far = lax.dynamic_index_in_dim(
        far_lists.reshape(NX, NZ, NC, NODE_DEV * FAR), z, 1, keepdims=False
    ).reshape(GROUP, NODE_DEV * FAR)
    remote = jnp.arange(LEAF_DEV * NB, dtype=jnp.int32) % NB > 0
    near_owner = jnp.where(remote, row_near // LEAF_DEV, -1)
    far_owner = row_far // NODE_DEV
    mine = (x * NZ + there) * NC + c

    def pick(owner, value, sources):
        hit = owner[:, None, :] == sources[:, :, None]
        return jnp.sum(jnp.where(hit, value[:, None, :], 0), axis=2, dtype=jnp.int32)

    send_sources = jnp.broadcast_to(mine[None, :], (GROUP, NZ))
    send_leaf = pick(near_owner, row_near % LEAF_DEV, send_sources)
    send_node = pick(far_owner, row_far % NODE_DEV, send_sources)
    member = jnp.arange(GROUP, dtype=jnp.int32)
    seen = ((member // NC)[:, None] * NZ + there[None, :]) * NC + (member % NC)[:, None]
    own_near = lax.dynamic_index_in_dim(near_owner, group, 0, keepdims=True)
    own_far = lax.dynamic_index_in_dim(far_owner, group, 0, keepdims=True)
    near_value = jnp.arange(LEAF_DEV * NB, dtype=jnp.int32)[None, :] // NB + 1
    far_value = jnp.arange(NODE_DEV * FAR, dtype=jnp.int32)[None, :] + 1
    take_leaf = pick(own_near, near_value, seen) - 1
    take_node = pick(own_far, far_value, seen) - 1
    return send_leaf, send_node, take_leaf, take_node


def shift(value, step):
    return lax.ppermute(value, "leaf", ring(step))


def travel(payload, half):
    arrived = [(payload,)]
    up, down = payload, payload
    for _ in range(1, NZ // 2):
        up = shift(up, 1)
        down = shift(down, -1)
        arrived += [(up,), (down,)]
    last_up = shift(up[:half], 1)
    last_down = shift(down[half:], -1)
    arrived.append((last_up, last_down))
    return arrived


def exchange(chosen):
    return lax.all_to_all(
        chosen, "leaf", split_axis=0, concat_axis=0, axis_index_groups=ROW_GROUPS, tiled=True
    )


def join_planes(quarter):
    joined = []
    for step in (1, NY - 1, 2):
        joined.append(lax.ppermute(quarter, "rhs", [(i, (i + step) % NY) for i in range(NY)]))
    return joined


def on_device(coords, rhs, basis, transfer_one, transfer_two, far_blocks, neighbours, far_lists):
    me = lax.axis_index("leaf").astype(jnp.int32)
    y = lax.axis_index("rhs").astype(jnp.int32).reshape(1)
    c, z, x = me % NC, (me // NC) % NZ, me // (NC * NZ)
    group = x * NC + c
    payload = pack(y, rhs, coords)
    leaves = travel(payload, LEAF_DEV // 2)
    nodes = travel(skeletons(payload, basis, transfer_one, transfer_two), NODE_DEV // 2)
    send_leaf, send_node, take_leaf, take_node = tables(neighbours, far_lists, x, z, c, group)
    targets, near = own_tiles(y, rhs, coords)
    blocks = far_blocks.reshape(NODE_DEV * FAR, RANK, RANK)
    far = None
    for chunks in LEAF_CHUNKS:
        got = [exchange(choose(low, send_leaf, leaves[low:high])) for low, high in chunks]
        quarter = [part[:, :, R:, :] for part in got]
        quarter = quarter[0] if len(quarter) == 1 else jnp.concatenate(quarter, axis=1)
        others = join_planes(quarter)
        near = near_chunk(chunks, take_leaf, got, others, targets, near)
    for low, high in NODE_CHUNKS:
        got = exchange(choose(low, send_node, nodes[low:high]))
        far = far_chunk(low, high, take_node, got, blocks, far)
    return finish(far, transfer_one, transfer_two, basis, near)


def solution(mesh):
    return jax.shard_map(
        on_device,
        mesh=mesh,
        in_specs=(
            P(None, "leaf"),
            P("rhs", "leaf"),
            P("leaf", None, None),
            P("leaf", None, None),
            P("leaf", None, None),
            P("leaf", None, None, None),
            P(),
            P(),
        ),
        out_specs=P("rhs", "leaf"),
        check_vma=False,
    )
```

time: 436 us -> 241 us (0.55)
  other arithmetic: 86.7 us -> 2.18 us
  waiting for transfers between devices: 171 us -> 93.3 us
  local copies, waits for them, and re-layouts: 92.1 us -> 24.3 us
  matrix products: 58.4 us -> 0 us
  starting transfers between devices: 23.9 us -> 72.1 us
  Pallas kernels: 0 us -> 45.7 us
    all_to_all x2 -> x6, waiting for transfers between devices: 171 us -> 7.29 us  [exchange(): lax.all_to_all(chosen, 'leaf', split_axis=0, concat_axis=0, axis_index_gr...]
    ppermute x0 -> x25, waiting for transfers between devices: none -> 86 us  [the longest x16 74.3 us: shift(): return lax.ppermute(value, 'leaf', ring(step))]
    dot_general x22 -> x0, matrix products: 58.4 us -> none  [the longest x15 48.5 us: tile_products(): jnp.einsum('gra,gab->grb', sources[:, FEAT:], kernel, preferred_element_t...]
    scatter-add x2 -> x0, other arithmetic: 50.9 us -> none  [arrivals(): jnp.nonzero((owners == device_index).reshape(-1), size=entry_count, fill_...]
    pallas_call x0 -> x15, Pallas kernels: none -> 45.7 us  [call(): pl.pallas_call(kernel, in_specs=[SMEM] * len(tables) + [VMEM] * len(array...]
    ppermute x0 -> x25, starting transfers between devices: none -> 38 us  [the longest x16 25.1 us: shift(): return lax.ppermute(value, 'leaf', ring(step))]
    scatter x2 -> x0, local copies, waits for them, and re-layouts: 29.3 us -> none  [the longest x1 19.6 us: on_device(): leaf_buffer = jnp.zeros((peer_count * near_slots, FEAT + R, LEAF), jnp.bf...]
    gather x12 -> x0, local copies, waits for them, and re-layouts: 26.2 us -> none  [the longest x1 8.69 us: on_device(): leaf_arrived.reshape(peer_count * near_slots, FEAT + R, LEAF)[my_slots]]
  transfers between devices with their start and end apart: 2 -> 31, of which waited for: 1 -> 14; matrix products, arithmetic and copies ran while one was open for 17% -> 3% of each run, Pallas kernels for 0% -> 15%
where the time goes in v1:
time: 241 us; the launch traced here: 238 us
  waiting for transfers between devices  93.3 us (39%)
  starting transfers between devices  72.1 us (30%)
  Pallas kernels  45.7 us (19%)
  local copies, waits for them, and re-layouts  24.3 us (10%)
    ppermute x16, waiting for transfers between devices, shift(): return lax.ppermute(value, 'leaf', ring(step))  74.3 us
    pallas_call x15, Pallas kernels, call(): pl.pallas_call(kernel, in_specs=[SMEM] * len(tables) + [VMEM] * len(array...  45.7 us
    all_to_all x6, starting transfers between devices, exchange(): lax.all_to_all(chosen, 'leaf', split_axis=0, concat_axis=0, axis_index_gr...  34.1 us
    ppermute x16, starting transfers between devices, shift(): return lax.ppermute(value, 'leaf', ring(step))  25.1 us
    unnamed x72, local copies, waits for them, and re-layouts  20.3 us
    ppermute x9, starting transfers between devices, join_planes(): lax.ppermute(quarter, 'rhs', [(i, (i + step) % NY) for i in range(NY)])  12.9 us
    ppermute x9, waiting for transfers between devices, join_planes(): lax.ppermute(quarter, 'rhs', [(i, (i + step) % NY) for i in range(NY)])  11.7 us
    all_to_all x6, waiting for transfers between devices, exchange(): lax.all_to_all(chosen, 'leaf', split_axis=0, concat_axis=0, axis_index_gr...  7.29 us
  transfers between devices with their start and end apart: 31, of which 14 were waited for; matrix products, arithmetic and copies ran while one was open for 3% of the time, Pallas kernels for 15%

profile of v1, /device:TPU:1, one launch (start us, length us, event | category | flops | bytes accessed | tf_op | source)
XLA Modules:
  0.0 238.0 jit_solution(4344303391840788538)
XLA Ops:
  4.1 2.5 %collective-permute-start = (bf16[14,64,256]{2,1,0:T(8,128)(2,1)S(1)}, bf16[14,64,256]{2,1,0:T(8,128)(2,1)S(1)}, u32[]{:S(2)}, u32[]{:S(2)}) collective-permute-start(bf16[14,64,256]{2,1,0:T(8,128)(2,1)S(1)} %shard_map.92.refs_0_), channel_id=1, source_target_pairs={{0,8},{4,12},{8,16},{12,20},{16,24},{20,28},{24,32},{28,36},{32,40... | collective-permute-start | bytes 1376264 | tf_op jit(solution)/shard_map/ppermute | solution.py:314
  6.6 4.0 %collective-permute-start.3 = (bf16[14,64,256]{2,1,0:T(8,128)(2,1)S(1)}, bf16[14,64,256]{2,1,0:T(8,128)(2,1)S(1)}, u32[]{:S(2)}, u32[]{:S(2)}) collective-permute-start(bf16[14,64,256]{2,1,0:T(8,128)(2,1)S(1)} %shard_map.92.refs_0_), channel_id=1, source_target_pairs={{0,56},{4,60},{8,0},{12,4},{16,8},{20,12},{24,16},{28,20},{32,24},... | collective-permute-start | bytes 1376264 | tf_op jit(solution)/shard_map/ppermute | solution.py:314
  11.1 9.7 %collective-permute-done.refs_1_ = bf16[14,64,256]{2,1,0:T(8,128)(2,1)S(1)} collective-permute-done((bf16[14,64,256]{2,1,0:T(8,128)(2,1)S(1)}, bf16[14,64,256]{2,1,0:T(8,128)(2,1)S(1)}, u32[]{:S(2)}, u32[]{:S(2)}) %collective-permute-start) | collective-permute-done | bytes 458784 | tf_op jit(solution)/shard_map/ppermute | solution.py:314
  20.8 2.7 %collective-permute-start.4 = (bf16[14,64,256]{2,1,0:T(8,128)(2,1)S(1)}, bf16[14,64,256]{2,1,0:T(8,128)(2,1)S(1)}, u32[]{:S(2)}, u32[]{:S(2)}) collective-permute-start(bf16[14,64,256]{2,1,0:T(8,128)(2,1)S(1)} %collective-permute-done.3.refs_2_), channel_id=1, source_target_pairs={{0,56},{4,60},{8,0},{12,4},{16,8},{20,12},{24,16},{28,20},{32,24},... | collective-permute-start | bytes 1376264 | tf_op jit(solution)/shard_map/ppermute | solution.py:314
  23.8 9.1 %collective-permute-done.1.refs_3_ = bf16[14,64,256]{2,1,0:T(8,128)(2,1)} collective-permute-done((bf16[14,64,256]{2,1,0:T(8,128)(2,1)S(1)}, bf16[14,64,256]{2,1,0:T(8,128)(2,1)}, u32[]{:S(2)}, u32[]{:S(2)}) %collective-permute-start.1) | collective-permute-done | bytes 458784 | tf_op jit(solution)/shard_map/ppermute | solution.py:314
  32.9 2.4 shard_map.94
  35.3 6.4 %all-to-all-start.1 = ((bf16[8,5,64,256]{3,2,1,0:T(8,128)(2,1)}), bf16[8,5,64,256]{3,2,1,0:T(8,128)(2,1)S(1)}, u32[]{:S(2)}, u32[]{:S(2)}) async-start(bf16[8,5,64,256]{3,2,1,0:T(8,128)(2,1)} %shard_map.94), calls=%async_computation.1 | async-start | bytes 2621440 | tf_op jit(solution)/shard_map/all_to_all | solution.py:331
  41.7 2.7 %collective-permute-start.5 = (bf16[14,64,256]{2,1,0:T(8,128)(2,1)}, bf16[14,64,256]{2,1,0:T(8,128)(2,1)S(1)}, u32[]{:S(2)}, u32[]{:S(2)}) collective-permute-start(bf16[14,64,256]{2,1,0:T(8,128)(2,1)} %copy-done.24), channel_id=1, source_target_pairs={{0,56},{4,60},{8,0},{12,4},{16,8},{20,12},{24,16},{28,20},{32,24},... | collective-permute-start | bytes 1376264 | tf_op jit(solution)/shard_map/ppermute | solution.py:314
  44.4 10.8 %collective-permute-done.2.refs_0_ = bf16[14,64,256]{2,1,0:T(8,128)(2,1)S(1)} collective-permute-done((bf16[14,64,256]{2,1,0:T(8,128)(2,1)}, bf16[14,64,256]{2,1,0:T(8,128)(2,1)S(1)}, u32[]{:S(2)}, u32[]{:S(2)}) %collective-permute-start.2) | collective-permute-done | bytes 458784 | tf_op jit(solution)/shard_map/ppermute | solution.py:314
  55.4 2.7 %collective-permute-start.7 = (bf16[7,64,256]{2,1,0:T(8,128)(2,1)S(1)}, bf16[7,64,256]{2,1,0:T(8,128)(2,1)S(1)}, u32[]{:S(2)}, u32[]{:S(2)}) collective-permute-start(bf16[7,64,256]{2,1,0:T(8,128)(2,1)S(1)} %slice.33), channel_id=1, source_target_pairs={{0,56},{4,60},{8,0},{12,4},{16,8},{20,12},{24,16},{28,20},{32,24},... | collective-permute-start | bytes 688136 | tf_op jit(solution)/shard_map/ppermute | solution.py:314
  58.2 1.3 collective-permute-start.8
  59.6 3.3 %collective-permute-done.6.refs_2_ = bf16[7,64,256]{2,1,0:T(8,128)(2,1)S(1)} collective-permute-done((bf16[7,64,256]{2,1,0:T(8,128)(2,1)S(1)}, bf16[7,64,256]{2,1,0:T(8,128)(2,1)S(1)}, u32[]{:S(2)}, u32[]{:S(2)}) %collective-permute-start.6) | collective-permute-done | bytes 229408 | tf_op jit(solution)/shard_map/ppermute | solution.py:314
  62.8 1.5 shard_map.93
  64.4 7.4 %all-to-all-start = ((bf16[8,3,64,256]{3,2,1,0:T(8,128)(2,1)}), bf16[8,3,64,256]{3,2,1,0:T(8,128)(2,1)S(1)}, u32[]{:S(2)}, u32[]{:S(2)}) async-start(bf16[8,3,64,256]{3,2,1,0:T(8,128)(2,1)} %shard_map.93), calls=%async_computation | async-start | bytes 1572864 | tf_op jit(solution)/shard_map/all_to_all | solution.py:331
  74.1 2.2 collective-permute-done.12.refs_2_
  77.0 2.5 %shard_map.100 = bf16[8,3,80,512]{3,2,1,0:T(8,128)(2,1)} custom-call(s32[8,8]{1,0:T(8,128)S(1)} %select_reduce_fusion.send_ref, bf16[8,80,512]{2,1,0:T(8,128)(2,1)S(1)} %shard_map.91.leaves_ref.refs_0_, bf16[8,80,512]{2,1,0:T(8,128)(2,1)} %collective-permute-done.8.refs_1_, bf16[8,80,512]{2,1,0:T(8,128)(2,1)S(1)} %collective-permute-done.12.refs_2_), custom_call_target="tpu_custom_call" | custom-call | flops 1000000000 | tf_op jit(solution)/shard_map/pallas_call | solution.py:58
  79.5 4.5 %all-to-all-done.got_ref = bf16[8,3,64,256]{3,2,1,0:T(8,128)(2,1)S(1)} async-done(((bf16[8,3,64,256]{3,2,1,0:T(8,128)(2,1)}), bf16[8,3,64,256]{3,2,1,0:T(8,128)(2,1)S(1)}, u32[]{:S(2)}, u32[]{:S(2)}) %all-to-all-start) | async-done | bytes 786464 | tf_op jit(solution)/shard_map/all_to_all | solution.py:331
  84.9 4.5 %all-to-all-start.4 = ((bf16[8,3,80,512]{3,2,1,0:T(8,128)(2,1)}), bf16[8,3,80,512]{3,2,1,0:T(8,128)(2,1)S(1)}, u32[]{:S(2)}, u32[]{:S(2)}) async-start(bf16[8,3,80,512]{3,2,1,0:T(8,128)(2,1)} %shard_map.100), calls=%async_computation.4 | async-start | bytes 3932160 | tf_op jit(solution)/shard_map/all_to_all | solution.py:331
  89.3 3.1 %collective-permute-start.13 = (bf16[8,80,512]{2,1,0:T(8,128)(2,1)S(1)}, bf16[8,80,512]{2,1,0:T(8,128)(2,1)S(1)}, u32[]{:S(2)}, u32[]{:S(2)}) collective-permute-start(bf16[8,80,512]{2,1,0:T(8,128)(2,1)S(1)} %collective-permute-done.12.refs_2_), channel_id=1, source_target_pairs={{0,56},{4,60},{8,0},{12,4},{16,8},{20,12},{24,16},{28,20},{32,24},... | collective-permute-start | bytes 1966088 | tf_op jit(solution)/shard_map/ppermute | solution.py:314
  92.4 13.9 %collective-permute-done.13.refs_1_ = bf16[8,80,512]{2,1,0:T(8,128)(2,1)S(1)} collective-permute-done((bf16[8,80,512]{2,1,0:T(8,128)(2,1)S(1)}, bf16[8,80,512]{2,1,0:T(8,128)(2,1)S(1)}, u32[]{:S(2)}, u32[]{:S(2)}) %collective-permute-start.13) | collective-permute-done | bytes 655392 | tf_op jit(solution)/shard_map/ppermute | solution.py:314
  106.3 3.3 %collective-permute-done.9.refs_0_ = bf16[8,80,512]{2,1,0:T(8,128)(2,1)S(1)} collective-permute-done((bf16[8,80,512]{2,1,0:T(8,128)(2,1)}, bf16[8,80,512]{2,1,0:T(8,128)(2,1)S(1)}, u32[]{:S(2)}, u32[]{:S(2)}) %collective-permute-start.9) | collective-permute-done | bytes 655392 | tf_op jit(solution)/shard_map/ppermute | solution.py:314
  112.3 1.9 all-to-all-done.4.refs_0_
  114.2 4.4 %all-to-all-start.5 = ((bf16[8,2,80,512]{3,2,1,0:T(8,128)(2,1)}), bf16[8,2,80,512]{3,2,1,0:T(8,128)(2,1)S(1)}, u32[]{:S(2)}, u32[]{:S(2)}) async-start(bf16[8,2,80,512]{3,2,1,0:T(8,128)(2,1)} %copy-done.2), calls=%async_computation.5 | async-start | bytes 2621440 | tf_op jit(solution)/shard_map/all_to_all | solution.py:331
  119.3 2.4 collective-permute-start.14
  122.1 14.6 %collective-permute-done.10.refs_0_ = bf16[8,80,512]{2,1,0:T(8,128)(2,1)S(1)} collective-permute-done((bf16[8,80,512]{2,1,0:T(8,128)(2,1)}, bf16[8,80,512]{2,1,0:T(8,128)(2,1)S(1)}, u32[]{:S(2)}, u32[]{:S(2)}) %collective-permute-start.10) | collective-permute-done | bytes 655392 | tf_op jit(solution)/shard_map/ppermute | solution.py:314
  136.8 2.7 %collective-permute-start.15 = (bf16[4,80,512]{2,1,0:T(8,128)(2,1)S(1)}, bf16[4,80,512]{2,1,0:T(8,128)(2,1)S(1)}, u32[]{:S(2)}, u32[]{:S(2)}) collective-permute-start(bf16[4,80,512]{2,1,0:T(8,128)(2,1)S(1)} %slice.35), channel_id=1, source_target_pairs={{0,56},{4,60},{8,0},{12,4},{16,8},{20,12},{24,16},{28,20},{32,24},... | collective-permute-start | bytes 983048 | tf_op jit(solution)/shard_map/ppermute | solution.py:314
  139.5 6.7 %collective-permute-done.11.refs_0_ = bf16[4,80,512]{2,1,0:T(8,128)(2,1)S(1)} collective-permute-done((bf16[4,80,512]{2,1,0:T(8,128)(2,1)S(1)}, bf16[4,80,512]{2,1,0:T(8,128)(2,1)S(1)}, u32[]{:S(2)}, u32[]{:S(2)}) %collective-permute-start.11) | collective-permute-done | bytes 327712 | tf_op jit(solution)/shard_map/ppermute | solution.py:314
  147.8 6.2 %all-to-all-start.2 = ((bf16[8,1,80,512]{3,2,1,0:T(8,128)(2,1)}), bf16[8,1,80,512]{3,2,1,0:T(8,128)(2,1)}, u32[]{:S(2)}, u32[]{:S(2)}) async-start(bf16[8,1,80,512]{3,2,1,0:T(8,128)(2,1)} %copy-done.6), calls=%async_computation.2 | async-start | bytes 1310720 | tf_op jit(solution)/shard_map/all_to_all | solution.py:331
  156.2 3.7 %shard_map.98 = (bf16[8,512,128]{2,1,0:T(8,128)(2,1)S(1)}, f32[8,512,64]{2,1,0:T(8,128)S(1)}) custom-call(s32[1]{0:T(128)} %bitcast.3.y_ref, bf16[64,4096]{1,0:T(8,128)(2,1)S(1)} %copy-done.19, bf16[64,4096]{1,0:T(8,128)(2,1)S(1)} %copy-done.21), custom_call_target="tpu_custom_call" | custom-call | flops 5000000000 | tf_op jit(solution)/shard_map/pallas_call | solution.py:58
  160.9 1.3 copy-done.30
  164.9 5.1 %all-to-all-start.3 = ((bf16[8,2,80,512]{3,2,1,0:T(8,128)(2,1)}), bf16[8,2,80,512]{3,2,1,0:T(8,128)(2,1)}, u32[]{:S(2)}, u32[]{:S(2)}) async-start(bf16[8,2,80,512]{3,2,1,0:T(8,128)(2,1)} %copy-done.3), calls=%async_computation.3 | async-start | bytes 2621440 | tf_op jit(solution)/shard_map/all_to_all | solution.py:331
  171.3 1.3 collective-permute-start.22
  172.6 1.4 collective-permute-start.23
  174.0 1.6 collective-permute-start.24
  175.7 3.1 %copy-done.11 = bf16[14,4,256,256]{3,2,1,0:T(8,128)(2,1)S(1)} copy-done((bf16[14,4,256,256]{3,2,1,0:T(8,128)(2,1)S(1)}, bf16[14,4,256,256]{3,2,1,0:T(8,128)(2,1)}, u32[]{:S(2)}) %copy-start.11) | copy-done | bytes 7340056
  178.8 2.6 %shard_map.95.refs_0_ = f32[14,64,256]{2,1,0:T(8,128)S(1)} custom-call(s32[8,8]{1,0:T(8,128)S(1)} %broadcast_add_fusion.1.take_ref, bf16[8,5,64,256]{3,2,1,0:T(8,128)(2,1)S(1)} %copy-done.1, bf16[56,256,256]{2,1,0:T(8,128)(2,1)S(1)} %bitcast.9), custom_call_target="tpu_custom_call" | custom-call | flops 5000000000 | tf_op jit(solution)/shard_map/pallas_call | solution.py:58
  181.4 2.3 shard_map.96.far_ref
  184.6 1.6 slice.36
  186.6 2.3 collective-permute-start.17
  190.3 2.3 collective-permute-start.20
  192.6 11.7 %collective-permute-done.24.refs_4_ = bf16[8,5,16,512]{3,2,1,0:T(8,128)(2,1)} collective-permute-done((bf16[8,5,16,512]{3,2,1,0:T(8,128)(2,1)}, bf16[8,5,16,512]{3,2,1,0:T(8,128)(2,1)}, u32[]{:S(2)}, u32[]{:S(2)}) %collective-permute-start.24) | collective-permute-done | bytes 655392 | tf_op jit(solution)/shard_map/ppermute | solution.py:339
  204.7 1.2 copy-done.28
  205.9 1.6 copy-done.31
  207.5 14.6 %shard_map.102.refs_5_ = f32[8,512,64]{2,1,0:T(8,128)S(1)} custom-call(s32[8,8]{1,0:T(8,128)S(1)} %broadcast_add_fusion.take_ref, bf16[8,3,80,512]{3,2,1,0:T(8,128)(2,1)S(1)} %all-to-all-done.4.refs_0_, bf16[8,2,80,512]{3,2,1,0:T(8,128)(2,1)S(1)} %all-to-all-done.5.refs_1_, bf16[8,5,16,512]{3,2,1,0:T(8,128)(2,1)} %collective-permute-done.22.refs_2_, ...), custom_call_target="tpu_custom_call" | custom-call | flops 16000000000 | tf_op jit(solution)/shard_map/pallas_call | solution.py:58
  222.1 2.7 %collective-permute-start.18 = (bf16[8,1,16,512]{3,2,1,0:T(8,128)(2,1)}, bf16[8,1,16,512]{3,2,1,0:T(8,128)(2,1)S(1)}, u32[]{:S(2)}, u32[]{:S(2)}) collective-permute-start(bf16[8,1,16,512]{3,2,1,0:T(8,128)(2,1)} %slice.36), channel_id=1, source_target_pairs={{0,2},{1,3},{2,0},{3,1},{4,6},{5,7},{6,4},{7,5},{8,10},{9,11},{10,... | collective-permute-start | bytes 393224 | tf_op jit(solution)/shard_map/ppermute | solution.py:339
  224.8 6.6 %shard_map.103.refs_5_ = f32[8,512,64]{2,1,0:T(8,128)S(1)} custom-call(s32[8,8]{1,0:T(8,128)S(1)} %broadcast_add_fusion.take_ref, bf16[8,2,80,512]{3,2,1,0:T(8,128)(2,1)} %all-to-all-done.3.refs_0_, bf16[8,2,16,512]{3,2,1,0:T(8,128)(2,1)S(1)} %collective-permute-done.19.refs_1_, bf16[8,2,16,512]{3,2,1,0:T(8,128)(2,1)S(1)} %collective-permute-done.20.refs_2_, ...), custom_call_target="tpu_custom_call" | custom-call | flops 6400000000 | tf_op jit(solution)/shard_map/pallas_call | solution.py:58
  231.6 4.0 %shard_map.104.near_ref = f32[8,512,64]{2,1,0:T(8,128)S(1)} custom-call(s32[8,8]{1,0:T(8,128)S(1)} %broadcast_add_fusion.take_ref, bf16[8,1,80,512]{3,2,1,0:T(8,128)(2,1)} %all-to-all-done.2.refs_0_, bf16[8,1,16,512]{3,2,1,0:T(8,128)(2,1)S(1)} %collective-permute-done.16.refs_1_, bf16[8,1,16,512]{3,2,1,0:T(8,128)(2,1)S(1)} %collective-permute-done.17.refs_2_, ...), custom_call_target="tpu_custom_call" | custom-call | flops 3200000000 | tf_op jit(solution)/shard_map/pallas_call | solution.py:58
  235.6 2.5 %shard_map.105 = f32[64,4096]{1,0:T(8,128)} custom-call(f32[14,64,256]{2,1,0:T(8,128)S(1)} %copy-done.26, bf16[4,512,256]{2,1,0:T(8,128)(2,1)S(1)} %copy-done.15, bf16[2,512,256]{2,1,0:T(8,128)(2,1)S(1)} %copy-done.23, bf16[8,512,256]{2,1,0:T(8,128)(2,1)S(1)} %copy-done.13, f32[8,512,64]{2,1,0:T(8,128)S(1)} %shard_map.104.near_ref), custom_call_target="tpu_custom_call" | custom-call | flops 4000000000 | tf_op jit(solution)/shard_map/pallas_call | solution.py:58
  (132 shorter events, 24.4 us)
Async XLA Ops:
  3.3 7.4 %copy-start.33 = (s32[896,4]{0,1:T(4,128)S(1)}, s32[896,4]{0,1:T(4,128)}, u32[]{:S(2)}) copy-start(s32[896,4]{0,1:T(4,128)} %param.16) | copy-start | bytes 43012
  3.3 7.8 %copy-start.34 = (s32[8]{0:T(128)S(1)}, s32[8]{0:T(128)}, u32[]{:S(2)}) copy-start(s32[8]{0:T(128)} %constant.165.clone) | copy-start | bytes 100
  4.1 16.7 %collective-permute-start = (bf16[14,64,256]{2,1,0:T(8,128)(2,1)S(1)}, bf16[14,64,256]{2,1,0:T(8,128)(2,1)S(1)}, u32[]{:S(2)}, u32[]{:S(2)}) collective-permute-start(bf16[14,64,256]{2,1,0:T(8,128)(2,1)S(1)} %shard_map.92.refs_0_), channel_id=1, source_target_pairs={{0,8},{4,12},{8,16},{12,20},{16,24},{20,28},{24,32},{28,36},{32,40... | collective-permute-start | bytes 1376264 | tf_op jit(solution)/shard_map/ppermute | solution.py:314
  6.6 14.2 %collective-permute-start.3 = (bf16[14,64,256]{2,1,0:T(8,128)(2,1)S(1)}, bf16[14,64,256]{2,1,0:T(8,128)(2,1)S(1)}, u32[]{:S(2)}, u32[]{:S(2)}) collective-permute-start(bf16[14,64,256]{2,1,0:T(8,128)(2,1)S(1)} %shard_map.92.refs_0_), channel_id=1, source_target_pairs={{0,56},{4,60},{8,0},{12,4},{16,8},{20,12},{24,16},{28,20},{32,24},... | collective-permute-start | bytes 1376264 | tf_op jit(solution)/shard_map/ppermute | solution.py:314
  20.8 12.1 %collective-permute-start.1 = (bf16[14,64,256]{2,1,0:T(8,128)(2,1)S(1)}, bf16[14,64,256]{2,1,0:T(8,128)(2,1)}, u32[]{:S(2)}, u32[]{:S(2)}) collective-permute-start(bf16[14,64,256]{2,1,0:T(8,128)(2,1)S(1)} %collective-permute-done.refs_1_), channel_id=1, source_target_pairs={{0,8},{4,12},{8,16},{12,20},{16,24},{20,28},{24,32},{28,36},{32,40... | collective-permute-start | bytes 1376264 | tf_op jit(solution)/shard_map/ppermute | solution.py:314
  20.8 12.1 %collective-permute-start.4 = (bf16[14,64,256]{2,1,0:T(8,128)(2,1)S(1)}, bf16[14,64,256]{2,1,0:T(8,128)(2,1)S(1)}, u32[]{:S(2)}, u32[]{:S(2)}) collective-permute-start(bf16[14,64,256]{2,1,0:T(8,128)(2,1)S(1)} %collective-permute-done.3.refs_2_), channel_id=1, source_target_pairs={{0,56},{4,60},{8,0},{12,4},{16,8},{20,12},{24,16},{28,20},{32,24},... | collective-permute-start | bytes 1376264 | tf_op jit(solution)/shard_map/ppermute | solution.py:314
  35.3 29.1 %all-to-all-start.1 = ((bf16[8,5,64,256]{3,2,1,0:T(8,128)(2,1)}), bf16[8,5,64,256]{3,2,1,0:T(8,128)(2,1)S(1)}, u32[]{:S(2)}, u32[]{:S(2)}) async-start(bf16[8,5,64,256]{3,2,1,0:T(8,128)(2,1)} %shard_map.94), calls=%async_computation.1 | async-start | bytes 2621440 | tf_op jit(solution)/shard_map/all_to_all | solution.py:331
  41.7 13.5 %collective-permute-start.2 = (bf16[14,64,256]{2,1,0:T(8,128)(2,1)}, bf16[14,64,256]{2,1,0:T(8,128)(2,1)S(1)}, u32[]{:S(2)}, u32[]{:S(2)}) collective-permute-start(bf16[14,64,256]{2,1,0:T(8,128)(2,1)} %collective-permute-done.1.refs_3_), channel_id=1, source_target_pairs={{0,8},{4,12},{8,16},{12,20},{16,24},{20,28},{24,32},{28,36},{32,40... | collective-permute-start | bytes 1376264 | tf_op jit(solution)/shard_map/ppermute | solution.py:314
  41.7 13.6 %collective-permute-start.5 = (bf16[14,64,256]{2,1,0:T(8,128)(2,1)}, bf16[14,64,256]{2,1,0:T(8,128)(2,1)S(1)}, u32[]{:S(2)}, u32[]{:S(2)}) collective-permute-start(bf16[14,64,256]{2,1,0:T(8,128)(2,1)} %copy-done.24), channel_id=1, source_target_pairs={{0,56},{4,60},{8,0},{12,4},{16,8},{20,12},{24,16},{28,20},{32,24},... | collective-permute-start | bytes 1376264 | tf_op jit(solution)/shard_map/ppermute | solution.py:314
  55.2 7.6 %collective-permute-start.6 = (bf16[7,64,256]{2,1,0:T(8,128)(2,1)S(1)}, bf16[7,64,256]{2,1,0:T(8,128)(2,1)S(1)}, u32[]{:S(2)}, u32[]{:S(2)}) collective-permute-start(bf16[7,64,256]{2,1,0:T(8,128)(2,1)S(1)} %slice.32), channel_id=1, source_target_pairs={{0,8},{4,12},{8,16},{12,20},{16,24},{20,28},{24,32},{28,36},{32,40... | collective-permute-start | bytes 688136 | tf_op jit(solution)/shard_map/ppermute | solution.py:314
  55.4 16.5 %copy-start.32 = (s32[512,8]{0,1:T(8,128)S(1)}, s32[512,8]{0,1:T(8,128)}, u32[]{:S(2)}) copy-start(s32[512,8]{0,1:T(8,128)} %param.15) | copy-start | bytes 49156
  55.4 7.5 %collective-permute-start.7 = (bf16[7,64,256]{2,1,0:T(8,128)(2,1)S(1)}, bf16[7,64,256]{2,1,0:T(8,128)(2,1)S(1)}, u32[]{:S(2)}, u32[]{:S(2)}) collective-permute-start(bf16[7,64,256]{2,1,0:T(8,128)(2,1)S(1)} %slice.33), channel_id=1, source_target_pairs={{0,56},{4,60},{8,0},{12,4},{16,8},{20,12},{24,16},{28,20},{32,24},... | collective-permute-start | bytes 688136 | tf_op jit(solution)/shard_map/ppermute | solution.py:314
  58.1 18.2 %collective-permute-start.12 = (bf16[8,80,512]{2,1,0:T(8,128)(2,1)S(1)}, bf16[8,80,512]{2,1,0:T(8,128)(2,1)S(1)}, u32[]{:S(2)}, u32[]{:S(2)}) collective-permute-start(bf16[8,80,512]{2,1,0:T(8,128)(2,1)S(1)} %shard_map.91.leaves_ref.refs_0_), channel_id=1, source_target_pairs={{0,56},{4,60},{8,0},{12,4},{16,8},{20,12},{24,16},{28,20},{32,24},... | collective-permute-start | bytes 1966088 | tf_op jit(solution)/shard_map/ppermute | solution.py:314
  58.2 18.7 %collective-permute-start.8 = (bf16[8,80,512]{2,1,0:T(8,128)(2,1)S(1)}, bf16[8,80,512]{2,1,0:T(8,128)(2,1)}, u32[]{:S(2)}, u32[]{:S(2)}) collective-permute-start(bf16[8,80,512]{2,1,0:T(8,128)(2,1)S(1)} %shard_map.91.leaves_ref.refs_0_), channel_id=1, source_target_pairs={{0,8},{4,12},{8,16},{12,20},{16,24},{20,28},{24,32},{28,36},{32,40... | collective-permute-start | bytes 1966088 | tf_op jit(solution)/shard_map/ppermute | solution.py:314
  64.4 15.1 %copy-start = (bf16[8,5,64,256]{3,2,1,0:T(8,128)(2,1)}, bf16[8,5,64,256]{3,2,1,0:T(8,128)(2,1)S(1)}, u32[]{:S(2)}) copy-start(bf16[8,5,64,256]{3,2,1,0:T(8,128)(2,1)S(1)} %all-to-all-done.1.got_ref) | copy-start | bytes 3932164
  64.4 19.6 %all-to-all-start = ((bf16[8,3,64,256]{3,2,1,0:T(8,128)(2,1)}), bf16[8,3,64,256]{3,2,1,0:T(8,128)(2,1)S(1)}, u32[]{:S(2)}, u32[]{:S(2)}) async-start(bf16[8,3,64,256]{3,2,1,0:T(8,128)(2,1)} %shard_map.93), calls=%async_computation | async-start | bytes 1572864 | tf_op jit(solution)/shard_map/all_to_all | solution.py:331
  84.9 29.3 %all-to-all-start.4 = ((bf16[8,3,80,512]{3,2,1,0:T(8,128)(2,1)}), bf16[8,3,80,512]{3,2,1,0:T(8,128)(2,1)S(1)}, u32[]{:S(2)}, u32[]{:S(2)}) async-start(bf16[8,3,80,512]{3,2,1,0:T(8,128)(2,1)} %shard_map.100), calls=%async_computation.4 | async-start | bytes 3932160 | tf_op jit(solution)/shard_map/all_to_all | solution.py:331
  89.3 17.0 %collective-permute-start.13 = (bf16[8,80,512]{2,1,0:T(8,128)(2,1)S(1)}, bf16[8,80,512]{2,1,0:T(8,128)(2,1)S(1)}, u32[]{:S(2)}, u32[]{:S(2)}) collective-permute-start(bf16[8,80,512]{2,1,0:T(8,128)(2,1)S(1)} %collective-permute-done.12.refs_2_), channel_id=1, source_target_pairs={{0,56},{4,60},{8,0},{12,4},{16,8},{20,12},{24,16},{28,20},{32,24},... | collective-permute-start | bytes 1966088 | tf_op jit(solution)/shard_map/ppermute | solution.py:314
  92.4 17.2 %collective-permute-start.9 = (bf16[8,80,512]{2,1,0:T(8,128)(2,1)}, bf16[8,80,512]{2,1,0:T(8,128)(2,1)S(1)}, u32[]{:S(2)}, u32[]{:S(2)}) collective-permute-start(bf16[8,80,512]{2,1,0:T(8,128)(2,1)} %collective-permute-done.8.refs_1_), channel_id=1, source_target_pairs={{0,8},{4,12},{8,16},{12,20},{16,24},{20,28},{24,32},{28,36},{32,40... | collective-permute-start | bytes 1966088 | tf_op jit(solution)/shard_map/ppermute | solution.py:314
  106.3 7.9 %copy-start.16 = (bf16[8,80,512]{2,1,0:T(8,128)(2,1)}, bf16[8,80,512]{2,1,0:T(8,128)(2,1)S(1)}, u32[]{:S(2)}) copy-start(bf16[8,80,512]{2,1,0:T(8,128)(2,1)S(1)} %collective-permute-done.13.refs_1_) | copy-start | bytes 1966084
  114.2 33.7 %all-to-all-start.5 = ((bf16[8,2,80,512]{3,2,1,0:T(8,128)(2,1)}), bf16[8,2,80,512]{3,2,1,0:T(8,128)(2,1)S(1)}, u32[]{:S(2)}, u32[]{:S(2)}) async-start(bf16[8,2,80,512]{3,2,1,0:T(8,128)(2,1)} %copy-done.2), calls=%async_computation.5 | async-start | bytes 2621440 | tf_op jit(solution)/shard_map/all_to_all | solution.py:331
  118.6 18.0 %collective-permute-start.10 = (bf16[8,80,512]{2,1,0:T(8,128)(2,1)}, bf16[8,80,512]{2,1,0:T(8,128)(2,1)S(1)}, u32[]{:S(2)}, u32[]{:S(2)}) collective-permute-start(bf16[8,80,512]{2,1,0:T(8,128)(2,1)} %copy-done.17), channel_id=1, source_target_pairs={{0,8},{4,12},{8,16},{12,20},{16,24},{20,28},{24,32},{28,36},{32,40... | collective-permute-start | bytes 1966088 | tf_op jit(solution)/shard_map/ppermute | solution.py:314
  119.3 17.4 %collective-permute-start.14 = (bf16[8,80,512]{2,1,0:T(8,128)(2,1)}, bf16[8,80,512]{2,1,0:T(8,128)(2,1)S(1)}, u32[]{:S(2)}, u32[]{:S(2)}) collective-permute-start(bf16[8,80,512]{2,1,0:T(8,128)(2,1)} %copy-done.16), channel_id=1, source_target_pairs={{0,56},{4,60},{8,0},{12,4},{16,8},{20,12},{24,16},{28,20},{32,24},... | collective-permute-start | bytes 1966088 | tf_op jit(solution)/shard_map/ppermute | solution.py:314
  136.6 9.6 %copy-start.7 = (bf16[8,80,512]{2,1,0:T(8,128)(2,1)}, bf16[8,80,512]{2,1,0:T(8,128)(2,1)S(1)}, u32[]{:S(2)}) copy-start(bf16[8,80,512]{2,1,0:T(8,128)(2,1)S(1)} %collective-permute-done.10.refs_0_) | copy-start | bytes 1966084
  136.6 9.6 %collective-permute-start.11 = (bf16[4,80,512]{2,1,0:T(8,128)(2,1)S(1)}, bf16[4,80,512]{2,1,0:T(8,128)(2,1)S(1)}, u32[]{:S(2)}, u32[]{:S(2)}) collective-permute-start(bf16[4,80,512]{2,1,0:T(8,128)(2,1)S(1)} %slice.34), channel_id=1, source_target_pairs={{0,8},{4,12},{8,16},{12,20},{16,24},{20,28},{24,32},{28,36},{32,40... | collective-permute-start | bytes 983048 | tf_op jit(solution)/shard_map/ppermute | solution.py:314
  136.7 9.5 %copy-start.9 = (bf16[8,80,512]{2,1,0:T(8,128)(2,1)}, bf16[8,80,512]{2,1,0:T(8,128)(2,1)S(1)}, u32[]{:S(2)}) copy-start(bf16[8,80,512]{2,1,0:T(8,128)(2,1)S(1)} %collective-permute-done.14.refs_1_) | copy-start | bytes 1966084
  136.8 9.5 %collective-permute-start.15 = (bf16[4,80,512]{2,1,0:T(8,128)(2,1)S(1)}, bf16[4,80,512]{2,1,0:T(8,128)(2,1)S(1)}, u32[]{:S(2)}, u32[]{:S(2)}) collective-permute-start(bf16[4,80,512]{2,1,0:T(8,128)(2,1)S(1)} %slice.35), channel_id=1, source_target_pairs={{0,56},{4,60},{8,0},{12,4},{16,8},{20,12},{24,16},{28,20},{32,24},... | collective-permute-start | bytes 983048 | tf_op jit(solution)/shard_map/ppermute | solution.py:314
  147.8 17.1 %all-to-all-start.2 = ((bf16[8,1,80,512]{3,2,1,0:T(8,128)(2,1)}), bf16[8,1,80,512]{3,2,1,0:T(8,128)(2,1)}, u32[]{:S(2)}, u32[]{:S(2)}) async-start(bf16[8,1,80,512]{3,2,1,0:T(8,128)(2,1)} %copy-done.6), calls=%async_computation.2 | async-start | bytes 1310720 | tf_op jit(solution)/shard_map/all_to_all | solution.py:331
  156.1 6.1 %copy-start.8 = (bf16[8,80,512]{2,1,0:T(8,128)(2,1)S(1)}, bf16[8,80,512]{2,1,0:T(8,128)(2,1)}, u32[]{:S(2)}) copy-start(bf16[8,80,512]{2,1,0:T(8,128)(2,1)} %copy-done.7) | copy-start | bytes 1966084
  156.2 6.1 %copy-start.10 = (bf16[8,80,512]{2,1,0:T(8,128)(2,1)S(1)}, bf16[8,80,512]{2,1,0:T(8,128)(2,1)}, u32[]{:S(2)}) copy-start(bf16[8,80,512]{2,1,0:T(8,128)(2,1)} %copy-done.9) | copy-start | bytes 1966084
  164.9 24.0 %all-to-all-start.3 = ((bf16[8,2,80,512]{3,2,1,0:T(8,128)(2,1)}), bf16[8,2,80,512]{3,2,1,0:T(8,128)(2,1)}, u32[]{:S(2)}, u32[]{:S(2)}) async-start(bf16[8,2,80,512]{3,2,1,0:T(8,128)(2,1)} %copy-done.3), calls=%async_computation.3 | async-start | bytes 2621440 | tf_op jit(solution)/shard_map/all_to_all | solution.py:331
  170.0 5.7 %copy-start.1 = (bf16[8,5,64,256]{3,2,1,0:T(8,128)(2,1)S(1)}, bf16[8,5,64,256]{3,2,1,0:T(8,128)(2,1)}, u32[]{:S(2)}) copy-start(bf16[8,5,64,256]{3,2,1,0:T(8,128)(2,1)} %copy-done) | copy-start | bytes 3932164
  171.3 18.6 %collective-permute-start.22 = (bf16[8,5,16,512]{3,2,1,0:T(8,128)(2,1)}, bf16[8,5,16,512]{3,2,1,0:T(8,128)(2,1)}, u32[]{:S(2)}, u32[]{:S(2)}) collective-permute-start(bf16[8,5,16,512]{3,2,1,0:T(8,128)(2,1)} %pad_maximum_fusion), channel_id=1, source_target_pairs={{0,1},{1,2},{2,3},{3,0},{4,5},{5,6},{6,7},{7,4},{8,9},{9,10},{10,1... | collective-permute-start | bytes 1966088 | tf_op jit(solution)/shard_map/ppermute | solution.py:339
  172.6 17.7 %collective-permute-start.23 = (bf16[8,5,16,512]{3,2,1,0:T(8,128)(2,1)}, bf16[8,5,16,512]{3,2,1,0:T(8,128)(2,1)}, u32[]{:S(2)}, u32[]{:S(2)}) collective-permute-start(bf16[8,5,16,512]{3,2,1,0:T(8,128)(2,1)} %pad_maximum_fusion), channel_id=1, source_target_pairs={{0,3},{1,0},{2,1},{3,2},{4,7},{5,4},{6,5},{7,6},{8,11},{9,8},{10,9... | collective-permute-start | bytes 1966088 | tf_op jit(solution)/shard_map/ppermute | solution.py:339
  174.0 30.3 %collective-permute-start.24 = (bf16[8,5,16,512]{3,2,1,0:T(8,128)(2,1)}, bf16[8,5,16,512]{3,2,1,0:T(8,128)(2,1)}, u32[]{:S(2)}, u32[]{:S(2)}) collective-permute-start(bf16[8,5,16,512]{3,2,1,0:T(8,128)(2,1)} %pad_maximum_fusion), channel_id=1, source_target_pairs={{0,2},{1,3},{2,0},{3,1},{4,6},{5,7},{6,4},{7,5},{8,10},{9,11},{10,... | collective-permute-start | bytes 1966088 | tf_op jit(solution)/shard_map/ppermute | solution.py:339
  175.7 3.1 %copy-start.11 = (bf16[14,4,256,256]{3,2,1,0:T(8,128)(2,1)S(1)}, bf16[14,4,256,256]{3,2,1,0:T(8,128)(2,1)}, u32[]{:S(2)}) copy-start(bf16[14,4,256,256]{3,2,1,0:T(8,128)(2,1)} %param.14) | copy-start | bytes 22020100
  178.8 2.6 %copy-start.5 = (bf16[8,3,64,256]{3,2,1,0:T(8,128)(2,1)S(1)}, bf16[8,3,64,256]{3,2,1,0:T(8,128)(2,1)}, u32[]{:S(2)}) copy-start(bf16[8,3,64,256]{3,2,1,0:T(8,128)(2,1)} %copy-done.4) | copy-start | bytes 2359300
  186.2 45.3 %collective-permute-start.16 = (bf16[8,1,16,512]{3,2,1,0:T(8,128)(2,1)}, bf16[8,1,16,512]{3,2,1,0:T(8,128)(2,1)S(1)}, u32[]{:S(2)}, u32[]{:S(2)}) collective-permute-start(bf16[8,1,16,512]{3,2,1,0:T(8,128)(2,1)} %slice.36), channel_id=1, source_target_pairs={{0,1},{1,2},{2,3},{3,0},{4,5},{5,6},{6,7},{7,4},{8,9},{9,10},{10,1... | collective-permute-start | bytes 393224 | tf_op jit(solution)/shard_map/ppermute | solution.py:339
  186.6 44.9 %collective-permute-start.17 = (bf16[8,1,16,512]{3,2,1,0:T(8,128)(2,1)}, bf16[8,1,16,512]{3,2,1,0:T(8,128)(2,1)S(1)}, u32[]{:S(2)}, u32[]{:S(2)}) collective-permute-start(bf16[8,1,16,512]{3,2,1,0:T(8,128)(2,1)} %slice.36), channel_id=1, source_target_pairs={{0,3},{1,0},{2,1},{3,2},{4,7},{5,4},{6,5},{7,6},{8,11},{9,8},{10,9... | collective-permute-start | bytes 393224 | tf_op jit(solution)/shard_map/ppermute | solution.py:339
  189.9 32.3 %collective-permute-start.19 = (bf16[8,2,16,512]{3,2,1,0:T(8,128)(2,1)S(1)}, bf16[8,2,16,512]{3,2,1,0:T(8,128)(2,1)S(1)}, u32[]{:S(2)}, u32[]{:S(2)}) collective-permute-start(bf16[8,2,16,512]{3,2,1,0:T(8,128)(2,1)S(1)} %slice.37), channel_id=1, source_target_pairs={{0,1},{1,2},{2,3},{3,0},{4,5},{5,6},{6,7},{7,4},{8,9},{9,10},{10,1... | collective-permute-start | bytes 786440 | tf_op jit(solution)/shard_map/ppermute | solution.py:339
  190.3 34.5 %collective-permute-start.20 = (bf16[8,2,16,512]{3,2,1,0:T(8,128)(2,1)S(1)}, bf16[8,2,16,512]{3,2,1,0:T(8,128)(2,1)S(1)}, u32[]{:S(2)}, u32[]{:S(2)}) collective-permute-start(bf16[8,2,16,512]{3,2,1,0:T(8,128)(2,1)S(1)} %slice.37), channel_id=1, source_target_pairs={{0,3},{1,0},{2,1},{3,2},{4,7},{5,4},{6,5},{7,6},{8,11},{9,8},{10,9... | collective-permute-start | bytes 786440 | tf_op jit(solution)/shard_map/ppermute | solution.py:339
  204.3 20.5 %collective-permute-start.21 = (bf16[8,2,16,512]{3,2,1,0:T(8,128)(2,1)S(1)}, bf16[8,2,16,512]{3,2,1,0:T(8,128)(2,1)S(1)}, u32[]{:S(2)}, u32[]{:S(2)}) collective-permute-start(bf16[8,2,16,512]{3,2,1,0:T(8,128)(2,1)S(1)} %slice.37), channel_id=1, source_target_pairs={{0,2},{1,3},{2,0},{3,1},{4,6},{5,7},{6,4},{7,5},{8,10},{9,11},{10,... | collective-permute-start | bytes 786440 | tf_op jit(solution)/shard_map/ppermute | solution.py:339
  207.5 17.4 %copy-start.29 = (bf16[8,512,128]{2,1,0:T(8,128)(2,1)S(1)}, bf16[8,512,128]{2,1,0:T(8,128)(2,1)}, u32[]{:S(2)}) copy-start(bf16[8,512,128]{2,1,0:T(8,128)(2,1)} %copy-done.27) | copy-start | bytes 3145732
  222.1 9.4 %collective-permute-start.18 = (bf16[8,1,16,512]{3,2,1,0:T(8,128)(2,1)}, bf16[8,1,16,512]{3,2,1,0:T(8,128)(2,1)S(1)}, u32[]{:S(2)}, u32[]{:S(2)}) collective-permute-start(bf16[8,1,16,512]{3,2,1,0:T(8,128)(2,1)} %slice.36), channel_id=1, source_target_pairs={{0,2},{1,3},{2,0},{3,1},{4,6},{5,7},{6,4},{7,5},{8,10},{9,11},{10,... | collective-permute-start | bytes 393224 | tf_op jit(solution)/shard_map/ppermute | solution.py:339
  231.5 4.0 %copy-start.13 = (bf16[8,512,256]{2,1,0:T(8,128)(2,1)S(1)}, bf16[8,512,256]{2,1,0:T(8,128)(2,1)}, u32[]{:S(2)}) copy-start(bf16[8,512,256]{2,1,0:T(8,128)(2,1)} %basis_ref.3) | copy-start | bytes 6291460
  231.5 4.0 %copy-start.15 = (bf16[4,512,256]{2,1,0:T(8,128)(2,1)S(1)}, bf16[4,512,256]{2,1,0:T(8,128)(2,1)}, u32[]{:S(2)}) copy-start(bf16[4,512,256]{2,1,0:T(8,128)(2,1)} %one_ref.3) | copy-start | bytes 3145732
  231.5 4.0 %copy-start.23 = (bf16[2,512,256]{2,1,0:T(8,128)(2,1)S(1)}, bf16[2,512,256]{2,1,0:T(8,128)(2,1)}, u32[]{:S(2)}) copy-start(bf16[2,512,256]{2,1,0:T(8,128)(2,1)} %two_ref.3) | copy-start | bytes 1572868
  231.5 4.0 %copy-start.26 = (f32[14,64,256]{2,1,0:T(8,128)S(1)}, f32[14,64,256]{2,1,0:T(8,128)}, u32[]{:S(2)}) copy-start(f32[14,64,256]{2,1,0:T(8,128)} %copy-done.25) | copy-start | bytes 2752516
  (18 other events, 23.2 us)

commit v2 on v1

v2 whole, which is shorter than its diff:
```python
import functools

import jax
import jax.numpy as jnp
from jax import lax
from jax.experimental import pallas as pl
from jax.experimental.pallas import tpu as pltpu
from jax.sharding import PartitionSpec as P


FEAT = 64
RANK = 256
R = 64
LEAF = 512
NB = 8
FAR = 4
NX, NZ, NC, NY = 4, 8, 2, 4
GROUP = NX * NC
LEAF_DEV = 8
NODE_DEV = 14
QUART = FEAT // NY
ROWS = R + QUART
AUG = 128
OFFSETS = (0, -1, 1, -2, 2, -3, 3, 4)
LEAF_CHUNKS = (((0, 3), (3, 5)), ((5, 7), (7, 8)))


F32 = jnp.float32
BF16 = jnp.bfloat16


def place(x, z, c):
    return (x * NZ + z % NZ) * NC + c


def ring(step):
    return [
        (place(x, z, c), place(x, z + step, c))
        for x in range(NX)
        for z in range(NZ)
        for c in range(NC)
    ]


def across(step):
    return [
        (place(x, z, c), place((x + step) % NX, z, c))
        for x in range(NX)
        for z in range(NZ)
        for c in range(NC)
    ]


FLIP = [(place(x, z, c), place(x, z, 1 - c)) for x in range(NX) for z in range(NZ) for c in range(NC)]
ROW_GROUPS = [[place(x, z, c) for x in range(NX) for c in range(NC)] for z in range(NZ)]


def cost(micros):
    return pl.CostEstimate(flops=int(micros * 1e9), bytes_accessed=0, transcendentals=0)


VMEM = pl.BlockSpec(memory_space=pltpu.VMEM)
SMEM = pl.BlockSpec(memory_space=pltpu.SMEM)


def call(kernel, micros, out, tables, arrays, scratch=(), megabytes=16):
    return pl.pallas_call(
        kernel,
        in_specs=[SMEM] * len(tables) + [VMEM] * len(arrays),
        out_specs=jax.tree.map(lambda _: VMEM, out),
        out_shape=out,
        scratch_shapes=list(scratch),
        compiler_params=pltpu.CompilerParams(vmem_limit_bytes=megabytes << 20),
        cost_estimate=cost(micros),
    )(*tables, *arrays)


def shaped(shape, kind):
    return jax.ShapeDtypeStruct(shape, kind)


def nt(a, b):
    return lax.dot_general(a, b, (((1,), (1,)), ((), ())), preferred_element_type=F32)


def pack_kernel(y_ref, rhs_ref, coords_ref, out_ref):
    start = pl.multiple_of(y_ref[0] * QUART, QUART)
    for leaf in range(LEAF_DEV):
        columns = slice(leaf * LEAF, (leaf + 1) * LEAF)
        out_ref[leaf, :R, :] = rhs_ref[:, columns]
        out_ref[leaf, R:, :] = coords_ref[pl.ds(start, QUART), columns]


def pack(y, rhs, coords):
    out = shaped((LEAF_DEV, ROWS, LEAF), BF16)
    return call(pack_kernel, 1, out, (y,), (rhs, coords), megabytes=8)


def square_rows(pieces, source):
    total = None
    for piece in pieces:
        wide = piece.astype(F32)
        part = jnp.sum(wide * wide, axis=0, keepdims=True)
        total = part if total is None else total + part
    total = total * -0.5
    high = total.astype(BF16).astype(F32)
    rest = total - high
    middle = rest.astype(BF16).astype(F32)
    low = rest - middle
    row = lax.broadcasted_iota(jnp.int32, (16, LEAF), 0)
    own = row if source else row - 3
    other = row - 3 if source else row
    block = jnp.where(own == 0, high, jnp.where(own == 1, middle, jnp.where(own == 2, low, 0.0)))
    block = jnp.where(jnp.logical_and(other >= 0, other < 3), 1.0, block)
    return block.astype(BF16)


def tile_product(target, spread, charges):
    exponent = jnp.dot(target, spread, preferred_element_type=F32)
    return nt(jnp.exp(exponent).astype(BF16), charges)


def own_kernel(pos_ref, rhs_ref, coords_ref, other_ref, target_ref, near_ref, spread_ref):
    y = pos_ref[0]
    empty = jnp.zeros((AUG - FEAT - 16, LEAF), BF16)
    for core, ref in enumerate((coords_ref, other_ref)):
        for leaf in range(LEAF_DEV):
            columns = slice(leaf * LEAF, (leaf + 1) * LEAF)
            pieces = []
            for shift_by in (0, NY - 1, 1, 2):
                start = pl.multiple_of(lax.rem(y + shift_by, NY) * QUART, QUART)
                pieces.append(ref[pl.ds(start, QUART), columns])
            wide = jnp.concatenate(pieces + [square_rows(pieces, False), empty], axis=0)
            target_ref[core * LEAF_DEV + leaf] = wide.astype(F32).T.astype(BF16)
            if core == 0:
                spread_ref[leaf, :FEAT, :] = jnp.concatenate(pieces, axis=0)
                spread_ref[leaf, FEAT : FEAT + 16, :] = square_rows(pieces, True)
                spread_ref[leaf, FEAT + 16 :, :] = empty

    def pair(i, carry):
        for leaf in (2 * i, 2 * i + 1):
            charges = rhs_ref[:, pl.ds(pl.multiple_of(leaf * LEAF, LEAF), LEAF)]
            product = tile_product(target_ref[leaf], spread_ref[leaf], charges)
            near_ref[:, pl.ds(pl.multiple_of(leaf * LEAF, LEAF), LEAF)] = product.T
        return carry

    lax.fori_loop(0, LEAF_DEV // 2, pair, 0)


def own_tiles(pos, rhs, coords, other):
    out = [shaped((2 * LEAF_DEV, LEAF, AUG), BF16), shaped((R, LEAF_DEV * LEAF), F32)]
    scratch = [pltpu.VMEM((LEAF_DEV, AUG, LEAF), BF16)]
    return call(own_kernel, 5, out, (pos,), (rhs, coords, other), scratch, 20)


UNROLL = 4


def near_kernel(chunks, take_ref, *refs):
    given = NX * len(chunks)
    got_refs, piece_refs = refs[:given], refs[given : given + NY]
    target_ref, *before_refs = refs[given + NY : -5]
    own_ref, other_ref, spread_ref, held_ref, near_ref = refs[-5:]
    near_ref[...] = jnp.zeros_like(near_ref)
    spread_ref[:, FEAT + 16 :, :] = jnp.zeros((UNROLL, AUG - FEAT - 16, LEAF), BF16)
    start, slots = chunks[0][0], chunks[-1][1] - chunks[0][0]
    for index, (low, high) in enumerate(chunks):
        for step in range(NX):
            for side in range(NC):
                block = got_refs[NX * index + step][side, :, :R, :]
                held_ref[NC * step + side, low - start : high - start] = block

    def some(i, carry):
        for buffer in range(UNROLL):
            item = i * UNROLL + buffer
            source, slot = item // slots, item % slots
            which = take_ref[source, start + slot]
            pieces = [ref[source, slot] for ref in piece_refs]
            for q, piece in enumerate(pieces):
                spread_ref[buffer, q * QUART : (q + 1) * QUART, :] = piece
            spread_ref[buffer, FEAT : FEAT + 16, :] = square_rows(pieces, True)
            charges = held_ref[source, slot]
            charges = jnp.where(which >= 0, charges, jnp.zeros_like(charges))
            leaf = jnp.maximum(which, 0)
            near_ref[leaf] += tile_product(target_ref[leaf], spread_ref[buffer], charges)
        return carry

    lax.fori_loop(0, GROUP * slots // UNROLL, some, 0)
    for core, out_ref in enumerate((own_ref, other_ref)):
        for leaf in range(LEAF_DEV):
            columns = slice(leaf * LEAF, (leaf + 1) * LEAF)
            near = near_ref[core * LEAF_DEV + leaf].T
            out_ref[:, columns] = near + before_refs[core][:, columns] if before_refs else near


def near_chunk(chunks, take, got, pieces, targets, before):
    slots = chunks[-1][1] - chunks[0][0]
    flat = shaped((R, LEAF_DEV * LEAF), F32)
    return call(
        functools.partial(near_kernel, chunks),
        3.2 * slots,
        [flat, flat],
        (take,),
        (*got, *pieces, targets, *before),
        [
            pltpu.VMEM((UNROLL, AUG, LEAF), BF16),
            pltpu.VMEM((GROUP, slots, R, LEAF), BF16),
            pltpu.VMEM((2 * LEAF_DEV, LEAF, R), F32),
        ],
        40,
    )


def quarter_kernel(*refs):
    out_ref = refs[-1]
    at = 0
    for first in range(0, len(refs) - 1, NX):
        count = refs[first].shape[1]
        for step in range(NX):
            for side in range(NC):
                out_ref[NC * step + side, at : at + count] = refs[first + step][side, :, R:, :]
        at += count


def quarters(got):
    slots = sum(part.shape[1] for part in got[::NX])
    out = shaped((GROUP, slots, QUART, LEAF), BF16)
    return call(quarter_kernel, 1, out, (), got, megabytes=16)


def choose_kernel(first, send_ref, *refs):
    out_ref = refs[-1]
    for slot, ref in enumerate(refs[:-1]):
        for target in range(GROUP):
            out_ref[target, slot] = ref[send_ref[target, first + slot]]


def choose_steps_kernel(first, send_ref, *refs):
    sources, outs = refs[:-NX], refs[-NX:]
    for slot, ref in enumerate(sources):
        for step in range(NX):
            for side in range(NC):
                outs[step][side, slot] = ref[send_ref[NC * step + side, first + slot]]


def choose(first, send, sources, kind):
    shape = sources[0].shape[1:]
    count = len(sources)
    if kind == "leaf":
        kernel, out = choose_steps_kernel, [shaped((NC, count, *shape), BF16)] * NX
    else:
        kernel, out = choose_kernel, shaped((GROUP, count, *shape), BF16)
    kernel = functools.partial(kernel, first)
    return call(kernel, 1, out, (send,), sources)


def skeleton_kernel(leaves_ref, basis_ref, one_ref, two_ref, out_ref):
    def rounded_dot(a, b):
        return jnp.dot(a, b, preferred_element_type=F32).astype(BF16)

    for leaf in range(LEAF_DEV):
        out_ref[leaf] = rounded_dot(leaves_ref[leaf, :R, :], basis_ref[leaf])
    for m in range(LEAF_DEV // 2):
        joined = jnp.concatenate([out_ref[2 * m], out_ref[2 * m + 1]], axis=1)
        out_ref[LEAF_DEV + m] = rounded_dot(joined, one_ref[m])
    for m in range(LEAF_DEV // 4):
        low = LEAF_DEV + 2 * m
        joined = jnp.concatenate([out_ref[low], out_ref[low + 1]], axis=1)
        out_ref[LEAF_DEV * 3 // 2 + m] = rounded_dot(joined, two_ref[m])


def skeletons(leaves, basis, one, two):
    out = shaped((NODE_DEV, R, RANK), BF16)
    return call(skeleton_kernel, 3, out, (), (leaves, basis, one, two))


def far_kernel(take_ref, got_ref, blocks_ref, out_ref, held_ref, sems):
    out_ref[...] = jnp.zeros_like(out_ref)

    def fetch(i):
        at = jnp.maximum(take_ref[i // NZ, i % NZ], 0)
        return pltpu.make_async_copy(blocks_ref.at[at], held_ref.at[i], sems.at[i])

    def begin(i, carry):
        fetch(i).start()
        return carry

    lax.fori_loop(0, GROUP * NZ, begin, 0)

    def source_of(source, carry):
        for slot in range(NZ):
            item = source * NZ + slot
            which = take_ref[source, slot]
            weights = got_ref[source, slot]
            weights = jnp.where(which >= 0, weights, jnp.zeros_like(weights))
            fetch(item).wait()
            out_ref[jnp.maximum(which, 0) // FAR] += jnp.dot(
                weights, held_ref[item], preferred_element_type=F32
            )
        return carry

    lax.fori_loop(0, GROUP, source_of, 0)


def far_part(take, got, blocks):
    return pl.pallas_call(
        far_kernel,
        in_specs=[SMEM, VMEM, pl.BlockSpec(memory_space=pltpu.HBM)],
        out_specs=VMEM,
        out_shape=shaped((NODE_DEV, R, RANK), F32),
        scratch_shapes=[
            pltpu.VMEM((GROUP * NZ, RANK, RANK), BF16),
            pltpu.SemaphoreType.DMA((GROUP * NZ,)),
        ],
        compiler_params=pltpu.CompilerParams(vmem_limit_bytes=20 << 20),
        cost_estimate=cost(5),
        name="far_part",
    )(take, got, blocks)


def finish_kernel(far_ref, one_ref, two_ref, basis_ref, self_ref, own_ref, other_ref, out_ref):
    for m in range(LEAF_DEV // 4):
        spread = nt(far_ref[LEAF_DEV * 3 // 2 + m].astype(BF16), two_ref[m])
        for side in range(2):
            node = 2 * m + side
            middle = far_ref[LEAF_DEV + node] + spread[:, side * RANK : (side + 1) * RANK]
            lower = nt(middle.astype(BF16), one_ref[node])
            for part in range(2):
                leaf = 2 * node + part
                lowest = far_ref[leaf] + lower[:, part * RANK : (part + 1) * RANK]
                columns = slice(leaf * LEAF, (leaf + 1) * LEAF)
                near = self_ref[:, columns] + own_ref[:, columns] + other_ref[:, columns]
                out_ref[:, columns] = near + nt(lowest.astype(BF16), basis_ref[leaf])


def finish(far, one, two, basis, *near):
    out = shaped((R, LEAF_DEV * LEAF), F32)
    return call(finish_kernel, 4, out, (), (far, one, two, basis, *near), megabytes=20)


def tables(neighbours, far_lists, x, z, c, group):
    offsets = jnp.asarray(OFFSETS, jnp.int32)
    there = (z + offsets + NZ) % NZ
    row_near = lax.dynamic_index_in_dim(
        neighbours.reshape(NX, NZ, NC, LEAF_DEV * NB), z, 1, keepdims=False
    ).reshape(GROUP, LEAF_DEV * NB)
    row_far = lax.dynamic_index_in_dim(
        far_lists.reshape(NX, NZ, NC, NODE_DEV * FAR), z, 1, keepdims=False
    ).reshape(GROUP, NODE_DEV * FAR)
    remote = jnp.arange(LEAF_DEV * NB, dtype=jnp.int32) % NB > 0
    near_owner = jnp.where(remote, row_near // LEAF_DEV, -1)
    far_owner = row_far // NODE_DEV
    mine = (x * NZ + there) * NC + c

    def pick(owner, value, sources):
        hit = owner[:, None, :] == sources[:, :, None]
        return jnp.sum(jnp.where(hit, value[:, None, :], 0), axis=2, dtype=jnp.int32)

    member = jnp.arange(GROUP, dtype=jnp.int32)
    sent_from = jnp.broadcast_to(mine[None, :], (GROUP, NZ))
    step, side = member // NC, member % NC
    core = jnp.where(side == 0, c, 1 - c)
    to_row = (x + step) % NX * NC + core
    send_leaf = pick(near_owner[to_row], row_near[to_row] % LEAF_DEV, sent_from)
    send_node = pick(far_owner, row_far % NODE_DEV, sent_from)
    came_from = (((x - step + NX) % NX)[:, None] * NZ + there[None, :]) * NC + c
    near_value = jnp.arange(LEAF_DEV * NB, dtype=jnp.int32)[None, :] // NB + 1
    near_value = near_value + side[:, None] * LEAF_DEV
    take_leaf = pick(near_owner[x * NC + core], near_value, came_from) - 1
    seen = ((member // NC)[:, None] * NZ + there[None, :]) * NC + (member % NC)[:, None]
    own_far = lax.dynamic_index_in_dim(far_owner, group, 0, keepdims=True)
    far_value = jnp.arange(NODE_DEV * FAR, dtype=jnp.int32)[None, :] + 1
    take_node = pick(own_far, far_value, seen) - 1
    return send_leaf, send_node, take_leaf, take_node


def shift(value, step):
    return lax.ppermute(value, "leaf", ring(step))


def travel(payload, last):
    arrived = [payload]
    up, down = payload, payload
    for _ in range(1, NZ // 2):
        up = shift(up, 1)
        down = shift(down, -1)
        arrived += [up, down]
    arrived.append(shift(up if last == 1 else down, last))
    return arrived


def cross(chosen):
    got = [chosen[0]]
    for step in range(1, NX):
        got.append(lax.ppermute(chosen[step], "leaf", across(step)))
    return got


def flip(value):
    return lax.ppermute(value, "leaf", FLIP)


def exchange(chosen):
    return lax.all_to_all(
        chosen, "leaf", split_axis=0, concat_axis=0, axis_index_groups=ROW_GROUPS, tiled=True
    )


def join_planes(quarter):
    joined = []
    for step in (1, NY - 1, 2):
        joined.append(lax.ppermute(quarter, "rhs", [(i, (i + step) % NY) for i in range(NY)]))
    return joined


def on_device(coords, rhs, basis, transfer_one, transfer_two, far_blocks, neighbours, far_lists):
    me = lax.axis_index("leaf").astype(jnp.int32)
    y = lax.axis_index("rhs").astype(jnp.int32).reshape(1)
    c, z, x = me % NC, (me // NC) % NZ, me // (NC * NZ)
    group = x * NC + c
    payload = pack(y, rhs, coords)
    other_coords = flip(coords)
    leaves = travel(payload, 1)
    nodes = travel(skeletons(payload, basis, transfer_one, transfer_two), -1)
    send_leaf, send_node, take_leaf, take_node = tables(neighbours, far_lists, x, z, c, group)
    targets, self_part = own_tiles(y, rhs, coords, other_coords)
    near = ()
    for chunks in LEAF_CHUNKS:
        got = []
        for low, high in chunks:
            got += cross(choose(low, send_leaf, leaves[low:high], "leaf"))
        quarter = quarters(got)
        pieces = [quarter] + join_planes(quarter)
        near = near_chunk(chunks, take_leaf, got, pieces, targets, near)
    own, other = near
    other = flip(other)
    got = exchange(choose(0, send_node, nodes, "node"))
    far = far_part(take_node, got, far_blocks.reshape(NODE_DEV * FAR, RANK, RANK))
    return finish(far, transfer_one, transfer_two, basis, self_part, own, other)


def solution(mesh):
    return jax.shard_map(
        on_device,
        mesh=mesh,
        in_specs=(
            P(None, "leaf"),
            P("rhs", "leaf"),
            P("leaf", None, None),
            P("leaf", None, None),
            P("leaf", None, None),
            P("leaf", None, None, None),
            P(),
            P(),
        ),
        out_specs=P("rhs", "leaf"),
        check_vma=False,
    )
```

time: 241 us -> 214 us (0.89)
  waiting for transfers between devices: 93.3 us -> 56.2 us
  Pallas kernels: 45.7 us -> 74.2 us
  starting transfers between devices: 72.1 us -> 55.3 us
    all_to_all x6 -> x1, starting transfers between devices: 34.1 us -> 8.92 us  [exchange(): lax.all_to_all(chosen, 'leaf', split_axis=0, concat_axis=0, axis_index_gr...]
    pallas_call x0 -> x1, Pallas kernels: none -> 23.7 us  [far_part(): pl.pallas_call(far_kernel, in_specs=[SMEM, VMEM, pl.BlockSpec(memory_spac...]
    ppermute x16 -> x14, waiting for transfers between devices: 74.3 us -> 53.4 us  [shift(): return lax.ppermute(value, 'leaf', ring(step))]
    ppermute x0 -> x14, starting transfers between devices: none -> 20.4 us  [the longest x12 18.5 us: cross(): got.append(lax.ppermute(chosen[step], 'leaf', across(step)))]
    ppermute x9 -> x6, waiting for transfers between devices: 11.7 us -> 0.02 us  [join_planes(): lax.ppermute(quarter, 'rhs', [(i, (i + step) % NY) for i in range(NY)])]
    ppermute x16 -> x14, starting transfers between devices: 25.1 us -> 16.1 us  [shift(): return lax.ppermute(value, 'leaf', ring(step))]
    all_to_all x6 -> x1, waiting for transfers between devices: 7.29 us -> 0.01 us  [exchange(): lax.all_to_all(chosen, 'leaf', split_axis=0, concat_axis=0, axis_index_gr...]
    pallas_call x15 -> x13, Pallas kernels: 45.7 us -> 50.5 us  [call(): pl.pallas_call(kernel, in_specs=[SMEM] * len(tables) + [VMEM] * len(array...]
  transfers between devices with their start and end apart: 31 -> 35, of which waited for: 14 -> 8; matrix products, arithmetic and copies ran while one was open for 3% -> 3% of each run, Pallas kernels for 15% -> 33%
where the time goes in v2:
time: 214 us; the launch traced here: 213 us
  Pallas kernels  74.2 us (35%)
  waiting for transfers between devices  56.2 us (26%)
  starting transfers between devices  55.3 us (26%)
  local copies, waits for them, and re-layouts  25 us (12%)
    ppermute x14, waiting for transfers between devices, shift(): return lax.ppermute(value, 'leaf', ring(step))  53.4 us
    pallas_call x13, Pallas kernels, call(): pl.pallas_call(kernel, in_specs=[SMEM] * len(tables) + [VMEM] * len(array...  50.5 us
    pallas_call x1, Pallas kernels, far_part(): pl.pallas_call(far_kernel, in_specs=[SMEM, VMEM, pl.BlockSpec(memory_spac...  23.7 us
    unnamed x114, local copies, waits for them, and re-layouts  22 us
    ppermute x12, starting transfers between devices, cross(): got.append(lax.ppermute(chosen[step], 'leaf', across(step)))  18.5 us
    ppermute x14, starting transfers between devices, shift(): return lax.ppermute(value, 'leaf', ring(step))  16.1 us
    ppermute x6, starting transfers between devices, join_planes(): lax.ppermute(quarter, 'rhs', [(i, (i + step) % NY) for i in range(NY)])  9.88 us
    all_to_all x1, starting transfers between devices, exchange(): lax.all_to_all(chosen, 'leaf', split_axis=0, concat_axis=0, axis_index_gr...  8.92 us
  transfers between devices with their start and end apart: 35, of which 8 were waited for; matrix products, arithmetic and copies ran while one was open for 3% of the time, Pallas kernels for 33%

profile of v2, /device:TPU:1, one launch (start us, length us, event | category | flops | bytes accessed | tf_op | source)
XLA Modules:
  0.0 212.8 jit_solution(15967511326105458910)
XLA Ops:
  0.0 1.2 copy-done.27
  1.2 1.1 shard_map.91.leaves_ref.refs_0_
  2.4 6.5 %collective-permute-start.11 = (bf16[8,80,512]{2,1,0:T(8,128)(2,1)S(1)}, bf16[8,80,512]{2,1,0:T(8,128)(2,1)}, u32[]{:S(2)}, u32[]{:S(2)}) collective-permute-start(bf16[8,80,512]{2,1,0:T(8,128)(2,1)S(1)} %shard_map.91.leaves_ref.refs_0_), channel_id=1, source_target_pairs={{0,56},{4,60},{8,0},{12,4},{16,8},{20,12},{24,16},{28,20},{32,24},... | collective-permute-start | bytes 1966088 | tf_op jit(solution)/shard_map/ppermute | solution.py:378
  10.6 3.0 %collective-permute-start.1 = (bf16[14,64,256]{2,1,0:T(8,128)(2,1)S(1)}, bf16[14,64,256]{2,1,0:T(8,128)(2,1)S(1)}, u32[]{:S(2)}, u32[]{:S(2)}) collective-permute-start(bf16[14,64,256]{2,1,0:T(8,128)(2,1)S(1)} %shard_map.92.refs_0_), channel_id=1, source_target_pairs={{0,56},{4,60},{8,0},{12,4},{16,8},{20,12},{24,16},{28,20},{32,24},... | collective-permute-start | bytes 1376264 | tf_op jit(solution)/shard_map/ppermute | solution.py:378
  14.6 10.9 %collective-permute-done.8.refs_1_ = bf16[8,80,512]{2,1,0:T(8,128)(2,1)} collective-permute-done((bf16[8,80,512]{2,1,0:T(8,128)(2,1)S(1)}, bf16[8,80,512]{2,1,0:T(8,128)(2,1)}, u32[]{:S(2)}, u32[]{:S(2)}) %collective-permute-start.8) | collective-permute-done | bytes 655392 | tf_op jit(solution)/shard_map/ppermute | solution.py:378
  26.4 5.7 %collective-permute-done.1.refs_2_ = bf16[14,64,256]{2,1,0:T(8,128)(2,1)S(1)} collective-permute-done((bf16[14,64,256]{2,1,0:T(8,128)(2,1)S(1)}, bf16[14,64,256]{2,1,0:T(8,128)(2,1)S(1)}, u32[]{:S(2)}, u32[]{:S(2)}) %collective-permute-start.1) | collective-permute-done | bytes 458784 | tf_op jit(solution)/shard_map/ppermute | solution.py:378
  32.1 3.4 %collective-permute-start.3 = (bf16[14,64,256]{2,1,0:T(8,128)(2,1)S(1)}, bf16[14,64,256]{2,1,0:T(8,128)(2,1)}, u32[]{:S(2)}, u32[]{:S(2)}) collective-permute-start(bf16[14,64,256]{2,1,0:T(8,128)(2,1)S(1)} %collective-permute-done.1.refs_2_), channel_id=1, source_target_pairs={{0,56},{4,60},{8,0},{12,4},{16,8},{20,12},{24,16},{28,20},{32,24},... | collective-permute-start | bytes 1376264 | tf_op jit(solution)/shard_map/ppermute | solution.py:378
  35.5 1.2 copy-done.26
  36.8 2.4 %shard_map.98 = (bf16[2,3,80,512]{3,2,1,0:T(8,128)(2,1)S(1)}, bf16[2,3,80,512]{3,2,1,0:T(8,128)(2,1)S(1)}, bf16[2,3,80,512]{3,2,1,0:T(8,128)(2,1)}, bf16[2,3,80,512]{3,2,1,0:T(8,128)(2,1)}) custom-call(s32[8,8]{1,0:T(8,128)S(1)} %select_reduce_fusion.send_ref, bf16[8,80,512]{2,1,0:T(8,128)(2,1)S(1)} %copy-done.26, ...), custom_call_target="tpu_custom_call" | custom-call | flops 1000000000 | tf_op jit(solution)/shard_map/pallas_call | solution.py:67
  39.2 1.2 collective-permute-start.24
  40.4 2.6 %collective-permute-start.12 = (bf16[8,80,512]{2,1,0:T(8,128)(2,1)}, bf16[8,80,512]{2,1,0:T(8,128)(2,1)}, u32[]{:S(2)}, u32[]{:S(2)}) collective-permute-start(bf16[8,80,512]{2,1,0:T(8,128)(2,1)} %collective-permute-done.11.refs_2_), channel_id=1, source_target_pairs={{0,56},{4,60},{8,0},{12,4},{16,8},{20,12},{24,16},{28,20},{32,24},... | collective-permute-start | bytes 1966088 | tf_op jit(solution)/shard_map/ppermute | solution.py:378
  43.0 6.4 %collective-permute-done.9.refs_0_ = bf16[8,80,512]{2,1,0:T(8,128)(2,1)} collective-permute-done((bf16[8,80,512]{2,1,0:T(8,128)(2,1)}, bf16[8,80,512]{2,1,0:T(8,128)(2,1)}, u32[]{:S(2)}, u32[]{:S(2)}) %collective-permute-start.9) | collective-permute-done | bytes 655392 | tf_op jit(solution)/shard_map/ppermute | solution.py:378
  49.5 2.8 %collective-permute-start.25 = (bf16[2,3,80,512]{3,2,1,0:T(8,128)(2,1)}, bf16[2,3,80,512]{3,2,1,0:T(8,128)(2,1)S(1)}, u32[]{:S(2)}, u32[]{:S(2)}) collective-permute-start(bf16[2,3,80,512]{3,2,1,0:T(8,128)(2,1)} %get-tuple-element.39), channel_id=1, source_target_pairs={{0,128},{4,132},{8,136},{12,140},{16,144},{20,148},{24,152},{28,15... | collective-permute-start | bytes 1474568 | tf_op jit(solution)/shard_map/ppermute | solution.py:395
  52.2 7.0 %collective-permute-done.2.refs_3_ = bf16[14,64,256]{2,1,0:T(8,128)(2,1)} collective-permute-done((bf16[14,64,256]{2,1,0:T(8,128)(2,1)S(1)}, bf16[14,64,256]{2,1,0:T(8,128)(2,1)}, u32[]{:S(2)}, u32[]{:S(2)}) %collective-permute-start.2) | collective-permute-done | bytes 458784 | tf_op jit(solution)/shard_map/ppermute | solution.py:378
  59.2 2.5 %collective-permute-start.26 = (bf16[2,3,80,512]{3,2,1,0:T(8,128)(2,1)}, bf16[2,3,80,512]{3,2,1,0:T(8,128)(2,1)S(1)}, u32[]{:S(2)}, u32[]{:S(2)}) collective-permute-start(bf16[2,3,80,512]{3,2,1,0:T(8,128)(2,1)} %get-tuple-element.40), channel_id=1, source_target_pairs={{0,192},{4,196},{8,200},{12,204},{16,208},{20,212},{24,216},{28,22... | collective-permute-start | bytes 1474568 | tf_op jit(solution)/shard_map/ppermute | solution.py:395
  61.8 1.0 copy.12
  62.8 1.2 reshape.348
  64.5 8.7 %collective-permute-done.10.refs_0_ = bf16[8,80,512]{2,1,0:T(8,128)(2,1)} collective-permute-done((bf16[8,80,512]{2,1,0:T(8,128)(2,1)}, bf16[8,80,512]{2,1,0:T(8,128)(2,1)}, u32[]{:S(2)}, u32[]{:S(2)}) %collective-permute-start.10) | collective-permute-done | bytes 655392 | tf_op jit(solution)/shard_map/ppermute | solution.py:378
  74.2 2.3 %shard_map.99 = (bf16[2,2,80,512]{3,2,1,0:T(8,128)(2,1)S(1)}, bf16[2,2,80,512]{3,2,1,0:T(8,128)(2,1)}, bf16[2,2,80,512]{3,2,1,0:T(8,128)(2,1)}, bf16[2,2,80,512]{3,2,1,0:T(8,128)(2,1)S(1)}) custom-call(s32[8,8]{1,0:T(8,128)S(1)} %select_reduce_fusion.send_ref, bf16[8,80,512]{2,1,0:T(8,128)(2,1)} %collective-permute-done.9.refs_0_, ...), custom_call_target="tpu_custom_call" | custom-call | flops 1000000000 | tf_op jit(solution)/shard_map/pallas_call | solution.py:67
  78.0 1.2 collective-permute-start.27
  79.2 2.5 %collective-permute-start.28 = (bf16[2,2,80,512]{3,2,1,0:T(8,128)(2,1)}, bf16[2,2,80,512]{3,2,1,0:T(8,128)(2,1)}, u32[]{:S(2)}, u32[]{:S(2)}) collective-permute-start(bf16[2,2,80,512]{3,2,1,0:T(8,128)(2,1)} %get-tuple-element.43), channel_id=1, source_target_pairs={{0,128},{4,132},{8,136},{12,140},{16,144},{20,148},{24,152},{28,15... | collective-permute-start | bytes 983048 | tf_op jit(solution)/shard_map/ppermute | solution.py:395
  81.7 3.0 %collective-permute-done.13.refs_1_ = bf16[8,80,512]{2,1,0:T(8,128)(2,1)} collective-permute-done((bf16[8,80,512]{2,1,0:T(8,128)(2,1)}, bf16[8,80,512]{2,1,0:T(8,128)(2,1)}, u32[]{:S(2)}, u32[]{:S(2)}) %collective-permute-start.13) | collective-permute-done | bytes 655392 | tf_op jit(solution)/shard_map/ppermute | solution.py:378
  85.2 1.4 shard_map.95
  87.3 11.7 %collective-permute-done.4.refs_5_ = bf16[14,64,256]{2,1,0:T(8,128)(2,1)S(1)} collective-permute-done((bf16[14,64,256]{2,1,0:T(8,128)(2,1)}, bf16[14,64,256]{2,1,0:T(8,128)(2,1)S(1)}, u32[]{:S(2)}, u32[]{:S(2)}) %collective-permute-start.4) | collective-permute-done | bytes 458784 | tf_op jit(solution)/shard_map/ppermute | solution.py:378
  99.0 1.3 collective-permute-start.14
  100.3 2.5 %collective-permute-start.15 = (bf16[2,2,80,512]{3,2,1,0:T(8,128)(2,1)S(1)}, bf16[2,2,80,512]{3,2,1,0:T(8,128)(2,1)S(1)}, u32[]{:S(2)}, u32[]{:S(2)}) collective-permute-start(bf16[2,2,80,512]{3,2,1,0:T(8,128)(2,1)S(1)} %get-tuple-element.30), channel_id=1, source_target_pairs={{0,128},{4,132},{8,136},{12,140},{16,144},{20,148},{24,152},{28,15... | collective-permute-start | bytes 983048 | tf_op jit(solution)/shard_map/ppermute | solution.py:395
  102.8 1.2 collective-permute-start.16
  103.9 1.9 shard_map.96
  107.6 1.0 shard_map.100.refs_8_
  108.6 1.3 collective-permute-start.30
  110.7 1.5 collective-permute-start.31
  112.2 2.7 %collective-permute-done.15.refs_2_ = bf16[2,2,80,512]{3,2,1,0:T(8,128)(2,1)S(1)} collective-permute-done((bf16[2,2,80,512]{3,2,1,0:T(8,128)(2,1)S(1)}, bf16[2,2,80,512]{3,2,1,0:T(8,128)(2,1)S(1)}, u32[]{:S(2)}, u32[]{:S(2)}) %collective-permute-start.15) | collective-permute-done | bytes 327712 | tf_op jit(solution)/shard_map/ppermute | solution.py:395
  115.7 2.9 %collective-permute-start.32 = (bf16[8,5,16,512]{3,2,1,0:T(8,128)(2,1)S(1)}, bf16[8,5,16,512]{3,2,1,0:T(8,128)(2,1)}, u32[]{:S(2)}, u32[]{:S(2)}) collective-permute-start(bf16[8,5,16,512]{3,2,1,0:T(8,128)(2,1)S(1)} %shard_map.100.refs_8_), channel_id=1, source_target_pairs={{0,2},{1,3},{2,0},{3,1},{4,6},{5,7},{6,4},{7,5},{8,10},{9,11},{10,... | collective-permute-start | bytes 1966088 | tf_op jit(solution)/shard_map/ppermute | solution.py:412
  119.9 2.0 collective-permute-start.20
  121.9 5.6 %shard_map.94 = (bf16[16,512,128]{2,1,0:T(8,128)(2,1)S(1)}, f32[64,4096]{1,0:T(8,128)S(1)}) custom-call(s32[1]{0:T(128)} %bitcast.3.y_ref.pos_ref, bf16[64,4096]{1,0:T(8,128)(2,1)S(1)} %copy-done.28, bf16[64,4096]{1,0:T(8,128)(2,1)} %coords_ref.3, bf16[64,4096]{1,0:T(8,128)(2,1)} %collective-permute-done.7.other_ref), custom_call_target="tpu_custom_call" | custom-call | flops 5000000000 | tf_op jit(solution)/shard_map/pallas_call | solution.py:67
  128.5 1.4 copy-done.51
  129.8 2.7 %shard_map.93 = bf16[8,8,64,256]{3,2,1,0:T(8,128)(2,1)} custom-call(s32[8,8]{1,0:T(8,128)S(1)} %select_reduce_fusion.2.send_ref, bf16[14,64,256]{2,1,0:T(8,128)(2,1)S(1)} %shard_map.92.refs_0_, bf16[14,64,256]{2,1,0:T(8,128)(2,1)S(1)} %copy-done.9, bf16[14,64,256]{2,1,0:T(8,128)(2,1)S(1)} %copy-done.7, bf16[14,64,256]{2,1,0:T(8,128)(2,1)} %collective-permute-done.2.refs_3_, ...), custom_call_target="tpu_custom_call" | custom-call | flops 1000000000 | tf_op jit(solution)/shard_map/pallas_call | solution.py:67
  132.6 8.9 %all-to-all-start = ((bf16[8,8,64,256]{3,2,1,0:T(8,128)(2,1)}), bf16[8,8,64,256]{3,2,1,0:T(8,128)(2,1)S(1)}, u32[]{:S(2)}, u32[]{:S(2)}) async-start(bf16[8,8,64,256]{3,2,1,0:T(8,128)(2,1)} %shard_map.93), calls=%async_computation | async-start | bytes 4194304 | tf_op jit(solution)/shard_map/all_to_all | solution.py:404
  141.6 1.1 copy-done.32
  146.5 1.0 shard_map.97.refs_8_
  148.3 2.0 collective-permute-start.22
  150.3 1.4 collective-permute-start.23
  151.8 1.6 copy-done.52
  153.4 16.2 %shard_map.101 = (f32[64,4096]{1,0:T(8,128)S(1)}, f32[64,4096]{1,0:T(8,128)S(1)}) custom-call(s32[8,8]{1,0:T(8,128)S(1)} %broadcast_add_fusion.1.take_ref, bf16[2,3,80,512]{3,2,1,0:T(8,128)(2,1)S(1)} %get-tuple-element.37.refs_0_, bf16[2,3,80,512]{3,2,1,0:T(8,128)(2,1)S(1)} %copy-done.1, bf16[2,3,80,512]{3,2,1,0:T(8,128)(2,1)S(1)} %copy-done.3, ...), custom_call_target="tpu_custom_call" | custom-call | flops 16000000000 | tf_op jit(solution)/shard_map/pallas_call | solution.py:67
  169.7 10.3 %shard_map.102 = (f32[64,4096]{1,0:T(8,128)S(1)}, f32[64,4096]{1,0:T(8,128)S(1)}) custom-call(s32[8,8]{1,0:T(8,128)S(1)} %broadcast_add_fusion.1.take_ref, bf16[2,2,80,512]{3,2,1,0:T(8,128)(2,1)S(1)} %copy-done.43, bf16[2,2,80,512]{3,2,1,0:T(8,128)(2,1)S(1)} %copy-done.33, bf16[2,2,80,512]{3,2,1,0:T(8,128)(2,1)S(1)} %copy-done.36, ...), custom_call_target="tpu_custom_call" | custom-call | flops 9600000000 | tf_op jit(solution)/shard_map/pallas_call | solution.py:67
  182.2 3.1 %copy-done.20 = bf16[14,4,256,256]{3,2,1,0:T(8,128)(2,1)S(1)} copy-done((bf16[14,4,256,256]{3,2,1,0:T(8,128)(2,1)S(1)}, bf16[14,4,256,256]{3,2,1,0:T(8,128)(2,1)}, u32[]{:S(2)}) %copy-start.20) | copy-done | bytes 7340056
  185.3 23.7 %far_part.1.far_ref = f32[14,64,256]{2,1,0:T(8,128)S(1)} custom-call(s32[8,8]{1,0:T(8,128)S(1)} %broadcast_add_fusion.2.take_ref, bf16[8,8,64,256]{3,2,1,0:T(8,128)(2,1)S(1)} %all-to-all-done.got_ref, bf16[56,256,256]{2,1,0:T(8,128)(2,1)S(1)} %bitcast.11), custom_call_target="tpu_custom_call" | custom-call | flops 5000000000 | tf_op jit(solution)/shard_map/far_part/pallas_call | solution.py:306
  209.1 3.7 %shard_map.103 = f32[64,4096]{1,0:T(8,128)} custom-call(f32[14,64,256]{2,1,0:T(8,128)S(1)} %far_part.1.far_ref, bf16[4,512,256]{2,1,0:T(8,128)(2,1)S(1)} %copy-done.24, bf16[2,512,256]{2,1,0:T(8,128)(2,1)S(1)} %copy-done.30, bf16[8,512,256]{2,1,0:T(8,128)(2,1)S(1)} %copy-done.22, f32[64,4096]{1,0:T(8,128)S(1)} %copy-done.48, f32[64,4096]{1,0:T(8,128)S(1)} %copy-done.50, ...), custom_call_target="tpu_custom_call" | custom-call | flops 4000000000 | tf_op jit(solution)/shard_map/pallas_call | solution.py:67
  (180 shorter events, 20.3 us)
Async XLA Ops:
  2.4 23.1 %copy-start.55 = (s32[8]{0:T(128)S(1)}, s32[8]{0:T(128)}, u32[]{:S(2)}) copy-start(s32[8]{0:T(128)} %constant.187.clone) | copy-start | bytes 100
  2.4 33.1 %collective-permute-start.11 = (bf16[8,80,512]{2,1,0:T(8,128)(2,1)S(1)}, bf16[8,80,512]{2,1,0:T(8,128)(2,1)}, u32[]{:S(2)}, u32[]{:S(2)}) collective-permute-start(bf16[8,80,512]{2,1,0:T(8,128)(2,1)S(1)} %shard_map.91.leaves_ref.refs_0_), channel_id=1, source_target_pairs={{0,56},{4,60},{8,0},{12,4},{16,8},{20,12},{24,16},{28,20},{32,24},... | collective-permute-start | bytes 1966088 | tf_op jit(solution)/shard_map/ppermute | solution.py:378
  8.9 16.7 %collective-permute-start.8 = (bf16[8,80,512]{2,1,0:T(8,128)(2,1)S(1)}, bf16[8,80,512]{2,1,0:T(8,128)(2,1)}, u32[]{:S(2)}, u32[]{:S(2)}) collective-permute-start(bf16[8,80,512]{2,1,0:T(8,128)(2,1)S(1)} %shard_map.91.leaves_ref.refs_0_), channel_id=1, source_target_pairs={{0,8},{4,12},{8,16},{12,20},{16,24},{20,28},{24,32},{28,36},{32,40... | collective-permute-start | bytes 1966088 | tf_op jit(solution)/shard_map/ppermute | solution.py:378
  8.9 31.6 %collective-permute-start.7 = (bf16[64,4096]{1,0:T(8,128)(2,1)}, bf16[64,4096]{1,0:T(8,128)(2,1)}, u32[]{:S(2)}, u32[]{:S(2)}) collective-permute-start(bf16[64,4096]{1,0:T(8,128)(2,1)} %coords_ref.3), channel_id=1, source_target_pairs={{0,4},{4,0},{8,12},{12,8},{16,20},{20,16},{24,28},{28,24},{32,36},... | collective-permute-start | bytes 1572872 | tf_op jit(solution)/shard_map/ppermute | solution.py:400
  10.6 21.5 %collective-permute-start.1 = (bf16[14,64,256]{2,1,0:T(8,128)(2,1)S(1)}, bf16[14,64,256]{2,1,0:T(8,128)(2,1)S(1)}, u32[]{:S(2)}, u32[]{:S(2)}) collective-permute-start(bf16[14,64,256]{2,1,0:T(8,128)(2,1)S(1)} %shard_map.92.refs_0_), channel_id=1, source_target_pairs={{0,56},{4,60},{8,0},{12,4},{16,8},{20,12},{24,16},{28,20},{32,24},... | collective-permute-start | bytes 1376264 | tf_op jit(solution)/shard_map/ppermute | solution.py:378
  13.7 21.8 %collective-permute-start = (bf16[14,64,256]{2,1,0:T(8,128)(2,1)S(1)}, bf16[14,64,256]{2,1,0:T(8,128)(2,1)S(1)}, u32[]{:S(2)}, u32[]{:S(2)}) collective-permute-start(bf16[14,64,256]{2,1,0:T(8,128)(2,1)S(1)} %shard_map.92.refs_0_), channel_id=1, source_target_pairs={{0,8},{4,12},{8,16},{12,20},{16,24},{20,28},{24,32},{28,36},{32,40... | collective-permute-start | bytes 1376264 | tf_op jit(solution)/shard_map/ppermute | solution.py:378
  13.8 48.0 %copy-start.54 = (s32[896,4]{0,1:T(4,128)S(1)}, s32[896,4]{0,1:T(4,128)}, u32[]{:S(2)}) copy-start(s32[896,4]{0,1:T(4,128)} %param.16) | copy-start | bytes 43012
  25.5 23.9 %collective-permute-start.9 = (bf16[8,80,512]{2,1,0:T(8,128)(2,1)}, bf16[8,80,512]{2,1,0:T(8,128)(2,1)}, u32[]{:S(2)}, u32[]{:S(2)}) collective-permute-start(bf16[8,80,512]{2,1,0:T(8,128)(2,1)} %collective-permute-done.8.refs_1_), channel_id=1, source_target_pairs={{0,8},{4,12},{8,16},{12,20},{16,24},{20,28},{24,32},{28,36},{32,40... | collective-permute-start | bytes 1966088 | tf_op jit(solution)/shard_map/ppermute | solution.py:378
  32.1 30.7 %copy-start.6 = (bf16[14,64,256]{2,1,0:T(8,128)(2,1)}, bf16[14,64,256]{2,1,0:T(8,128)(2,1)S(1)}, u32[]{:S(2)}) copy-start(bf16[14,64,256]{2,1,0:T(8,128)(2,1)S(1)} %collective-permute-done.1.refs_2_) | copy-start | bytes 1376260
  32.1 17.4 %collective-permute-start.3 = (bf16[14,64,256]{2,1,0:T(8,128)(2,1)S(1)}, bf16[14,64,256]{2,1,0:T(8,128)(2,1)}, u32[]{:S(2)}, u32[]{:S(2)}) collective-permute-start(bf16[14,64,256]{2,1,0:T(8,128)(2,1)S(1)} %collective-permute-done.1.refs_2_), channel_id=1, source_target_pairs={{0,56},{4,60},{8,0},{12,4},{16,8},{20,12},{24,16},{28,20},{32,24},... | collective-permute-start | bytes 1376264 | tf_op jit(solution)/shard_map/ppermute | solution.py:378
  35.5 23.7 %copy-start.8 = (bf16[14,64,256]{2,1,0:T(8,128)(2,1)}, bf16[14,64,256]{2,1,0:T(8,128)(2,1)S(1)}, u32[]{:S(2)}) copy-start(bf16[14,64,256]{2,1,0:T(8,128)(2,1)S(1)} %collective-permute-done.refs_1_) | copy-start | bytes 1376260
  35.5 23.7 %collective-permute-start.2 = (bf16[14,64,256]{2,1,0:T(8,128)(2,1)S(1)}, bf16[14,64,256]{2,1,0:T(8,128)(2,1)}, u32[]{:S(2)}, u32[]{:S(2)}) collective-permute-start(bf16[14,64,256]{2,1,0:T(8,128)(2,1)S(1)} %collective-permute-done.refs_1_), channel_id=1, source_target_pairs={{0,8},{4,12},{8,16},{12,20},{16,24},{20,28},{24,32},{28,36},{32,40... | collective-permute-start | bytes 1376264 | tf_op jit(solution)/shard_map/ppermute | solution.py:378
  39.2 22.5 %collective-permute-start.24 = (bf16[2,3,80,512]{3,2,1,0:T(8,128)(2,1)S(1)}, bf16[2,3,80,512]{3,2,1,0:T(8,128)(2,1)S(1)}, u32[]{:S(2)}, u32[]{:S(2)}) collective-permute-start(bf16[2,3,80,512]{3,2,1,0:T(8,128)(2,1)S(1)} %get-tuple-element.38), channel_id=1, source_target_pairs={{0,64},{4,68},{8,72},{12,76},{16,80},{20,84},{24,88},{28,92},{32,9... | collective-permute-start | bytes 1474568 | tf_op jit(solution)/shard_map/ppermute | solution.py:395
  40.4 23.6 %collective-permute-start.12 = (bf16[8,80,512]{2,1,0:T(8,128)(2,1)}, bf16[8,80,512]{2,1,0:T(8,128)(2,1)}, u32[]{:S(2)}, u32[]{:S(2)}) collective-permute-start(bf16[8,80,512]{2,1,0:T(8,128)(2,1)} %collective-permute-done.11.refs_2_), channel_id=1, source_target_pairs={{0,56},{4,60},{8,0},{12,4},{16,8},{20,12},{24,16},{28,20},{32,24},... | collective-permute-start | bytes 1966088 | tf_op jit(solution)/shard_map/ppermute | solution.py:378
  49.4 23.9 %collective-permute-start.10 = (bf16[8,80,512]{2,1,0:T(8,128)(2,1)}, bf16[8,80,512]{2,1,0:T(8,128)(2,1)}, u32[]{:S(2)}, u32[]{:S(2)}) collective-permute-start(bf16[8,80,512]{2,1,0:T(8,128)(2,1)} %collective-permute-done.9.refs_0_), channel_id=1, source_target_pairs={{0,8},{4,12},{8,16},{12,20},{16,24},{20,28},{24,32},{28,36},{32,40... | collective-permute-start | bytes 1966088 | tf_op jit(solution)/shard_map/ppermute | solution.py:378
  49.5 24.6 %collective-permute-start.25 = (bf16[2,3,80,512]{3,2,1,0:T(8,128)(2,1)}, bf16[2,3,80,512]{3,2,1,0:T(8,128)(2,1)S(1)}, u32[]{:S(2)}, u32[]{:S(2)}) collective-permute-start(bf16[2,3,80,512]{3,2,1,0:T(8,128)(2,1)} %get-tuple-element.39), channel_id=1, source_target_pairs={{0,128},{4,132},{8,136},{12,140},{16,144},{20,148},{24,152},{28,15... | collective-permute-start | bytes 1474568 | tf_op jit(solution)/shard_map/ppermute | solution.py:395
  59.2 18.0 %collective-permute-start.26 = (bf16[2,3,80,512]{3,2,1,0:T(8,128)(2,1)}, bf16[2,3,80,512]{3,2,1,0:T(8,128)(2,1)S(1)}, u32[]{:S(2)}, u32[]{:S(2)}) collective-permute-start(bf16[2,3,80,512]{3,2,1,0:T(8,128)(2,1)} %get-tuple-element.40), channel_id=1, source_target_pairs={{0,192},{4,196},{8,200},{12,204},{16,208},{20,212},{24,216},{28,22... | collective-permute-start | bytes 1474568 | tf_op jit(solution)/shard_map/ppermute | solution.py:395
  61.7 44.8 %copy-start = (bf16[2,3,80,512]{3,2,1,0:T(8,128)(2,1)}, bf16[2,3,80,512]{3,2,1,0:T(8,128)(2,1)S(1)}, u32[]{:S(2)}) copy-start(bf16[2,3,80,512]{3,2,1,0:T(8,128)(2,1)S(1)} %collective-permute-done.24.refs_1_) | copy-start | bytes 1474564
  61.7 17.5 %collective-permute-start.5 = (bf16[14,64,256]{2,1,0:T(8,128)(2,1)}, bf16[14,64,256]{2,1,0:T(8,128)(2,1)}, u32[]{:S(2)}, u32[]{:S(2)}) collective-permute-start(bf16[14,64,256]{2,1,0:T(8,128)(2,1)} %collective-permute-done.3.refs_4_), channel_id=1, source_target_pairs={{0,56},{4,60},{8,0},{12,4},{16,8},{20,12},{24,16},{28,20},{32,24},... | collective-permute-start | bytes 1376264 | tf_op jit(solution)/shard_map/ppermute | solution.py:378
  64.0 20.6 %collective-permute-start.13 = (bf16[8,80,512]{2,1,0:T(8,128)(2,1)}, bf16[8,80,512]{2,1,0:T(8,128)(2,1)}, u32[]{:S(2)}, u32[]{:S(2)}) collective-permute-start(bf16[8,80,512]{2,1,0:T(8,128)(2,1)} %collective-permute-done.12.refs_1_), channel_id=1, source_target_pairs={{0,56},{4,60},{8,0},{12,4},{16,8},{20,12},{24,16},{28,20},{32,24},... | collective-permute-start | bytes 1966088 | tf_op jit(solution)/shard_map/ppermute | solution.py:378
  73.3 29.5 %collective-permute-start.17 = (bf16[8,80,512]{2,1,0:T(8,128)(2,1)}, bf16[8,80,512]{2,1,0:T(8,128)(2,1)}, u32[]{:S(2)}, u32[]{:S(2)}) collective-permute-start(bf16[8,80,512]{2,1,0:T(8,128)(2,1)} %collective-permute-done.10.refs_0_), channel_id=1, source_target_pairs={{0,8},{4,12},{8,16},{12,20},{16,24},{20,28},{24,32},{28,36},{32,40... | collective-permute-start | bytes 1966088 | tf_op jit(solution)/shard_map/ppermute | solution.py:378
  74.1 32.4 %copy-start.2 = (bf16[2,3,80,512]{3,2,1,0:T(8,128)(2,1)}, bf16[2,3,80,512]{3,2,1,0:T(8,128)(2,1)S(1)}, u32[]{:S(2)}) copy-start(bf16[2,3,80,512]{3,2,1,0:T(8,128)(2,1)S(1)} %collective-permute-done.25.refs_2_) | copy-start | bytes 1474564
  74.1 24.9 %collective-permute-start.4 = (bf16[14,64,256]{2,1,0:T(8,128)(2,1)}, bf16[14,64,256]{2,1,0:T(8,128)(2,1)S(1)}, u32[]{:S(2)}, u32[]{:S(2)}) collective-permute-start(bf16[14,64,256]{2,1,0:T(8,128)(2,1)} %collective-permute-done.2.refs_3_), channel_id=1, source_target_pairs={{0,8},{4,12},{8,16},{12,20},{16,24},{20,28},{24,32},{28,36},{32,40... | collective-permute-start | bytes 1376264 | tf_op jit(solution)/shard_map/ppermute | solution.py:378
  78.0 28.6 %copy-start.4 = (bf16[2,3,80,512]{3,2,1,0:T(8,128)(2,1)}, bf16[2,3,80,512]{3,2,1,0:T(8,128)(2,1)S(1)}, u32[]{:S(2)}) copy-start(bf16[2,3,80,512]{3,2,1,0:T(8,128)(2,1)S(1)} %collective-permute-done.26.refs_3_) | copy-start | bytes 1474564
  78.0 21.0 %collective-permute-start.27 = (bf16[2,2,80,512]{3,2,1,0:T(8,128)(2,1)}, bf16[2,2,80,512]{3,2,1,0:T(8,128)(2,1)S(1)}, u32[]{:S(2)}, u32[]{:S(2)}) collective-permute-start(bf16[2,2,80,512]{3,2,1,0:T(8,128)(2,1)} %get-tuple-element.42), channel_id=1, source_target_pairs={{0,64},{4,68},{8,72},{12,76},{16,80},{20,84},{24,88},{28,92},{32,9... | collective-permute-start | bytes 983048 | tf_op jit(solution)/shard_map/ppermute | solution.py:395
  79.2 21.1 %collective-permute-start.28 = (bf16[2,2,80,512]{3,2,1,0:T(8,128)(2,1)}, bf16[2,2,80,512]{3,2,1,0:T(8,128)(2,1)}, u32[]{:S(2)}, u32[]{:S(2)}) collective-permute-start(bf16[2,2,80,512]{3,2,1,0:T(8,128)(2,1)} %get-tuple-element.43), channel_id=1, source_target_pairs={{0,128},{4,132},{8,136},{12,140},{16,144},{20,148},{24,152},{28,15... | collective-permute-start | bytes 983048 | tf_op jit(solution)/shard_map/ppermute | solution.py:395
  84.6 21.2 %collective-permute-start.29 = (bf16[2,2,80,512]{3,2,1,0:T(8,128)(2,1)}, bf16[2,2,80,512]{3,2,1,0:T(8,128)(2,1)S(1)}, u32[]{:S(2)}, u32[]{:S(2)}) collective-permute-start(bf16[2,2,80,512]{3,2,1,0:T(8,128)(2,1)} %copy-done.40), channel_id=1, source_target_pairs={{0,192},{4,196},{8,200},{12,204},{16,208},{20,212},{24,216},{28,22... | collective-permute-start | bytes 983048 | tf_op jit(solution)/shard_map/ppermute | solution.py:395
  87.3 19.3 %copy-start.13 = (bf16[2,2,80,512]{3,2,1,0:T(8,128)(2,1)S(1)}, bf16[2,2,80,512]{3,2,1,0:T(8,128)(2,1)}, u32[]{:S(2)}) copy-start(bf16[2,2,80,512]{3,2,1,0:T(8,128)(2,1)} %copy-done.12) | copy-start | bytes 983044
  99.0 9.6 %collective-permute-start.6 = (bf16[14,64,256]{2,1,0:T(8,128)(2,1)}, bf16[14,64,256]{2,1,0:T(8,128)(2,1)S(1)}, u32[]{:S(2)}, u32[]{:S(2)}) collective-permute-start(bf16[14,64,256]{2,1,0:T(8,128)(2,1)} %collective-permute-done.5.refs_6_), channel_id=1, source_target_pairs={{0,56},{4,60},{8,0},{12,4},{16,8},{20,12},{24,16},{28,20},{32,24},... | collective-permute-start | bytes 1376264 | tf_op jit(solution)/shard_map/ppermute | solution.py:378
  99.0 10.9 %collective-permute-start.14 = (bf16[2,2,80,512]{3,2,1,0:T(8,128)(2,1)S(1)}, bf16[2,2,80,512]{3,2,1,0:T(8,128)(2,1)S(1)}, u32[]{:S(2)}, u32[]{:S(2)}) collective-permute-start(bf16[2,2,80,512]{3,2,1,0:T(8,128)(2,1)S(1)} %get-tuple-element.29), channel_id=1, source_target_pairs={{0,64},{4,68},{8,72},{12,76},{16,80},{20,84},{24,88},{28,92},{32,9... | collective-permute-start | bytes 983048 | tf_op jit(solution)/shard_map/ppermute | solution.py:395
  100.3 14.6 %collective-permute-start.15 = (bf16[2,2,80,512]{3,2,1,0:T(8,128)(2,1)S(1)}, bf16[2,2,80,512]{3,2,1,0:T(8,128)(2,1)S(1)}, u32[]{:S(2)}, u32[]{:S(2)}) collective-permute-start(bf16[2,2,80,512]{3,2,1,0:T(8,128)(2,1)S(1)} %get-tuple-element.30), channel_id=1, source_target_pairs={{0,128},{4,132},{8,136},{12,140},{16,144},{20,148},{24,152},{28,15... | collective-permute-start | bytes 983048 | tf_op jit(solution)/shard_map/ppermute | solution.py:395
  102.8 15.8 %collective-permute-start.16 = (bf16[2,2,80,512]{3,2,1,0:T(8,128)(2,1)S(1)}, bf16[2,2,80,512]{3,2,1,0:T(8,128)(2,1)S(1)}, u32[]{:S(2)}, u32[]{:S(2)}) collective-permute-start(bf16[2,2,80,512]{3,2,1,0:T(8,128)(2,1)S(1)} %get-tuple-element.31), channel_id=1, source_target_pairs={{0,192},{4,196},{8,200},{12,204},{16,208},{20,212},{24,216},{28,22... | collective-permute-start | bytes 983048 | tf_op jit(solution)/shard_map/ppermute | solution.py:395
  105.9 14.0 %collective-permute-start.18 = (bf16[2,1,80,512]{3,2,1,0:T(8,128)(2,1)S(1)}, bf16[2,1,80,512]{3,2,1,0:T(8,128)(2,1)S(1)}, u32[]{:S(2)}, u32[]{:S(2)}) collective-permute-start(bf16[2,1,80,512]{3,2,1,0:T(8,128)(2,1)S(1)} %get-tuple-element.33), channel_id=1, source_target_pairs={{0,64},{4,68},{8,72},{12,76},{16,80},{20,84},{24,88},{28,92},{32,9... | collective-permute-start | bytes 491528 | tf_op jit(solution)/shard_map/ppermute | solution.py:395
  108.6 41.7 %collective-permute-start.30 = (bf16[8,5,16,512]{3,2,1,0:T(8,128)(2,1)S(1)}, bf16[8,5,16,512]{3,2,1,0:T(8,128)(2,1)}, u32[]{:S(2)}, u32[]{:S(2)}) collective-permute-start(bf16[8,5,16,512]{3,2,1,0:T(8,128)(2,1)S(1)} %shard_map.100.refs_8_), channel_id=1, source_target_pairs={{0,1},{1,2},{2,3},{3,0},{4,5},{5,6},{6,7},{7,4},{8,9},{9,10},{10,1... | collective-permute-start | bytes 1966088 | tf_op jit(solution)/shard_map/ppermute | solution.py:412
  110.7 41.0 %collective-permute-start.31 = (bf16[8,5,16,512]{3,2,1,0:T(8,128)(2,1)S(1)}, bf16[8,5,16,512]{3,2,1,0:T(8,128)(2,1)}, u32[]{:S(2)}, u32[]{:S(2)}) collective-permute-start(bf16[8,5,16,512]{3,2,1,0:T(8,128)(2,1)S(1)} %shard_map.100.refs_8_), channel_id=1, source_target_pairs={{0,3},{1,0},{2,1},{3,2},{4,7},{5,4},{6,5},{7,6},{8,11},{9,8},{10,9... | collective-permute-start | bytes 1966088 | tf_op jit(solution)/shard_map/ppermute | solution.py:412
  115.7 36.0 %collective-permute-start.32 = (bf16[8,5,16,512]{3,2,1,0:T(8,128)(2,1)S(1)}, bf16[8,5,16,512]{3,2,1,0:T(8,128)(2,1)}, u32[]{:S(2)}, u32[]{:S(2)}) collective-permute-start(bf16[8,5,16,512]{3,2,1,0:T(8,128)(2,1)S(1)} %shard_map.100.refs_8_), channel_id=1, source_target_pairs={{0,2},{1,3},{2,0},{3,1},{4,6},{5,7},{6,4},{7,5},{8,10},{9,11},{10,... | collective-permute-start | bytes 1966088 | tf_op jit(solution)/shard_map/ppermute | solution.py:412
  119.3 22.2 %collective-permute-start.19 = (bf16[2,1,80,512]{3,2,1,0:T(8,128)(2,1)}, bf16[2,1,80,512]{3,2,1,0:T(8,128)(2,1)}, u32[]{:S(2)}, u32[]{:S(2)}) collective-permute-start(bf16[2,1,80,512]{3,2,1,0:T(8,128)(2,1)} %get-tuple-element.34), channel_id=1, source_target_pairs={{0,128},{4,132},{8,136},{12,140},{16,144},{20,148},{24,152},{28,15... | collective-permute-start | bytes 491528 | tf_op jit(solution)/shard_map/ppermute | solution.py:395
  119.9 21.7 %collective-permute-start.20 = (bf16[2,1,80,512]{3,2,1,0:T(8,128)(2,1)}, bf16[2,1,80,512]{3,2,1,0:T(8,128)(2,1)}, u32[]{:S(2)}, u32[]{:S(2)}) collective-permute-start(bf16[2,1,80,512]{3,2,1,0:T(8,128)(2,1)} %get-tuple-element.35), channel_id=1, source_target_pairs={{0,192},{4,196},{8,200},{12,204},{16,208},{20,212},{24,216},{28,22... | collective-permute-start | bytes 491528 | tf_op jit(solution)/shard_map/ppermute | solution.py:395
  132.6 49.6 %all-to-all-start = ((bf16[8,8,64,256]{3,2,1,0:T(8,128)(2,1)}), bf16[8,8,64,256]{3,2,1,0:T(8,128)(2,1)S(1)}, u32[]{:S(2)}, u32[]{:S(2)}) async-start(bf16[8,8,64,256]{3,2,1,0:T(8,128)(2,1)} %shard_map.93), calls=%async_computation | async-start | bytes 4194304 | tf_op jit(solution)/shard_map/all_to_all | solution.py:404
  147.5 22.0 %collective-permute-start.21 = (bf16[8,3,16,512]{3,2,1,0:T(8,128)(2,1)S(1)}, bf16[8,3,16,512]{3,2,1,0:T(8,128)(2,1)S(1)}, u32[]{:S(2)}, u32[]{:S(2)}) collective-permute-start(bf16[8,3,16,512]{3,2,1,0:T(8,128)(2,1)S(1)} %shard_map.97.refs_8_), channel_id=1, source_target_pairs={{0,1},{1,2},{2,3},{3,0},{4,5},{5,6},{6,7},{7,4},{8,9},{9,10},{10,1... | collective-permute-start | bytes 1179656 | tf_op jit(solution)/shard_map/ppermute | solution.py:412
  148.3 21.3 %collective-permute-start.22 = (bf16[8,3,16,512]{3,2,1,0:T(8,128)(2,1)S(1)}, bf16[8,3,16,512]{3,2,1,0:T(8,128)(2,1)S(1)}, u32[]{:S(2)}, u32[]{:S(2)}) collective-permute-start(bf16[8,3,16,512]{3,2,1,0:T(8,128)(2,1)S(1)} %shard_map.97.refs_8_), channel_id=1, source_target_pairs={{0,3},{1,0},{2,1},{3,2},{4,7},{5,4},{6,5},{7,6},{8,11},{9,8},{10,9... | collective-permute-start | bytes 1179656 | tf_op jit(solution)/shard_map/ppermute | solution.py:412
  150.3 19.3 %collective-permute-start.23 = (bf16[8,3,16,512]{3,2,1,0:T(8,128)(2,1)S(1)}, bf16[8,3,16,512]{3,2,1,0:T(8,128)(2,1)S(1)}, u32[]{:S(2)}, u32[]{:S(2)}) collective-permute-start(bf16[8,3,16,512]{3,2,1,0:T(8,128)(2,1)S(1)} %shard_map.97.refs_8_), channel_id=1, source_target_pairs={{0,2},{1,3},{2,0},{3,1},{4,6},{5,7},{6,4},{7,5},{8,10},{9,11},{10,... | collective-permute-start | bytes 1179656 | tf_op jit(solution)/shard_map/ppermute | solution.py:412
  181.0 28.1 %collective-permute-start.33 = (f32[64,4096]{1,0:T(8,128)S(1)}, f32[64,4096]{1,0:T(8,128)}, u32[]{:S(2)}, u32[]{:S(2)}) collective-permute-start(f32[64,4096]{1,0:T(8,128)S(1)} %get-tuple-element.48), channel_id=1, source_target_pairs={{0,4},{4,0},{8,12},{12,8},{16,20},{20,16},{24,28},{28,24},{32,36},... | collective-permute-start | bytes 3145736 | tf_op jit(solution)/shard_map/ppermute | solution.py:400
  185.3 23.8 %copy-start.22 = (bf16[8,512,256]{2,1,0:T(8,128)(2,1)S(1)}, bf16[8,512,256]{2,1,0:T(8,128)(2,1)}, u32[]{:S(2)}) copy-start(bf16[8,512,256]{2,1,0:T(8,128)(2,1)} %basis_ref.3) | copy-start | bytes 6291460
  185.3 23.8 %copy-start.24 = (bf16[4,512,256]{2,1,0:T(8,128)(2,1)S(1)}, bf16[4,512,256]{2,1,0:T(8,128)(2,1)}, u32[]{:S(2)}) copy-start(bf16[4,512,256]{2,1,0:T(8,128)(2,1)} %one_ref.3) | copy-start | bytes 3145732
  185.3 23.8 %copy-start.30 = (bf16[2,512,256]{2,1,0:T(8,128)(2,1)S(1)}, bf16[2,512,256]{2,1,0:T(8,128)(2,1)}, u32[]{:S(2)}) copy-start(bf16[2,512,256]{2,1,0:T(8,128)(2,1)} %two_ref.3) | copy-start | bytes 1572868
  185.3 23.8 %copy-start.48 = (f32[64,4096]{1,0:T(8,128)S(1)}, f32[64,4096]{1,0:T(8,128)}, u32[]{:S(2)}) copy-start(f32[64,4096]{1,0:T(8,128)} %copy-done.47) | copy-start | bytes 3145732
  185.3 23.8 %copy-start.50 = (f32[64,4096]{1,0:T(8,128)S(1)}, f32[64,4096]{1,0:T(8,128)}, u32[]{:S(2)}) copy-start(f32[64,4096]{1,0:T(8,128)} %copy-done.49) | copy-start | bytes 3145732
  (43 other events, 302.3 us)

commit v3 on v2

--- a/solution.py
+++ b/solution.py
@@ -22,7 +22,7 @@
 ROWS = R + QUART
 AUG = 128
 OFFSETS = (0, -1, 1, -2, 2, -3, 3, 4)
-LEAF_CHUNKS = (((0, 3), (3, 5)), ((5, 7), (7, 8)))
+LEAF_CHUNKS = (((0, 3),), ((3, 5), (5, 7)), ((7, 8),))
 
 
 F32 = jnp.float32
@@ -123,9 +123,10 @@
 def own_kernel(pos_ref, rhs_ref, coords_ref, other_ref, target_ref, near_ref, spread_ref):
     y = pos_ref[0]
     empty = jnp.zeros((AUG - FEAT - 16, LEAF), BF16)
-    for core, ref in enumerate((coords_ref, other_ref)):
-        for leaf in range(LEAF_DEV):
-            columns = slice(leaf * LEAF, (leaf + 1) * LEAF)
+
+    def spread_leaf(leaf, carry):
+        columns = pl.ds(pl.multiple_of(leaf * LEAF, LEAF), LEAF)
+        for core, ref in enumerate((coords_ref, other_ref)):
             pieces = []
             for shift_by in (0, NY - 1, 1, 2):
                 start = pl.multiple_of(lax.rem(y + shift_by, NY) * QUART, QUART)
@@ -136,6 +137,9 @@
                 spread_ref[leaf, :FEAT, :] = jnp.concatenate(pieces, axis=0)
                 spread_ref[leaf, FEAT : FEAT + 16, :] = square_rows(pieces, True)
                 spread_ref[leaf, FEAT + 16 :, :] = empty
+        return carry
+
+    lax.fori_loop(0, LEAF_DEV, spread_leaf, 0)
 
     def pair(i, carry):
         for leaf in (2 * i, 2 * i + 1):
@@ -186,11 +190,15 @@
         return carry
 
     lax.fori_loop(0, GROUP * slots // UNROLL, some, 0)
-    for core, out_ref in enumerate((own_ref, other_ref)):
-        for leaf in range(LEAF_DEV):
-            columns = slice(leaf * LEAF, (leaf + 1) * LEAF)
+
+    def emit(leaf, carry):
+        columns = pl.ds(pl.multiple_of(leaf * LEAF, LEAF), LEAF)
+        for core, out_ref in enumerate((own_ref, other_ref)):
             near = near_ref[core * LEAF_DEV + leaf].T
             out_ref[:, columns] = near + before_refs[core][:, columns] if before_refs else near
+        return carry
+
+    lax.fori_loop(0, LEAF_DEV, emit, 0)
 
 
 def near_chunk(chunks, take, got, pieces, targets, before):
@@ -207,7 +215,7 @@
             pltpu.VMEM((GROUP, slots, R, LEAF), BF16),
             pltpu.VMEM((2 * LEAF_DEV, LEAF, R), F32),
         ],
-        40,
+        28,
     )
 
 
@@ -230,17 +238,25 @@
 
 def choose_kernel(first, send_ref, *refs):
     out_ref = refs[-1]
-    for slot, ref in enumerate(refs[:-1]):
-        for target in range(GROUP):
+
+    def fill(target, carry):
+        for slot, ref in enumerate(refs[:-1]):
             out_ref[target, slot] = ref[send_ref[target, first + slot]]
+        return carry
+
+    lax.fori_loop(0, GROUP, fill, 0)
 
 
 def choose_steps_kernel(first, send_ref, *refs):
     sources, outs = refs[:-NX], refs[-NX:]
-    for slot, ref in enumerate(sources):
-        for step in range(NX):
-            for side in range(NC):
+
+    def fill(side, carry):
+        for slot, ref in enumerate(sources):
+            for step in range(NX):
                 outs[step][side, slot] = ref[send_ref[NC * step + side, first + slot]]
+        return carry
+
+    lax.fori_loop(0, NC, fill, 0)
 
 
 def choose(first, send, sources, kind):
@@ -274,51 +290,29 @@
     return call(skeleton_kernel, 3, out, (), (leaves, basis, one, two))
 
 
-def far_kernel(take_ref, got_ref, blocks_ref, out_ref, held_ref, sems):
+def far_kernel(take_ref, got_ref, blocks_ref, out_ref):
     out_ref[...] = jnp.zeros_like(out_ref)
 
-    def fetch(i):
-        at = jnp.maximum(take_ref[i // NZ, i % NZ], 0)
-        return pltpu.make_async_copy(blocks_ref.at[at], held_ref.at[i], sems.at[i])
-
-    def begin(i, carry):
-        fetch(i).start()
-        return carry
-
-    lax.fori_loop(0, GROUP * NZ, begin, 0)
-
-    def source_of(source, carry):
-        for slot in range(NZ):
-            item = source * NZ + slot
+    def some(i, carry):
+        for buffer in range(UNROLL):
+            item = i * UNROLL + buffer
+            source, slot = item // NZ, item % NZ
             which = take_ref[source, slot]
             weights = got_ref[source, slot]
             weights = jnp.where(which >= 0, weights, jnp.zeros_like(weights))
-            fetch(item).wait()
-            out_ref[jnp.maximum(which, 0) // FAR] += jnp.dot(
-                weights, held_ref[item], preferred_element_type=F32
-            )
-        return carry
-
-    lax.fori_loop(0, GROUP, source_of, 0)
+            at = jnp.maximum(which, 0)
+            out_ref[at // FAR] += jnp.dot(weights, blocks_ref[at], preferred_element_type=F32)
+        return carry
+
+    lax.fori_loop(0, GROUP * NZ // UNROLL, some, 0)
 
 
 def far_part(take, got, blocks):
-    return pl.pallas_call(
-        far_kernel,
-        in_specs=[SMEM, VMEM, pl.BlockSpec(memory_space=pltpu.HBM)],
-        out_specs=VMEM,
-        out_shape=shaped((NODE_DEV, R, RANK), F32),
-        scratch_shapes=[
-            pltpu.VMEM((GROUP * NZ, RANK, RANK), BF16),
-            pltpu.SemaphoreType.DMA((GROUP * NZ,)),
-        ],
-        compiler_params=pltpu.CompilerParams(vmem_limit_bytes=20 << 20),
-        cost_estimate=cost(5),
-        name="far_part",
-    )(take, got, blocks)
-
-
-def finish_kernel(far_ref, one_ref, two_ref, basis_ref, self_ref, own_ref, other_ref, out_ref):
+    out = shaped((NODE_DEV, R, RANK), F32)
+    return call(far_kernel, 5, out, (take,), (got, blocks))
+
+
+def finish_kernel(far_ref, one_ref, two_ref, basis_ref, self_ref, own_ref, other_ref, out_ref, low_ref):
     for m in range(LEAF_DEV // 4):
         spread = nt(far_ref[LEAF_DEV * 3 // 2 + m].astype(BF16), two_ref[m])
         for side in range(2):
@@ -328,14 +322,22 @@
             for part in range(2):
                 leaf = 2 * node + part
                 lowest = far_ref[leaf] + lower[:, part * RANK : (part + 1) * RANK]
-                columns = slice(leaf * LEAF, (leaf + 1) * LEAF)
-                near = self_ref[:, columns] + own_ref[:, columns] + other_ref[:, columns]
-                out_ref[:, columns] = near + nt(lowest.astype(BF16), basis_ref[leaf])
+                low_ref[leaf] = lowest.astype(BF16)
+
+    def emit(i, carry):
+        for leaf in (2 * i, 2 * i + 1):
+            columns = pl.ds(pl.multiple_of(leaf * LEAF, LEAF), LEAF)
+            near = self_ref[:, columns] + own_ref[:, columns] + other_ref[:, columns]
+            out_ref[:, columns] = near + nt(low_ref[leaf], basis_ref[leaf])
+        return carry
+
+    lax.fori_loop(0, LEAF_DEV // 2, emit, 0)
 
 
 def finish(far, one, two, basis, *near):
     out = shaped((R, LEAF_DEV * LEAF), F32)
-    return call(finish_kernel, 4, out, (), (far, one, two, basis, *near), megabytes=20)
+    scratch = [pltpu.VMEM((LEAF_DEV, R, RANK), BF16)]
+    return call(finish_kernel, 4, out, (), (far, one, two, basis, *near), scratch, 20)
 
 
 def tables(neighbours, far_lists, x, z, c, group):

time: 214 us -> 200 us (0.935)
  Pallas kernels: 74.2 us -> 61.8 us
  local copies, waits for them, and re-layouts: 25 us -> 17.4 us
  starting transfers between devices: 55.3 us -> 61.4 us
  other arithmetic: 1.39 us -> 5.24 us
  waiting for transfers between devices: 56.2 us -> 52.5 us
    pallas_call x1 -> x0, Pallas kernels: 23.7 us -> none  [far_part(): pl.pallas_call(far_kernel, in_specs=[SMEM, VMEM, pl.BlockSpec(memory_spac...]
    pallas_call x13 -> x16, Pallas kernels: 50.5 us -> 61.8 us  [call(): pl.pallas_call(kernel, in_specs=[SMEM] * len(tables) + [VMEM] * len(array...]
    unnamed x114 -> x108, local copies, waits for them, and re-layouts: 22 us -> 14.8 us
    ppermute x14, waiting for transfers between devices: 53.4 us -> 48.7 us  [shift(): return lax.ppermute(value, 'leaf', ring(step))]
    ppermute x14, starting transfers between devices: 16.1 us -> 20.5 us  [shift(): return lax.ppermute(value, 'leaf', ring(step))]
    ppermute x6 -> x9, starting transfers between devices: 9.88 us -> 12.7 us  [join_planes(): lax.ppermute(quarter, 'rhs', [(i, (i + step) % NY) for i in range(NY)])]
  transfers between devices with their start and end apart: 35 -> 38, of which waited for: 8 -> 9; matrix products, arithmetic and copies ran while one was open for 3% -> 4% of each run, Pallas kernels for 33% -> 28%
where the time goes in v3:
time: 200 us; the launch traced here: 199 us
  Pallas kernels  61.8 us (31%)
  starting transfers between devices  61.4 us (31%)
  waiting for transfers between devices  52.5 us (26%)
  local copies, waits for them, and re-layouts  17.4 us (9%)
  other arithmetic  5.24 us (3%)
    pallas_call x16, Pallas kernels, call(): pl.pallas_call(kernel, in_specs=[SMEM] * len(tables) + [VMEM] * len(array...  61.8 us
    ppermute x14, waiting for transfers between devices, shift(): return lax.ppermute(value, 'leaf', ring(step))  48.7 us
    ppermute x14, starting transfers between devices, shift(): return lax.ppermute(value, 'leaf', ring(step))  20.5 us
    ppermute x12, starting transfers between devices, cross(): got.append(lax.ppermute(chosen[step], 'leaf', across(step)))  18.5 us
    unnamed x108, local copies, waits for them, and re-layouts  14.8 us
    ppermute x9, starting transfers between devices, join_planes(): lax.ppermute(quarter, 'rhs', [(i, (i + step) % NY) for i in range(NY)])  12.7 us
    all_to_all x1, starting transfers between devices, exchange(): lax.all_to_all(chosen, 'leaf', split_axis=0, concat_axis=0, axis_index_gr...  7.85 us
  transfers between devices with their start and end apart: 38, of which 9 were waited for; matrix products, arithmetic and copies ran while one was open for 4% of the time, Pallas kernels for 28%

profile of v3, /device:TPU:1, one launch (start us, length us, event | category | flops | bytes accessed | tf_op | source)
XLA Modules:
  0.0 199.1 jit_solution(15383533950744521215)
XLA Ops:
  1.2 2.0 shard_map.91.leaves_ref.refs_0_
  3.2 6.4 %collective-permute-start.18 = (bf16[8,80,512]{2,1,0:T(8,128)(2,1)}, bf16[8,80,512]{2,1,0:T(8,128)(2,1)S(1)}, u32[]{:S(2)}, u32[]{:S(2)}) collective-permute-start(bf16[8,80,512]{2,1,0:T(8,128)(2,1)} %shard_map.91.leaves_ref.refs_0_), channel_id=1, source_target_pairs={{0,56},{4,60},{8,0},{12,4},{16,8},{20,12},{24,16},{28,20},{32,24},... | collective-permute-start | bytes 1966088 | tf_op jit(solution)/shard_map/ppermute | solution.py:380
  10.5 1.9 shard_map.92.refs_0_
  12.4 3.0 %collective-permute-start.1 = (bf16[14,64,256]{2,1,0:T(8,128)(2,1)S(1)}, bf16[14,64,256]{2,1,0:T(8,128)(2,1)S(1)}, u32[]{:S(2)}, u32[]{:S(2)}) collective-permute-start(bf16[14,64,256]{2,1,0:T(8,128)(2,1)S(1)} %shard_map.92.refs_0_), channel_id=1, source_target_pairs={{0,56},{4,60},{8,0},{12,4},{16,8},{20,12},{24,16},{28,20},{32,24},... | collective-permute-start | bytes 1376264 | tf_op jit(solution)/shard_map/ppermute | solution.py:380
  15.9 10.6 %collective-permute-done.8.refs_1_ = bf16[8,80,512]{2,1,0:T(8,128)(2,1)} collective-permute-done((bf16[8,80,512]{2,1,0:T(8,128)(2,1)}, bf16[8,80,512]{2,1,0:T(8,128)(2,1)}, u32[]{:S(2)}, u32[]{:S(2)}) %collective-permute-start.8) | collective-permute-done | bytes 655392 | tf_op jit(solution)/shard_map/ppermute | solution.py:380
  27.6 2.7 %collective-permute-start.19 = (bf16[8,80,512]{2,1,0:T(8,128)(2,1)S(1)}, bf16[8,80,512]{2,1,0:T(8,128)(2,1)}, u32[]{:S(2)}, u32[]{:S(2)}) collective-permute-start(bf16[8,80,512]{2,1,0:T(8,128)(2,1)S(1)} %collective-permute-done.18.refs_2_), channel_id=1, source_target_pairs={{0,56},{4,60},{8,0},{12,4},{16,8},{20,12},{24,16},{28,20},{32,24},... | collective-permute-start | bytes 1966088 | tf_op jit(solution)/shard_map/ppermute | solution.py:380
  31.1 1.9 collective-permute-done.1.refs_2_
  33.0 3.4 %collective-permute-start.3 = (bf16[14,64,256]{2,1,0:T(8,128)(2,1)S(1)}, bf16[14,64,256]{2,1,0:T(8,128)(2,1)S(1)}, u32[]{:S(2)}, u32[]{:S(2)}) collective-permute-start(bf16[14,64,256]{2,1,0:T(8,128)(2,1)S(1)} %collective-permute-done.1.refs_2_), channel_id=1, source_target_pairs={{0,56},{4,60},{8,0},{12,4},{16,8},{20,12},{24,16},{28,20},{32,24},... | collective-permute-start | bytes 1376264 | tf_op jit(solution)/shard_map/ppermute | solution.py:380
  36.5 13.9 %collective-permute-done.9.refs_0_ = bf16[8,80,512]{2,1,0:T(8,128)(2,1)} collective-permute-done((bf16[8,80,512]{2,1,0:T(8,128)(2,1)}, bf16[8,80,512]{2,1,0:T(8,128)(2,1)}, u32[]{:S(2)}, u32[]{:S(2)}) %collective-permute-start.9) | collective-permute-done | bytes 655392 | tf_op jit(solution)/shard_map/ppermute | solution.py:380
  50.4 2.5 %shard_map.101 = (bf16[2,3,80,512]{3,2,1,0:T(8,128)(2,1)S(1)}, bf16[2,3,80,512]{3,2,1,0:T(8,128)(2,1)}, bf16[2,3,80,512]{3,2,1,0:T(8,128)(2,1)}, bf16[2,3,80,512]{3,2,1,0:T(8,128)(2,1)S(1)}) custom-call(s32[8,8]{1,0:T(8,128)S(1)} %select_reduce_fusion.send_ref, bf16[8,80,512]{2,1,0:T(8,128)(2,1)} %shard_map.91.leaves_ref.refs_0_, ...), custom_call_target="tpu_custom_call" | custom-call | flops 1000000000 | tf_op jit(solution)/shard_map/pallas_call | solution.py:67
  53.7 1.2 collective-permute-start.30
  54.9 2.0 %collective-permute-done.3.refs_4_ = bf16[14,64,256]{2,1,0:T(8,128)(2,1)S(1)} collective-permute-done((bf16[14,64,256]{2,1,0:T(8,128)(2,1)S(1)}, bf16[14,64,256]{2,1,0:T(8,128)(2,1)S(1)}, u32[]{:S(2)}, u32[]{:S(2)}) %collective-permute-start.3) | collective-permute-done | bytes 458784 | tf_op jit(solution)/shard_map/ppermute | solution.py:380
  56.9 2.7 %collective-permute-start.31 = (bf16[2,3,80,512]{3,2,1,0:T(8,128)(2,1)}, bf16[2,3,80,512]{3,2,1,0:T(8,128)(2,1)}, u32[]{:S(2)}, u32[]{:S(2)}) collective-permute-start(bf16[2,3,80,512]{3,2,1,0:T(8,128)(2,1)} %get-tuple-element.45), channel_id=1, source_target_pairs={{0,128},{4,132},{8,136},{12,140},{16,144},{20,148},{24,152},{28,15... | collective-permute-start | bytes 1474568 | tf_op jit(solution)/shard_map/ppermute | solution.py:397
  59.7 3.4 %collective-permute-start.23 = (bf16[8,80,512]{2,1,0:T(8,128)(2,1)}, bf16[8,80,512]{2,1,0:T(8,128)(2,1)}, u32[]{:S(2)}, u32[]{:S(2)}) collective-permute-start(bf16[8,80,512]{2,1,0:T(8,128)(2,1)} %collective-permute-done.19.refs_1_), channel_id=1, source_target_pairs={{0,56},{4,60},{8,0},{12,4},{16,8},{20,12},{24,16},{28,20},{32,24},... | collective-permute-start | bytes 1966088 | tf_op jit(solution)/shard_map/ppermute | solution.py:380
  63.7 2.6 %collective-permute-done.10.refs_0_ = bf16[8,80,512]{2,1,0:T(8,128)(2,1)} collective-permute-done((bf16[8,80,512]{2,1,0:T(8,128)(2,1)}, bf16[8,80,512]{2,1,0:T(8,128)(2,1)}, u32[]{:S(2)}, u32[]{:S(2)}) %collective-permute-start.10) | collective-permute-done | bytes 655392 | tf_op jit(solution)/shard_map/ppermute | solution.py:380
  67.8 8.4 %collective-permute-done.2.refs_3_ = bf16[14,64,256]{2,1,0:T(8,128)(2,1)S(1)} collective-permute-done((bf16[14,64,256]{2,1,0:T(8,128)(2,1)S(1)}, bf16[14,64,256]{2,1,0:T(8,128)(2,1)S(1)}, u32[]{:S(2)}, u32[]{:S(2)}) %collective-permute-start.2) | collective-permute-done | bytes 458784 | tf_op jit(solution)/shard_map/ppermute | solution.py:380
  76.2 2.4 %collective-permute-start.32 = (bf16[2,3,80,512]{3,2,1,0:T(8,128)(2,1)}, bf16[2,3,80,512]{3,2,1,0:T(8,128)(2,1)}, u32[]{:S(2)}, u32[]{:S(2)}) collective-permute-start(bf16[2,3,80,512]{3,2,1,0:T(8,128)(2,1)} %copy-done.9), channel_id=1, source_target_pairs={{0,192},{4,196},{8,200},{12,204},{16,208},{20,212},{24,216},{28,22... | collective-permute-start | bytes 1474568 | tf_op jit(solution)/shard_map/ppermute | solution.py:397
  78.6 1.5 collective-permute-start.4
  80.0 2.1 %shard_map.98 = (bf16[2,2,80,512]{3,2,1,0:T(8,128)(2,1)S(1)}, bf16[2,2,80,512]{3,2,1,0:T(8,128)(2,1)}, bf16[2,2,80,512]{3,2,1,0:T(8,128)(2,1)S(1)}, bf16[2,2,80,512]{3,2,1,0:T(8,128)(2,1)S(1)}) custom-call(s32[8,8]{1,0:T(8,128)S(1)} %select_reduce_fusion.send_ref, bf16[8,80,512]{2,1,0:T(8,128)(2,1)} %collective-permute-done.9.refs_0_, ...), custom_call_target="tpu_custom_call" | custom-call | flops 1000000000 | tf_op jit(solution)/shard_map/pallas_call | solution.py:67
  86.4 1.4 shard_map.99
  87.8 1.8 collective-permute-start.21
  90.7 9.3 %collective-permute-done.4.refs_5_ = bf16[14,64,256]{2,1,0:T(8,128)(2,1)S(1)} collective-permute-done((bf16[14,64,256]{2,1,0:T(8,128)(2,1)S(1)}, bf16[14,64,256]{2,1,0:T(8,128)(2,1)S(1)}, u32[]{:S(2)}, u32[]{:S(2)}) %collective-permute-start.4) | collective-permute-done | bytes 458784 | tf_op jit(solution)/shard_map/ppermute | solution.py:380
  99.9 1.2 collective-permute-start.24
  101.1 2.5 %collective-permute-start.25 = (bf16[2,2,80,512]{3,2,1,0:T(8,128)(2,1)S(1)}, bf16[2,2,80,512]{3,2,1,0:T(8,128)(2,1)S(1)}, u32[]{:S(2)}, u32[]{:S(2)}) collective-permute-start(bf16[2,2,80,512]{3,2,1,0:T(8,128)(2,1)S(1)} %get-tuple-element.41), channel_id=1, source_target_pairs={{0,128},{4,132},{8,136},{12,140},{16,144},{20,148},{24,152},{28,15... | collective-permute-start | bytes 983048 | tf_op jit(solution)/shard_map/ppermute | solution.py:397
  106.3 1.4 shard_map.102.refs_4_
  107.7 1.9 shard_map.96
  110.3 1.3 collective-permute-start.33
  111.6 1.5 collective-permute-start.34
  113.1 1.5 collective-permute-start.35
  115.8 2.8 %collective-permute-done.26.refs_7_ = bf16[2,2,80,512]{3,2,1,0:T(8,128)(2,1)S(1)} collective-permute-done((bf16[2,2,80,512]{3,2,1,0:T(8,128)(2,1)S(1)}, bf16[2,2,80,512]{3,2,1,0:T(8,128)(2,1)S(1)}, u32[]{:S(2)}, u32[]{:S(2)}) %collective-permute-start.26) | collective-permute-done | bytes 327712 | tf_op jit(solution)/shard_map/ppermute | solution.py:397
  118.5 1.4 collective-permute-start.12
  119.9 6.0 %shard_map.95 = (bf16[16,512,128]{2,1,0:T(8,128)(2,1)S(1)}, f32[64,4096]{1,0:T(8,128)S(1)}) custom-call(s32[1]{0:T(128)} %bitcast.3.y_ref.pos_ref, bf16[64,4096]{1,0:T(8,128)(2,1)S(1)} %copy-done.6, bf16[64,4096]{1,0:T(8,128)(2,1)} %coords_ref.3, bf16[64,4096]{1,0:T(8,128)(2,1)} %collective-permute-done.7.other_ref), custom_call_target="tpu_custom_call" | custom-call | flops 5000000000 | tf_op jit(solution)/shard_map/pallas_call | solution.py:67
  127.0 1.3 collective-permute-start.27
  128.3 1.7 collective-permute-start.28
  130.1 1.3 collective-permute-start.29
  131.4 3.0 %collective-permute-start.13 = (bf16[2,1,80,512]{3,2,1,0:T(8,128)(2,1)}, bf16[2,1,80,512]{3,2,1,0:T(8,128)(2,1)}, u32[]{:S(2)}, u32[]{:S(2)}) collective-permute-start(bf16[2,1,80,512]{3,2,1,0:T(8,128)(2,1)} %get-tuple-element.32), channel_id=1, source_target_pairs={{0,128},{4,132},{8,136},{12,140},{16,144},{20,148},{24,152},{28,15... | collective-permute-start | bytes 491528 | tf_op jit(solution)/shard_map/ppermute | solution.py:397
  135.1 10.9 %shard_map.103 = (f32[64,4096]{1,0:T(8,128)S(1)}, f32[64,4096]{1,0:T(8,128)S(1)}) custom-call(s32[8,8]{1,0:T(8,128)S(1)} %broadcast_add_fusion.1.take_ref, bf16[2,3,80,512]{3,2,1,0:T(8,128)(2,1)S(1)} %copy-done.33, bf16[2,3,80,512]{3,2,1,0:T(8,128)(2,1)} %collective-permute-done.30.refs_1_, bf16[2,3,80,512]{3,2,1,0:T(8,128)(2,1)} %collective-permute-done.31.refs_2_, ...), custom_call_target="tpu_custom_call" | custom-call | flops 9600000000 | tf_op jit(solution)/shard_map/pallas_call | solution.py:67
  148.0 2.1 %shard_map.93 = bf16[8,8,64,256]{3,2,1,0:T(8,128)(2,1)} custom-call(s32[8,8]{1,0:T(8,128)S(1)} %select_reduce_fusion.2.send_ref, bf16[14,64,256]{2,1,0:T(8,128)(2,1)S(1)} %shard_map.92.refs_0_, bf16[14,64,256]{2,1,0:T(8,128)(2,1)S(1)} %collective-permute-done.refs_1_, bf16[14,64,256]{2,1,0:T(8,128)(2,1)S(1)} %collective-permute-done.1.refs_2_, ...), custom_call_target="tpu_custom_call" | custom-call | flops 1000000000 | tf_op jit(solution)/shard_map/pallas_call | solution.py:67
  150.1 7.9 %all-to-all-start = ((bf16[8,8,64,256]{3,2,1,0:T(8,128)(2,1)}), bf16[8,8,64,256]{3,2,1,0:T(8,128)(2,1)S(1)}, u32[]{:S(2)}, u32[]{:S(2)}) async-start(bf16[8,8,64,256]{3,2,1,0:T(8,128)(2,1)} %shard_map.93), calls=%async_computation | async-start | bytes 4194304 | tf_op jit(solution)/shard_map/all_to_all | solution.py:406
  159.3 2.7 %collective-permute-start.16 = (bf16[8,1,16,512]{3,2,1,0:T(8,128)(2,1)S(1)}, bf16[8,1,16,512]{3,2,1,0:T(8,128)(2,1)S(1)}, u32[]{:S(2)}, u32[]{:S(2)}) collective-permute-start(bf16[8,1,16,512]{3,2,1,0:T(8,128)(2,1)S(1)} %shard_map.97.refs_4_), channel_id=1, source_target_pairs={{0,3},{1,0},{2,1},{3,2},{4,7},{5,4},{6,5},{7,6},{8,11},{9,8},{10,9... | collective-permute-start | bytes 393224 | tf_op jit(solution)/shard_map/ppermute | solution.py:414
  162.0 1.2 collective-permute-start.17
  163.3 1.6 copy-done.35
  164.9 1.2 copy-done.46
  166.1 13.8 %shard_map.104 = (f32[64,4096]{1,0:T(8,128)S(1)}, f32[64,4096]{1,0:T(8,128)S(1)}) custom-call(s32[8,8]{1,0:T(8,128)S(1)} %broadcast_add_fusion.1.take_ref, bf16[2,2,80,512]{3,2,1,0:T(8,128)(2,1)S(1)} %copy-done.29, bf16[2,2,80,512]{3,2,1,0:T(8,128)(2,1)S(1)} %collective-permute-done.20.refs_1_, bf16[2,2,80,512]{3,2,1,0:T(8,128)(2,1)S(1)} %copy-done.11, ...), custom_call_target="tpu_custom_call" | custom-call | flops 12800000000 | tf_op jit(solution)/shard_map/pallas_call | solution.py:67
  179.9 5.4 %shard_map.105 = (f32[64,4096]{1,0:T(8,128)S(1)}, f32[64,4096]{1,0:T(8,128)S(1)}) custom-call(s32[8,8]{1,0:T(8,128)S(1)} %broadcast_add_fusion.1.take_ref, bf16[2,1,80,512]{3,2,1,0:T(8,128)(2,1)S(1)} %copy-done.42, bf16[2,1,80,512]{3,2,1,0:T(8,128)(2,1)S(1)} %copy-done.26, bf16[2,1,80,512]{3,2,1,0:T(8,128)(2,1)} %collective-permute-done.13.refs_2_, ...), custom_call_target="tpu_custom_call" | custom-call | flops 3200000000 | tf_op jit(solution)/shard_map/pallas_call | solution.py:67
  187.6 3.1 %copy-done = bf16[14,4,256,256]{3,2,1,0:T(8,128)(2,1)S(1)} copy-done((bf16[14,4,256,256]{3,2,1,0:T(8,128)(2,1)S(1)}, bf16[14,4,256,256]{3,2,1,0:T(8,128)(2,1)}, u32[]{:S(2)}) %copy-start) | copy-done | bytes 7340056
  190.7 4.3 %shard_map.94.far_ref = f32[14,64,256]{2,1,0:T(8,128)S(1)} custom-call(s32[8,8]{1,0:T(8,128)S(1)} %broadcast_add_fusion.2.take_ref, bf16[8,8,64,256]{3,2,1,0:T(8,128)(2,1)S(1)} %all-to-all-done.got_ref, bf16[56,256,256]{2,1,0:T(8,128)(2,1)S(1)} %bitcast.11), custom_call_target="tpu_custom_call" | custom-call | flops 5000000000 | tf_op jit(solution)/shard_map/pallas_call | solution.py:67
  195.1 4.0 %shard_map.106 = f32[64,4096]{1,0:T(8,128)} custom-call(f32[14,64,256]{2,1,0:T(8,128)S(1)} %shard_map.94.far_ref, bf16[4,512,256]{2,1,0:T(8,128)(2,1)S(1)} %copy-done.4, bf16[2,512,256]{2,1,0:T(8,128)(2,1)S(1)} %copy-done.8, bf16[8,512,256]{2,1,0:T(8,128)(2,1)S(1)} %copy-done.2, f32[64,4096]{1,0:T(8,128)S(1)} %copy-done.37, f32[64,4096]{1,0:T(8,128)S(1)} %copy-done.39, ...), custom_call_target="tpu_custom_call" | custom-call | flops 4000000000 | tf_op jit(solution)/shard_map/pallas_call | solution.py:67
  (182 shorter events, 24.2 us)
Async XLA Ops:
  3.2 27.4 %copy-start.50 = (s32[896,4]{0,1:T(4,128)S(1)}, s32[896,4]{0,1:T(4,128)}, u32[]{:S(2)}) copy-start(s32[896,4]{0,1:T(4,128)} %param.16) | copy-start | bytes 43012
  3.2 24.4 %collective-permute-start.18 = (bf16[8,80,512]{2,1,0:T(8,128)(2,1)}, bf16[8,80,512]{2,1,0:T(8,128)(2,1)S(1)}, u32[]{:S(2)}, u32[]{:S(2)}) collective-permute-start(bf16[8,80,512]{2,1,0:T(8,128)(2,1)} %shard_map.91.leaves_ref.refs_0_), channel_id=1, source_target_pairs={{0,56},{4,60},{8,0},{12,4},{16,8},{20,12},{24,16},{28,20},{32,24},... | collective-permute-start | bytes 1966088 | tf_op jit(solution)/shard_map/ppermute | solution.py:380
  9.6 16.9 %collective-permute-start.8 = (bf16[8,80,512]{2,1,0:T(8,128)(2,1)}, bf16[8,80,512]{2,1,0:T(8,128)(2,1)}, u32[]{:S(2)}, u32[]{:S(2)}) collective-permute-start(bf16[8,80,512]{2,1,0:T(8,128)(2,1)} %shard_map.91.leaves_ref.refs_0_), channel_id=1, source_target_pairs={{0,8},{4,12},{8,16},{12,20},{16,24},{20,28},{24,32},{28,36},{32,40... | collective-permute-start | bytes 1966088 | tf_op jit(solution)/shard_map/ppermute | solution.py:380
  9.6 44.1 %collective-permute-start.7 = (bf16[64,4096]{1,0:T(8,128)(2,1)}, bf16[64,4096]{1,0:T(8,128)(2,1)}, u32[]{:S(2)}, u32[]{:S(2)}) collective-permute-start(bf16[64,4096]{1,0:T(8,128)(2,1)} %coords_ref.3), channel_id=1, source_target_pairs={{0,4},{4,0},{8,12},{12,8},{16,20},{20,16},{24,28},{28,24},{32,36},... | collective-permute-start | bytes 1572872 | tf_op jit(solution)/shard_map/ppermute | solution.py:402
  12.4 20.6 %collective-permute-start.1 = (bf16[14,64,256]{2,1,0:T(8,128)(2,1)S(1)}, bf16[14,64,256]{2,1,0:T(8,128)(2,1)S(1)}, u32[]{:S(2)}, u32[]{:S(2)}) collective-permute-start(bf16[14,64,256]{2,1,0:T(8,128)(2,1)S(1)} %shard_map.92.refs_0_), channel_id=1, source_target_pairs={{0,56},{4,60},{8,0},{12,4},{16,8},{20,12},{24,16},{28,20},{32,24},... | collective-permute-start | bytes 1376264 | tf_op jit(solution)/shard_map/ppermute | solution.py:380
  15.5 34.9 %collective-permute-start = (bf16[14,64,256]{2,1,0:T(8,128)(2,1)S(1)}, bf16[14,64,256]{2,1,0:T(8,128)(2,1)S(1)}, u32[]{:S(2)}, u32[]{:S(2)}) collective-permute-start(bf16[14,64,256]{2,1,0:T(8,128)(2,1)S(1)} %shard_map.92.refs_0_), channel_id=1, source_target_pairs={{0,8},{4,12},{8,16},{12,20},{16,24},{20,28},{24,32},{28,36},{32,40... | collective-permute-start | bytes 1376264 | tf_op jit(solution)/shard_map/ppermute | solution.py:380
  15.8 15.0 %copy-start.51 = (s32[8]{0:T(128)}, s32[8]{0:T(128)S(1)}, u32[]{:S(2)}) copy-start(s32[8]{0:T(128)S(1)} %get-tuple-element.53) | copy-start | bytes 100
  26.4 23.9 %collective-permute-start.9 = (bf16[8,80,512]{2,1,0:T(8,128)(2,1)}, bf16[8,80,512]{2,1,0:T(8,128)(2,1)}, u32[]{:S(2)}, u32[]{:S(2)}) collective-permute-start(bf16[8,80,512]{2,1,0:T(8,128)(2,1)} %collective-permute-done.8.refs_1_), channel_id=1, source_target_pairs={{0,8},{4,12},{8,16},{12,20},{16,24},{20,28},{24,32},{28,36},{32,40... | collective-permute-start | bytes 1966088 | tf_op jit(solution)/shard_map/ppermute | solution.py:380
  27.6 32.1 %collective-permute-start.19 = (bf16[8,80,512]{2,1,0:T(8,128)(2,1)S(1)}, bf16[8,80,512]{2,1,0:T(8,128)(2,1)}, u32[]{:S(2)}, u32[]{:S(2)}) collective-permute-start(bf16[8,80,512]{2,1,0:T(8,128)(2,1)S(1)} %collective-permute-done.18.refs_2_), channel_id=1, source_target_pairs={{0,56},{4,60},{8,0},{12,4},{16,8},{20,12},{24,16},{28,20},{32,24},... | collective-permute-start | bytes 1966088 | tf_op jit(solution)/shard_map/ppermute | solution.py:380
  31.0 47.5 %copy-start.47 = (s32[4,8,2,56]{3,2,1,0:T(2,128)}, s32[4,8,2,56]{3,2,1,0:T(2,128)S(1)}, u32[]{:S(2)}) copy-start(s32[4,8,2,56]{3,2,1,0:T(2,128)S(1)} %reshape.348) | copy-start | bytes 43012
  33.0 23.9 %collective-permute-start.3 = (bf16[14,64,256]{2,1,0:T(8,128)(2,1)S(1)}, bf16[14,64,256]{2,1,0:T(8,128)(2,1)S(1)}, u32[]{:S(2)}, u32[]{:S(2)}) collective-permute-start(bf16[14,64,256]{2,1,0:T(8,128)(2,1)S(1)} %collective-permute-done.1.refs_2_), channel_id=1, source_target_pairs={{0,56},{4,60},{8,0},{12,4},{16,8},{20,12},{24,16},{28,20},{32,24},... | collective-permute-start | bytes 1376264 | tf_op jit(solution)/shard_map/ppermute | solution.py:380
  50.3 16.0 %collective-permute-start.10 = (bf16[8,80,512]{2,1,0:T(8,128)(2,1)}, bf16[8,80,512]{2,1,0:T(8,128)(2,1)}, u32[]{:S(2)}, u32[]{:S(2)}) collective-permute-start(bf16[8,80,512]{2,1,0:T(8,128)(2,1)} %collective-permute-done.9.refs_0_), channel_id=1, source_target_pairs={{0,8},{4,12},{8,16},{12,20},{16,24},{20,28},{24,32},{28,36},{32,40... | collective-permute-start | bytes 1966088 | tf_op jit(solution)/shard_map/ppermute | solution.py:380
  50.4 25.8 %collective-permute-start.2 = (bf16[14,64,256]{2,1,0:T(8,128)(2,1)S(1)}, bf16[14,64,256]{2,1,0:T(8,128)(2,1)S(1)}, u32[]{:S(2)}, u32[]{:S(2)}) collective-permute-start(bf16[14,64,256]{2,1,0:T(8,128)(2,1)S(1)} %collective-permute-done.refs_1_), channel_id=1, source_target_pairs={{0,8},{4,12},{8,16},{12,20},{16,24},{20,28},{24,32},{28,36},{32,40... | collective-permute-start | bytes 1376264 | tf_op jit(solution)/shard_map/ppermute | solution.py:380
  53.7 24.9 %collective-permute-start.30 = (bf16[2,3,80,512]{3,2,1,0:T(8,128)(2,1)}, bf16[2,3,80,512]{3,2,1,0:T(8,128)(2,1)}, u32[]{:S(2)}, u32[]{:S(2)}) collective-permute-start(bf16[2,3,80,512]{3,2,1,0:T(8,128)(2,1)} %get-tuple-element.44), channel_id=1, source_target_pairs={{0,64},{4,68},{8,72},{12,76},{16,80},{20,84},{24,88},{28,92},{32,9... | collective-permute-start | bytes 1474568 | tf_op jit(solution)/shard_map/ppermute | solution.py:397
  56.9 21.6 %collective-permute-start.31 = (bf16[2,3,80,512]{3,2,1,0:T(8,128)(2,1)}, bf16[2,3,80,512]{3,2,1,0:T(8,128)(2,1)}, u32[]{:S(2)}, u32[]{:S(2)}) collective-permute-start(bf16[2,3,80,512]{3,2,1,0:T(8,128)(2,1)} %get-tuple-element.45), channel_id=1, source_target_pairs={{0,128},{4,132},{8,136},{12,140},{16,144},{20,148},{24,152},{28,15... | collective-permute-start | bytes 1474568 | tf_op jit(solution)/shard_map/ppermute | solution.py:397
  59.7 24.7 %collective-permute-start.23 = (bf16[8,80,512]{2,1,0:T(8,128)(2,1)}, bf16[8,80,512]{2,1,0:T(8,128)(2,1)}, u32[]{:S(2)}, u32[]{:S(2)}) collective-permute-start(bf16[8,80,512]{2,1,0:T(8,128)(2,1)} %collective-permute-done.19.refs_1_), channel_id=1, source_target_pairs={{0,56},{4,60},{8,0},{12,4},{16,8},{20,12},{24,16},{28,20},{32,24},... | collective-permute-start | bytes 1966088 | tf_op jit(solution)/shard_map/ppermute | solution.py:380
  66.3 37.3 %collective-permute-start.11 = (bf16[8,80,512]{2,1,0:T(8,128)(2,1)}, bf16[8,80,512]{2,1,0:T(8,128)(2,1)}, u32[]{:S(2)}, u32[]{:S(2)}) collective-permute-start(bf16[8,80,512]{2,1,0:T(8,128)(2,1)} %collective-permute-done.10.refs_0_), channel_id=1, source_target_pairs={{0,8},{4,12},{8,16},{12,20},{16,24},{20,28},{24,32},{28,36},{32,40... | collective-permute-start | bytes 1966088 | tf_op jit(solution)/shard_map/ppermute | solution.py:380
  76.2 11.6 %collective-permute-start.32 = (bf16[2,3,80,512]{3,2,1,0:T(8,128)(2,1)}, bf16[2,3,80,512]{3,2,1,0:T(8,128)(2,1)}, u32[]{:S(2)}, u32[]{:S(2)}) collective-permute-start(bf16[2,3,80,512]{3,2,1,0:T(8,128)(2,1)} %copy-done.9), channel_id=1, source_target_pairs={{0,192},{4,196},{8,200},{12,204},{16,208},{20,212},{24,216},{28,22... | collective-permute-start | bytes 1474568 | tf_op jit(solution)/shard_map/ppermute | solution.py:397
  78.5 11.1 %collective-permute-start.5 = (bf16[14,64,256]{2,1,0:T(8,128)(2,1)S(1)}, bf16[14,64,256]{2,1,0:T(8,128)(2,1)S(1)}, u32[]{:S(2)}, u32[]{:S(2)}) collective-permute-start(bf16[14,64,256]{2,1,0:T(8,128)(2,1)S(1)} %collective-permute-done.3.refs_4_), channel_id=1, source_target_pairs={{0,56},{4,60},{8,0},{12,4},{16,8},{20,12},{24,16},{28,20},{32,24},... | collective-permute-start | bytes 1376264 | tf_op jit(solution)/shard_map/ppermute | solution.py:380
  78.6 21.4 %collective-permute-start.4 = (bf16[14,64,256]{2,1,0:T(8,128)(2,1)S(1)}, bf16[14,64,256]{2,1,0:T(8,128)(2,1)S(1)}, u32[]{:S(2)}, u32[]{:S(2)}) collective-permute-start(bf16[14,64,256]{2,1,0:T(8,128)(2,1)S(1)} %collective-permute-done.2.refs_3_), channel_id=1, source_target_pairs={{0,8},{4,12},{8,16},{12,20},{16,24},{20,28},{24,32},{28,36},{32,40... | collective-permute-start | bytes 1376264 | tf_op jit(solution)/shard_map/ppermute | solution.py:380
  84.4 16.8 %collective-permute-start.20 = (bf16[2,2,80,512]{3,2,1,0:T(8,128)(2,1)}, bf16[2,2,80,512]{3,2,1,0:T(8,128)(2,1)S(1)}, u32[]{:S(2)}, u32[]{:S(2)}) collective-permute-start(bf16[2,2,80,512]{3,2,1,0:T(8,128)(2,1)} %get-tuple-element.36), channel_id=1, source_target_pairs={{0,64},{4,68},{8,72},{12,76},{16,80},{20,84},{24,88},{28,92},{32,9... | collective-permute-start | bytes 983048 | tf_op jit(solution)/shard_map/ppermute | solution.py:397
  85.6 20.7 %copy-start.33 = (bf16[2,3,80,512]{3,2,1,0:T(8,128)(2,1)S(1)}, bf16[2,3,80,512]{3,2,1,0:T(8,128)(2,1)}, u32[]{:S(2)}) copy-start(bf16[2,3,80,512]{3,2,1,0:T(8,128)(2,1)} %copy-done.32) | copy-start | bytes 1474564
  87.8 38.3 %copy-start.30 = (bf16[2,2,80,512]{3,2,1,0:T(8,128)(2,1)}, bf16[2,2,80,512]{3,2,1,0:T(8,128)(2,1)S(1)}, u32[]{:S(2)}) copy-start(bf16[2,2,80,512]{3,2,1,0:T(8,128)(2,1)S(1)} %get-tuple-element.39.refs_4_) | copy-start | bytes 983044
  87.8 22.5 %collective-permute-start.21 = (bf16[2,2,80,512]{3,2,1,0:T(8,128)(2,1)S(1)}, bf16[2,2,80,512]{3,2,1,0:T(8,128)(2,1)S(1)}, u32[]{:S(2)}, u32[]{:S(2)}) collective-permute-start(bf16[2,2,80,512]{3,2,1,0:T(8,128)(2,1)S(1)} %copy-done.23), channel_id=1, source_target_pairs={{0,128},{4,132},{8,136},{12,140},{16,144},{20,148},{24,152},{28,15... | collective-permute-start | bytes 983048 | tf_op jit(solution)/shard_map/ppermute | solution.py:397
  89.6 22.0 %collective-permute-start.22 = (bf16[2,2,80,512]{3,2,1,0:T(8,128)(2,1)S(1)}, bf16[2,2,80,512]{3,2,1,0:T(8,128)(2,1)S(1)}, u32[]{:S(2)}, u32[]{:S(2)}) collective-permute-start(bf16[2,2,80,512]{3,2,1,0:T(8,128)(2,1)S(1)} %copy-done.21), channel_id=1, source_target_pairs={{0,192},{4,196},{8,200},{12,204},{16,208},{20,212},{24,216},{28,22... | collective-permute-start | bytes 983048 | tf_op jit(solution)/shard_map/ppermute | solution.py:397
  99.9 13.2 %collective-permute-start.24 = (bf16[2,2,80,512]{3,2,1,0:T(8,128)(2,1)S(1)}, bf16[2,2,80,512]{3,2,1,0:T(8,128)(2,1)S(1)}, u32[]{:S(2)}, u32[]{:S(2)}) collective-permute-start(bf16[2,2,80,512]{3,2,1,0:T(8,128)(2,1)S(1)} %get-tuple-element.40), channel_id=1, source_target_pairs={{0,64},{4,68},{8,72},{12,76},{16,80},{20,84},{24,88},{28,92},{32,9... | collective-permute-start | bytes 983048 | tf_op jit(solution)/shard_map/ppermute | solution.py:397
  101.1 14.6 %collective-permute-start.25 = (bf16[2,2,80,512]{3,2,1,0:T(8,128)(2,1)S(1)}, bf16[2,2,80,512]{3,2,1,0:T(8,128)(2,1)S(1)}, u32[]{:S(2)}, u32[]{:S(2)}) collective-permute-start(bf16[2,2,80,512]{3,2,1,0:T(8,128)(2,1)S(1)} %get-tuple-element.41), channel_id=1, source_target_pairs={{0,128},{4,132},{8,136},{12,140},{16,144},{20,148},{24,152},{28,15... | collective-permute-start | bytes 983048 | tf_op jit(solution)/shard_map/ppermute | solution.py:397
  103.6 14.9 %collective-permute-start.26 = (bf16[2,2,80,512]{3,2,1,0:T(8,128)(2,1)S(1)}, bf16[2,2,80,512]{3,2,1,0:T(8,128)(2,1)S(1)}, u32[]{:S(2)}, u32[]{:S(2)}) collective-permute-start(bf16[2,2,80,512]{3,2,1,0:T(8,128)(2,1)S(1)} %get-tuple-element.42), channel_id=1, source_target_pairs={{0,192},{4,196},{8,200},{12,204},{16,208},{20,212},{24,216},{28,22... | collective-permute-start | bytes 983048 | tf_op jit(solution)/shard_map/ppermute | solution.py:397
  110.3 15.7 %copy-start.10 = (bf16[2,2,80,512]{3,2,1,0:T(8,128)(2,1)}, bf16[2,2,80,512]{3,2,1,0:T(8,128)(2,1)S(1)}, u32[]{:S(2)}) copy-start(bf16[2,2,80,512]{3,2,1,0:T(8,128)(2,1)S(1)} %collective-permute-done.21.refs_2_) | copy-start | bytes 983044
  110.3 16.7 %collective-permute-start.33 = (bf16[8,3,16,512]{3,2,1,0:T(8,128)(2,1)S(1)}, bf16[8,3,16,512]{3,2,1,0:T(8,128)(2,1)S(1)}, u32[]{:S(2)}, u32[]{:S(2)}) collective-permute-start(bf16[8,3,16,512]{3,2,1,0:T(8,128)(2,1)S(1)} %shard_map.102.refs_4_), channel_id=1, source_target_pairs={{0,1},{1,2},{2,3},{3,0},{4,5},{5,6},{6,7},{7,4},{8,9},{9,10},{10,1... | collective-permute-start | bytes 1179656 | tf_op jit(solution)/shard_map/ppermute | solution.py:414
  111.6 14.5 %copy-start.12 = (bf16[2,2,80,512]{3,2,1,0:T(8,128)(2,1)}, bf16[2,2,80,512]{3,2,1,0:T(8,128)(2,1)S(1)}, u32[]{:S(2)}) copy-start(bf16[2,2,80,512]{3,2,1,0:T(8,128)(2,1)S(1)} %collective-permute-done.22.refs_3_) | copy-start | bytes 983044
  111.6 16.8 %collective-permute-start.34 = (bf16[8,3,16,512]{3,2,1,0:T(8,128)(2,1)S(1)}, bf16[8,3,16,512]{3,2,1,0:T(8,128)(2,1)S(1)}, u32[]{:S(2)}, u32[]{:S(2)}) collective-permute-start(bf16[8,3,16,512]{3,2,1,0:T(8,128)(2,1)S(1)} %shard_map.102.refs_4_), channel_id=1, source_target_pairs={{0,3},{1,0},{2,1},{3,2},{4,7},{5,4},{6,5},{7,6},{8,11},{9,8},{10,9... | collective-permute-start | bytes 1179656 | tf_op jit(solution)/shard_map/ppermute | solution.py:414
  113.1 16.9 %collective-permute-start.35 = (bf16[8,3,16,512]{3,2,1,0:T(8,128)(2,1)S(1)}, bf16[8,3,16,512]{3,2,1,0:T(8,128)(2,1)S(1)}, u32[]{:S(2)}, u32[]{:S(2)}) collective-permute-start(bf16[8,3,16,512]{3,2,1,0:T(8,128)(2,1)S(1)} %shard_map.102.refs_4_), channel_id=1, source_target_pairs={{0,2},{1,3},{2,0},{3,1},{4,6},{5,7},{6,4},{7,5},{8,10},{9,11},{10,... | collective-permute-start | bytes 1179656 | tf_op jit(solution)/shard_map/ppermute | solution.py:414
  115.8 15.7 %collective-permute-start.6 = (bf16[14,64,256]{2,1,0:T(8,128)(2,1)S(1)}, bf16[14,64,256]{2,1,0:T(8,128)(2,1)S(1)}, u32[]{:S(2)}, u32[]{:S(2)}) collective-permute-start(bf16[14,64,256]{2,1,0:T(8,128)(2,1)S(1)} %collective-permute-done.5.refs_6_), channel_id=1, source_target_pairs={{0,56},{4,60},{8,0},{12,4},{16,8},{20,12},{24,16},{28,20},{32,24},... | collective-permute-start | bytes 1376264 | tf_op jit(solution)/shard_map/ppermute | solution.py:380
  118.5 15.9 %collective-permute-start.12 = (bf16[2,1,80,512]{3,2,1,0:T(8,128)(2,1)S(1)}, bf16[2,1,80,512]{3,2,1,0:T(8,128)(2,1)S(1)}, u32[]{:S(2)}, u32[]{:S(2)}) collective-permute-start(bf16[2,1,80,512]{3,2,1,0:T(8,128)(2,1)S(1)} %get-tuple-element.31), channel_id=1, source_target_pairs={{0,64},{4,68},{8,72},{12,76},{16,80},{20,84},{24,88},{28,92},{32,9... | collective-permute-start | bytes 491528 | tf_op jit(solution)/shard_map/ppermute | solution.py:397
  126.0 20.1 %copy-start.34 = (bf16[16,512,128]{2,1,0:T(8,128)(2,1)}, bf16[16,512,128]{2,1,0:T(8,128)(2,1)S(1)}, u32[]{:S(2)}) copy-start(bf16[16,512,128]{2,1,0:T(8,128)(2,1)S(1)} %get-tuple-element.34.refs_8_.refs_12_) | copy-start | bytes 6291460
  127.0 35.0 %collective-permute-start.27 = (bf16[8,4,16,512]{3,2,1,0:T(8,128)(2,1)}, bf16[8,4,16,512]{3,2,1,0:T(8,128)(2,1)}, u32[]{:S(2)}, u32[]{:S(2)}) collective-permute-start(bf16[8,4,16,512]{3,2,1,0:T(8,128)(2,1)} %shard_map.100.refs_8_), channel_id=1, source_target_pairs={{0,1},{1,2},{2,3},{3,0},{4,5},{5,6},{6,7},{7,4},{8,9},{9,10},{10,1... | collective-permute-start | bytes 1572872 | tf_op jit(solution)/shard_map/ppermute | solution.py:414
  128.3 34.9 %collective-permute-start.28 = (bf16[8,4,16,512]{3,2,1,0:T(8,128)(2,1)}, bf16[8,4,16,512]{3,2,1,0:T(8,128)(2,1)}, u32[]{:S(2)}, u32[]{:S(2)}) collective-permute-start(bf16[8,4,16,512]{3,2,1,0:T(8,128)(2,1)} %shard_map.100.refs_8_), channel_id=1, source_target_pairs={{0,3},{1,0},{2,1},{3,2},{4,7},{5,4},{6,5},{7,6},{8,11},{9,8},{10,9... | collective-permute-start | bytes 1572872 | tf_op jit(solution)/shard_map/ppermute | solution.py:414
  130.1 33.1 %collective-permute-start.29 = (bf16[8,4,16,512]{3,2,1,0:T(8,128)(2,1)}, bf16[8,4,16,512]{3,2,1,0:T(8,128)(2,1)}, u32[]{:S(2)}, u32[]{:S(2)}) collective-permute-start(bf16[8,4,16,512]{3,2,1,0:T(8,128)(2,1)} %shard_map.100.refs_8_), channel_id=1, source_target_pairs={{0,2},{1,3},{2,0},{3,1},{4,6},{5,7},{6,4},{7,5},{8,10},{9,11},{10,... | collective-permute-start | bytes 1572872 | tf_op jit(solution)/shard_map/ppermute | solution.py:414
  131.4 26.6 %collective-permute-start.13 = (bf16[2,1,80,512]{3,2,1,0:T(8,128)(2,1)}, bf16[2,1,80,512]{3,2,1,0:T(8,128)(2,1)}, u32[]{:S(2)}, u32[]{:S(2)}) collective-permute-start(bf16[2,1,80,512]{3,2,1,0:T(8,128)(2,1)} %get-tuple-element.32), channel_id=1, source_target_pairs={{0,128},{4,132},{8,136},{12,140},{16,144},{20,148},{24,152},{28,15... | collective-permute-start | bytes 491528 | tf_op jit(solution)/shard_map/ppermute | solution.py:397
  135.1 22.9 %collective-permute-start.14 = (bf16[2,1,80,512]{3,2,1,0:T(8,128)(2,1)}, bf16[2,1,80,512]{3,2,1,0:T(8,128)(2,1)}, u32[]{:S(2)}, u32[]{:S(2)}) collective-permute-start(bf16[2,1,80,512]{3,2,1,0:T(8,128)(2,1)} %get-tuple-element.33), channel_id=1, source_target_pairs={{0,192},{4,196},{8,200},{12,204},{16,208},{20,212},{24,216},{28,22... | collective-permute-start | bytes 491528 | tf_op jit(solution)/shard_map/ppermute | solution.py:397
  150.1 37.5 %all-to-all-start = ((bf16[8,8,64,256]{3,2,1,0:T(8,128)(2,1)}), bf16[8,8,64,256]{3,2,1,0:T(8,128)(2,1)S(1)}, u32[]{:S(2)}, u32[]{:S(2)}) async-start(bf16[8,8,64,256]{3,2,1,0:T(8,128)(2,1)} %shard_map.93), calls=%async_computation | async-start | bytes 4194304 | tf_op jit(solution)/shard_map/all_to_all | solution.py:406
  159.2 20.7 %collective-permute-start.15 = (bf16[8,1,16,512]{3,2,1,0:T(8,128)(2,1)S(1)}, bf16[8,1,16,512]{3,2,1,0:T(8,128)(2,1)S(1)}, u32[]{:S(2)}, u32[]{:S(2)}) collective-permute-start(bf16[8,1,16,512]{3,2,1,0:T(8,128)(2,1)S(1)} %shard_map.97.refs_4_), channel_id=1, source_target_pairs={{0,1},{1,2},{2,3},{3,0},{4,5},{5,6},{6,7},{7,4},{8,9},{9,10},{10,1... | collective-permute-start | bytes 393224 | tf_op jit(solution)/shard_map/ppermute | solution.py:414
  159.3 20.6 %collective-permute-start.16 = (bf16[8,1,16,512]{3,2,1,0:T(8,128)(2,1)S(1)}, bf16[8,1,16,512]{3,2,1,0:T(8,128)(2,1)S(1)}, u32[]{:S(2)}, u32[]{:S(2)}) collective-permute-start(bf16[8,1,16,512]{3,2,1,0:T(8,128)(2,1)S(1)} %shard_map.97.refs_4_), channel_id=1, source_target_pairs={{0,3},{1,0},{2,1},{3,2},{4,7},{5,4},{6,5},{7,6},{8,11},{9,8},{10,9... | collective-permute-start | bytes 393224 | tf_op jit(solution)/shard_map/ppermute | solution.py:414
  162.0 17.9 %collective-permute-start.17 = (bf16[8,1,16,512]{3,2,1,0:T(8,128)(2,1)S(1)}, bf16[8,1,16,512]{3,2,1,0:T(8,128)(2,1)S(1)}, u32[]{:S(2)}, u32[]{:S(2)}) collective-permute-start(bf16[8,1,16,512]{3,2,1,0:T(8,128)(2,1)S(1)} %shard_map.97.refs_4_), channel_id=1, source_target_pairs={{0,2},{1,3},{2,0},{3,1},{4,6},{5,7},{6,4},{7,5},{8,10},{9,11},{10,... | collective-permute-start | bytes 393224 | tf_op jit(solution)/shard_map/ppermute | solution.py:414
  166.1 13.8 %copy-start.26 = (bf16[2,1,80,512]{3,2,1,0:T(8,128)(2,1)S(1)}, bf16[2,1,80,512]{3,2,1,0:T(8,128)(2,1)}, u32[]{:S(2)}) copy-start(bf16[2,1,80,512]{3,2,1,0:T(8,128)(2,1)} %copy-done.24) | copy-start | bytes 491524
  166.1 13.8 %copy-start.42 = (bf16[2,1,80,512]{3,2,1,0:T(8,128)(2,1)S(1)}, bf16[2,1,80,512]{3,2,1,0:T(8,128)(2,1)}, u32[]{:S(2)}) copy-start(bf16[2,1,80,512]{3,2,1,0:T(8,128)(2,1)} %copy-done.40) | copy-start | bytes 491524
  186.3 8.7 %collective-permute-start.36 = (f32[64,4096]{1,0:T(8,128)S(1)}, f32[64,4096]{1,0:T(8,128)}, u32[]{:S(2)}, u32[]{:S(2)}) collective-permute-start(f32[64,4096]{1,0:T(8,128)S(1)} %get-tuple-element.52), channel_id=1, source_target_pairs={{0,4},{4,0},{8,12},{12,8},{16,20},{20,16},{24,28},{28,24},{32,36},... | collective-permute-start | bytes 3145736 | tf_op jit(solution)/shard_map/ppermute | solution.py:402
  (43 other events, 227.8 us)
